TPU v7x, 32 devices: a whole 2x2x4 slice. The times are simulated.
32 devices in a mesh: tx: 4 (over z), ty: 2 (over y), vel: 4 (over x, core).
Axes of the slice: x: 2, y: 2, z: 4, core: 2. Of those that a mesh axis runs over, the one named last changes fastest.
Arguments:
- initial: float32 [32, 16, 16, 3072], P('tx', 'ty', None, 'vel'), may hold values from -2 to 3.5
- velocity: float32 [3, 3072], P(None, 'vel'), may hold values from -3 to 3, as said below
- weights: float32 [3072], P('vel'), may hold values from 0.5 to 2
- wall: int32 [32, 16, 16], P('tx', 'ty'), may hold values 0 or 1
- wall_temp: float32 [32, 16, 16], P('tx', 'ty'), may hold values from -1 to 1
- mass_target: float32 [], replicated, may hold values from 0.5 to 1.5
Outputs:
- distribution: float32 [32, 16, 16, 3072], P('tx', 'ty', None, 'vel')
- macro_fields: float32 [5, 32, 16, 16], P(None, 'tx', 'ty')
Inputs may be any that keep to these rules, and one draw needn't show every extreme that they name: `velocity`: within each aligned block of 768 velocities the first quarter has positive x and y components, the second positive x and negative y, the third negative x and positive y, the fourth negative x and y; x and y components are 0.05 or more in magnitude.
All inputs are finite; a program needn't handle non-finite values. No bound on the sum of `wall` on one device may be relied on, other than what follows from the above.
Results may differ from a plain program's by a relative error of at most 0.0003.
Values sent between devices are 32-bit elements; how exact they have to be, the bound alone decides.
No kernel may reach another device: no remote copies, remote signals or barrier semaphores. Data moves between devices by JAX's collectives and lax.ppermute only.
A program may use at most 128 MiB of HBM per device.

v0:
```python
import jax
import jax.numpy as jnp
from jax import lax
from jax.sharding import PartitionSpec as P

ITERS = 3
MACRO_STEPS = 4


step_time = 0.1
collision = 1.0
macro_time = 0.1
viscosity = 1.0
conduction = 1.0
highest = lax.Precision.HIGHEST


def padded_2(cells, sides, width):
    for axis, dim in sides:
        count = lax.axis_size(axis)
        head = lax.slice_in_dim(cells, 0, width, axis=dim)
        tail = lax.slice_in_dim(cells, cells.shape[dim] - width, cells.shape[dim], axis=dim)
        cells = jnp.concatenate(
            [
                lax.ppermute(tail, axis, [(i, (i + 1) % count) for i in range(count)]),
                cells,
                lax.ppermute(head, axis, [((i + 1) % count, i) for i in range(count)]),
            ],
            axis=dim,
        )
    return cells


def basis(velocity):
    speed_sq = velocity[0] * velocity[0] + velocity[1] * velocity[1] + velocity[2] * velocity[2]
    return jnp.stack(
        [
            jnp.ones_like(speed_sq),
            2.0 * velocity[0],
            2.0 * velocity[1],
            2.0 * velocity[2],
            speed_sq - 1.5,
        ]
    )


def projector(velocity, weights, total_count):
    vel_x, vel_y, vel_z = (velocity[0], velocity[1], velocity[2])
    speed_sq = vel_x * vel_x + vel_y * vel_y + vel_z * vel_z
    moment_rows = jnp.stack(
        [
            jnp.ones_like(speed_sq),
            vel_x,
            vel_y,
            vel_z,
            2.0 / 3.0 * speed_sq - 1.0,
            2.0 * (vel_x * vel_x - speed_sq / 3.0),
            2.0 * (vel_y * vel_y - speed_sq / 3.0),
            2.0 * (vel_z * vel_z - speed_sq / 3.0),
            2.0 * vel_x * vel_y,
            2.0 * vel_x * vel_z,
            2.0 * vel_y * vel_z,
            vel_x * (speed_sq - 2.5),
            vel_y * (speed_sq - 2.5),
            vel_z * (speed_sq - 2.5),
        ]
    )
    return moment_rows * (weights / total_count)[None, :]


def differences(shifted):
    grads = [(shifted(direction, 1) - shifted(direction, -1)) * 0.5 for direction in (1, 2, 3)]
    middle = shifted(1, 0)
    laplace = (
        shifted(1, 1)
        + shifted(1, -1)
        - 2.0 * middle
        + (shifted(2, 1) + shifted(2, -1) - 2.0 * middle)
    )
    laplace = laplace + (shifted(3, 1) + shifted(3, -1) - 2.0 * middle)
    return (grads, laplace, middle)


def macro_sources(shifted):
    grads, laplace, middle = differences(shifted)
    grad_x, grad_y, grad_z = grads
    sig_x = grad_x[0] + grad_y[3] + grad_z[4]
    sig_y = grad_x[3] + grad_y[1] + grad_z[5]
    sig_z = grad_x[4] + grad_y[5] + grad_z[2]
    heat_flow = grad_x[6] + grad_y[7] + grad_z[8]
    return jnp.stack(
        [
            -0.5 * (sig_x + viscosity * laplace[9]),
            -0.5 * (sig_y + viscosity * laplace[10]),
            -0.5 * (sig_z + viscosity * laplace[11]),
            -(2.0 / 3.0) * (heat_flow + conduction * laplace[12]),
        ]
    )


def macro_step(shifted, sources):
    grads, laplace, middle = differences(shifted)
    grad_x, grad_y, grad_z = grads
    div_u = grad_x[1] + grad_y[2] + grad_z[3]
    change_rates = [-div_u]
    for component in range(3):
        along = grads[component]
        change_rates.append(
            -0.5 * (along[0] + along[4])
            + 0.5 * viscosity * laplace[1 + component]
            + sources[component]
        )
    change_rates.append(-(2.0 / 3.0) * div_u + 2.0 / 3.0 * conduction * laplace[4] + sources[3])
    return middle + macro_time * jnp.stack(change_rates)


def kinetic_update(corrected, equilibrium, before_x, after_x, before_y, after_y, velocity):
    plus_part = jnp.maximum(velocity, 0.0)
    minus_part = jnp.minimum(velocity, 0.0)
    before_z = jnp.roll(corrected, 1, 2)
    after_z = jnp.roll(corrected, -1, 2)
    transport = plus_part[0] * (corrected - before_x) + minus_part[0] * (after_x - corrected)
    transport = transport + (
        plus_part[1] * (corrected - before_y) + minus_part[1] * (after_y - corrected)
    )
    transport = transport + (
        plus_part[2] * (corrected - before_z) + minus_part[2] * (after_z - corrected)
    )
    return corrected - step_time * transport + step_time * collision * (equilibrium - corrected)


def padded_view(padded):

    def shifted(direction, offset):
        selector = [slice(None), slice(1, -1), slice(1, -1), slice(1, -1)]
        extent = padded.shape[direction]
        selector[direction] = slice(1 + offset, extent - 1 + offset)
        return padded[tuple(selector)]

    return shifted


def wrap_depth(padded):
    return jnp.concatenate([padded[..., -1:], padded, padded[..., :1]], axis=3)


def pad_sources(fields):
    padded = wrap_depth(padded_2(fields, (("tx", 1), ("ty", 2)), 1))
    return padded


def pad_state(macro_state):
    padded = wrap_depth(padded_2(macro_state, (("tx", 1), ("ty", 2)), 1))
    return padded


def total_mass(local_sum):
    summed = lax.psum(local_sum, ("tx", "ty"))
    return summed


def on_device(initial, velocity, weights, wall, wall_temp, mass_target):
    width_dev = weights.shape[0]
    total_velocities = float(width_dev * lax.axis_size("vel"))
    cell_count = float(
        wall.shape[0] * wall.shape[1] * wall.shape[2] * lax.axis_size("tx") * lax.axis_size("ty")
    )
    moment_rows = projector(velocity, weights, total_velocities)
    rows = basis(velocity)
    is_wall = (wall == 1)[..., None]
    wall_state = wall_temp[..., None] * rows[4]
    distribution = initial
    macro_state = None
    for iteration in range(ITERS):
        local_moments = jnp.einsum("kv,xyzv->kxyz", moment_rows, distribution, precision=highest)
        moments = lax.psum(local_moments, "vel")
        kinetic_state = moments[0:5]
        fields = jnp.concatenate([moments[5:14], moments[1:5]])
        mass_total = total_mass(jnp.sum(kinetic_state[0]))
        sources = macro_sources(padded_view(pad_sources(fields)))
        macro_state = kinetic_state
        for sweep in range(MACRO_STEPS):
            macro_state = macro_step(padded_view(pad_state(macro_state)), sources)
        density_mean = mass_total / cell_count
        macro_state = jnp.concatenate(
            [(macro_state[0] - density_mean + mass_target)[None], macro_state[1:]]
        )
        change = macro_state - kinetic_state
        corrected = distribution + jnp.einsum("kxyz,kv->xyzv", change, rows, precision=highest)
        equilibrium = jnp.einsum("kxyz,kv->xyzv", macro_state, rows, precision=highest)
        padded = padded_2(corrected, (("tx", 0), ("ty", 1)), 1)
        before_x = padded[:-2, 1:-1]
        after_x = padded[2:, 1:-1]
        before_y = padded[1:-1, :-2]
        after_y = padded[1:-1, 2:]
        updated = kinetic_update(
            corrected, equilibrium, before_x, after_x, before_y, after_y, velocity
        )
        distribution = jnp.where(is_wall, wall_state, updated)
    return (distribution, macro_state)


def solution(mesh):
    placed = (
        P("tx", "ty", None, "vel"),
        P(None, "vel"),
        P("vel"),
        P("tx", "ty", None),
        P("tx", "ty", None),
        P(),
    )
    return jax.shard_map(
        on_device,
        mesh=mesh,
        in_specs=placed,
        out_specs=(P("tx", "ty", None, "vel"), P(None, "tx", "ty", None)),
        check_vma=False,
    )
```

profile of v0, /device:TPU:0, one launch (start us, length us, event | category | flops | bytes accessed | tf_op | source)
XLA Modules:
  0.0 449.7 jit_solution(716490009049969232)
XLA Ops:
  4.4 12.9 %fusion.73 = f32[14,8,8,16]{3,0,2,1:T(8,128)S(1)} fusion(f32[8,8,16,768]{3,2,1,0:T(8,128)} %param.6, f32[14,768]{1,0:T(8,128)S(1)} %stack.29, f32[768]{0:T(1024)S(1)} %broadcast_multiply_fusion), kind=kOutput, calls=%fused_computation.583 | convolution fusion | flops 132131328 | bytes 3249152 | tf_op jit(solution)/shard_map/kv,xyzv->kxyz/dot_general | solution.py:175
  17.5 17.4 %psum.42 = f32[14,8,8,16]{3,2,1,0:T(8,128)S(1)} all-reduce(f32[14,8,8,16]{3,2,1,0:T(8,128)S(1)} %copy.9), channel_id=1, replica_groups=mesh['tx'=4,'ty'=2,'vel'=4] {'vel'}, use_global_device_ids=true, to_apply=%region_0.0 | all-reduce | flops 14336 | bytes 114688 | tf_op jit(solution)/shard_map/psum | solution.py:176
  36.5 2.2 collective-permute-start
  44.1 2.7 collective-permute-start.4
  51.1 2.2 collective-permute-done.7
  58.4 2.8 collective-permute-start.8
  61.2 1.7 collective-permute-done.9
  65.1 1.8 collective-permute-done.11
  70.0 2.8 collective-permute-start.12
  76.6 1.8 collective-permute-done.15
  82.4 2.6 collective-permute-start.16
  89.4 21.9 %psum.43 = f32[]{:T(128)} all-reduce(f32[]{:T(128)} %slice_reduce_fusion.2), channel_id=1, replica_groups=mesh['tx'=4,'ty'=2,'vel'=4] {'tx','ty'}, use_global_device_ids=true, to_apply=%region_2.0 | all-reduce | flops 1 | bytes 8 | tf_op jit(solution)/shard_map/psum | solution.py:158
  114.7 2.8 convolution_add_fusion.2
  117.6 4.2 collective-permute-start.21
  122.0 5.3 %collective-permute-done.20 = f32[1,8,16,768]{3,2,1,0:T(8,128)S(1)} collective-permute-done((f32[1,8,16,768]{3,2,1,0:T(8,128)S(1)}, f32[1,8,16,768]{3,2,1,0:T(8,128)S(1)}, u32[]{:S(2)}, u32[]{:S(2)}) %collective-permute-start.20) | collective-permute-done | bytes 393248 | tf_op jit(solution)/shard_map/ppermute | solution.py:25
  127.3 2.8 collective-permute-done.21
  130.2 2.0 collective-permute-start.23
  133.1 5.9 %collective-permute-done.22 = f32[10,1,16,768]{3,2,1,0:T(8,128)S(1)} collective-permute-done((f32[10,1,16,768]{3,2,1,0:T(8,128)S(1)}, f32[10,1,16,768]{3,2,1,0:T(8,128)S(1)}, u32[]{:S(2)}, u32[]{:S(2)}) %collective-permute-start.22) | collective-permute-done | bytes 491552 | tf_op jit(solution)/shard_map/ppermute | solution.py:25
  139.0 5.3 %collective-permute-done.23 = f32[10,1,16,768]{3,2,1,0:T(8,128)S(1)} collective-permute-done((f32[10,1,16,768]{3,2,1,0:T(8,128)S(1)}, f32[10,1,16,768]{3,2,1,0:T(8,128)S(1)}, u32[]{:S(2)}, u32[]{:S(2)}) %collective-permute-start.23) | collective-permute-done | bytes 491552 | tf_op jit(solution)/shard_map/ppermute | solution.py:27
  144.4 6.1 %multiply_select_fusion.2 = f32[8,8,16,768]{3,2,1,0:T(8,128)S(1)} fusion(f32[8,8,16,768]{3,2,1,0:T(8,128)S(1)} %convolution_add_fusion.2, f32[10,1,16,768]{3,2,1,0:T(8,128)S(1)} %collective-permute-done.23, f32[1,8,16,768]{3,2,1,0:T(8,128)S(1)} %collective-permute-done.21, f32[1,8,16,768]{3,2,1,0:T(8,128)S(1)} %collective-permute-done.20, ...), kind=kOutput, calls=%fused_computation.2 | convolution fusion | flops 73924608 | bytes 14414848 | tf_op jit(solution)/shard_map/kxyz,kv->xyzv/dot_general | solution.py:190
  150.5 11.2 %fusion.71 = f32[14,8,8,16]{3,0,2,1:T(8,128)S(1)} fusion(f32[8,8,16,768]{3,2,1,0:T(8,128)S(1)} %multiply_select_fusion.2, f32[14,768]{1,0:T(8,128)S(1)} %stack.29, f32[768]{0:T(1024)S(1)} %broadcast_multiply_fusion), kind=kOutput, calls=%fused_computation.581 | convolution fusion | flops 132131328 | bytes 3249152 | tf_op jit(solution)/shard_map/kv,xyzv->kxyz/dot_general | solution.py:175
  162.6 16.1 %psum.44 = f32[14,8,8,16]{3,2,1,0:T(8,128)} all-reduce(f32[14,8,8,16]{3,2,1,0:T(8,128)} %copy.12), channel_id=1, replica_groups=mesh['tx'=4,'ty'=2,'vel'=4] {'vel'}, use_global_device_ids=true, to_apply=%region_3.4 | all-reduce | flops 14336 | bytes 114688 | tf_op jit(solution)/shard_map/psum | solution.py:176
  180.5 2.8 collective-permute-start.24
  186.3 2.0 collective-permute-start.26
  188.4 3.8 collective-permute-start.28
  194.6 1.9 collective-permute-start.30
  196.5 2.2 collective-permute-done.31
  202.9 3.8 collective-permute-start.32
  210.6 1.8 collective-permute-done.35
  216.0 2.8 collective-permute-start.36
  222.6 1.8 collective-permute-done.39
  227.6 2.7 collective-permute-start.40
  230.4 1.8 collective-permute-done.41
  236.3 22.7 %psum.45 = f32[]{:T(128)} all-reduce(f32[]{:T(128)} %slice_reduce_fusion.1), channel_id=1, replica_groups=mesh['tx'=4,'ty'=2,'vel'=4] {'tx','ty'}, use_global_device_ids=true, to_apply=%region_5.6 | all-reduce | flops 1 | bytes 8 | tf_op jit(solution)/shard_map/psum | solution.py:158
  264.9 2.8 convolution_add_fusion.1
  267.9 4.2 collective-permute-start.45
  272.1 5.5 %collective-permute-done.44 = f32[1,8,16,768]{3,2,1,0:T(8,128)S(1)} collective-permute-done((f32[1,8,16,768]{3,2,1,0:T(8,128)S(1)}, f32[1,8,16,768]{3,2,1,0:T(8,128)S(1)}, u32[]{:S(2)}, u32[]{:S(2)}) %collective-permute-start.44) | collective-permute-done | bytes 393248 | tf_op jit(solution)/shard_map/ppermute | solution.py:25
  277.5 2.8 collective-permute-done.45
  280.5 2.0 collective-permute-start.47
  283.4 5.9 %collective-permute-done.46 = f32[10,1,16,768]{3,2,1,0:T(8,128)S(1)} collective-permute-done((f32[10,1,16,768]{3,2,1,0:T(8,128)S(1)}, f32[10,1,16,768]{3,2,1,0:T(8,128)S(1)}, u32[]{:S(2)}, u32[]{:S(2)}) %collective-permute-start.46) | collective-permute-done | bytes 491552 | tf_op jit(solution)/shard_map/ppermute | solution.py:25
  289.3 5.3 %collective-permute-done.47 = f32[10,1,16,768]{3,2,1,0:T(8,128)S(1)} collective-permute-done((f32[10,1,16,768]{3,2,1,0:T(8,128)S(1)}, f32[10,1,16,768]{3,2,1,0:T(8,128)S(1)}, u32[]{:S(2)}, u32[]{:S(2)}) %collective-permute-start.47) | collective-permute-done | bytes 491552 | tf_op jit(solution)/shard_map/ppermute | solution.py:27
  294.6 6.1 %multiply_select_fusion.1 = f32[8,8,16,768]{3,2,1,0:T(8,128)S(1)} fusion(f32[8,8,16,768]{3,2,1,0:T(8,128)S(1)} %convolution_add_fusion.1, f32[10,1,16,768]{3,2,1,0:T(8,128)S(1)} %collective-permute-done.47, f32[1,8,16,768]{3,2,1,0:T(8,128)S(1)} %collective-permute-done.45, f32[1,8,16,768]{3,2,1,0:T(8,128)S(1)} %collective-permute-done.44, ...), kind=kOutput, calls=%fused_computation.1 | convolution fusion | flops 73924608 | bytes 14414848 | tf_op jit(solution)/shard_map/kxyz,kv->xyzv/dot_general | solution.py:190
  300.8 11.2 %fusion.69 = f32[14,8,8,16]{3,0,2,1:T(8,128)S(1)} fusion(f32[8,8,16,768]{3,2,1,0:T(8,128)S(1)} %multiply_select_fusion.1, f32[14,768]{1,0:T(8,128)S(1)} %stack.29, f32[768]{0:T(1024)S(1)} %copy-done.6), kind=kOutput, calls=%fused_computation.579 | convolution fusion | flops 132131328 | bytes 3249152 | tf_op jit(solution)/shard_map/kv,xyzv->kxyz/dot_general | solution.py:175
  312.9 16.1 %psum.46 = f32[14,8,8,16]{3,2,1,0:T(8,128)} all-reduce(f32[14,8,8,16]{3,2,1,0:T(8,128)} %copy.15), channel_id=1, replica_groups=mesh['tx'=4,'ty'=2,'vel'=4] {'vel'}, use_global_device_ids=true, to_apply=%region_6.7 | all-reduce | flops 14336 | bytes 114688 | tf_op jit(solution)/shard_map/psum | solution.py:176
  329.7 3.8 collective-permute-start.48
  336.5 2.0 collective-permute-start.50
  338.6 3.8 collective-permute-start.52
  344.8 1.9 collective-permute-start.54
  346.8 2.2 collective-permute-done.55
  353.1 3.8 collective-permute-start.56
  360.8 1.8 collective-permute-done.59
  366.2 2.8 collective-permute-start.60
  372.9 1.8 collective-permute-done.63
  377.9 2.7 collective-permute-start.64
  380.6 1.8 collective-permute-done.65
  386.5 22.9 %psum.47 = f32[]{:T(128)} all-reduce(f32[]{:T(128)} %slice_reduce_fusion), channel_id=1, replica_groups=mesh['tx'=4,'ty'=2,'vel'=4] {'tx','ty'}, use_global_device_ids=true, to_apply=%region_8.9 | all-reduce | flops 1 | bytes 8 | tf_op jit(solution)/shard_map/psum | solution.py:158
  412.3 2.8 convolution_add_fusion
  415.2 3.8 collective-permute-start.69
  419.0 5.9 %collective-permute-done.68 = f32[1,8,16,768]{3,2,1,0:T(8,128)S(1)} collective-permute-done((f32[1,8,16,768]{3,2,1,0:T(8,128)S(1)}, f32[1,8,16,768]{3,2,1,0:T(8,128)S(1)}, u32[]{:S(2)}, u32[]{:S(2)}) %collective-permute-start.68) | collective-permute-done | bytes 393248 | tf_op jit(solution)/shard_map/ppermute | solution.py:25
  424.9 2.4 collective-permute-done.69
  427.4 2.0 collective-permute-start.71
  430.4 5.9 %collective-permute-done.70 = f32[10,1,16,768]{3,2,1,0:T(8,128)S(1)} collective-permute-done((f32[10,1,16,768]{3,2,1,0:T(8,128)S(1)}, f32[10,1,16,768]{3,2,1,0:T(8,128)S(1)}, u32[]{:S(2)}, u32[]{:S(2)}) %collective-permute-start.70) | collective-permute-done | bytes 491552 | tf_op jit(solution)/shard_map/ppermute | solution.py:25
  436.2 5.3 %collective-permute-done.71 = f32[10,1,16,768]{3,2,1,0:T(8,128)S(1)} collective-permute-done((f32[10,1,16,768]{3,2,1,0:T(8,128)S(1)}, f32[10,1,16,768]{3,2,1,0:T(8,128)S(1)}, u32[]{:S(2)}, u32[]{:S(2)}) %collective-permute-start.71) | collective-permute-done | bytes 491552 | tf_op jit(solution)/shard_map/ppermute | solution.py:27
  441.6 7.9 %multiply_select_fusion = f32[8,8,16,768]{3,2,1,0:T(8,128)} fusion(f32[8,8,16,768]{3,2,1,0:T(8,128)S(1)} %convolution_add_fusion, f32[10,1,16,768]{3,2,1,0:T(8,128)S(1)} %collective-permute-done.71, f32[1,8,16,768]{3,2,1,0:T(8,128)S(1)} %collective-permute-done.69, f32[1,8,16,768]{3,2,1,0:T(8,128)S(1)} %collective-permute-done.68, ...), kind=kOutput, calls=%fused_computation | convolution fusion | flops 73924608 | bytes 14414848 | tf_op jit(solution)/shard_map/kxyz,kv->xyzv/dot_general | solution.py:190
  (387 shorter events, 110.2 us)
Async XLA Ops:
  34.9 5.6 %collective-permute-start.1 = (f32[5,1,8,16]{3,2,1,0:T(8,128)S(1)}, f32[5,1,8,16]{3,2,1,0:T(8,128)S(1)}, u32[]{:S(2)}, u32[]{:S(2)}) collective-permute-start(f32[5,1,8,16]{3,2,1,0:T(8,128)S(1)} %get-tuple-element.84), channel_id=1, source_target_pairs={{0,8},{8,16},{16,24},{24,0},{1,9},{9,17},{17,25},{25,1},{2,10},{10... | collective-permute-start | bytes 7688 | tf_op jit(solution)/shard_map/ppermute | solution.py:25
  36.5 4.0 collective-permute-start
  40.6 6.2 %collective-permute-start.3 = (f32[5,10,1,16]{3,2,1,0:T(1,128)S(1)}, f32[5,10,1,16]{3,2,1,0:T(1,128)S(1)}, u32[]{:S(2)}, u32[]{:S(2)}) collective-permute-start(f32[5,10,1,16]{3,2,1,0:T(1,128)S(1)} %get-tuple-element.162), channel_id=1, source_target_pairs={{0,4},{4,0},{1,5},{5,1},{2,6},{6,2},{3,7},{7,3},{8,12},{12,8},{9,1... | collective-permute-start | bytes 9608 | tf_op jit(solution)/shard_map/ppermute | solution.py:25
  42.2 4.6 %collective-permute-start.2 = (f32[5,10,1,16]{3,2,1,0:T(1,128)S(1)}, f32[5,10,1,16]{3,2,1,0:T(1,128)S(1)}, u32[]{:S(2)}, u32[]{:S(2)}) collective-permute-start(f32[5,10,1,16]{3,2,1,0:T(1,128)S(1)} %get-tuple-element.163), channel_id=1, source_target_pairs={{4,0},{0,4},{5,1},{1,5},{6,2},{2,6},{7,3},{3,7},{12,8},{8,12},{13,... | collective-permute-start | bytes 9608 | tf_op jit(solution)/shard_map/ppermute | solution.py:27
  42.7 6.1 %collective-permute-start.5 = (f32[13,1,8,16]{3,2,1,0:T(8,128)S(1)}, f32[13,1,8,16]{3,2,1,0:T(8,128)S(1)}, u32[]{:S(2)}, u32[]{:S(2)}) collective-permute-start(f32[13,1,8,16]{3,2,1,0:T(8,128)S(1)} %get-tuple-element.90), channel_id=1, source_target_pairs={{0,8},{8,16},{16,24},{24,0},{1,9},{9,17},{17,25},{25,1},{2,10},{10... | collective-permute-start | bytes 19976 | tf_op jit(solution)/shard_map/ppermute | solution.py:25
  44.1 4.9 %collective-permute-start.4 = (f32[13,1,8,16]{3,2,1,0:T(8,128)S(1)}, f32[13,1,8,16]{3,2,1,0:T(8,128)S(1)}, u32[]{:S(2)}, u32[]{:S(2)}) collective-permute-start(f32[13,1,8,16]{3,2,1,0:T(8,128)S(1)} %get-tuple-element.91), channel_id=1, source_target_pairs={{8,0},{16,8},{24,16},{0,24},{9,1},{17,9},{25,17},{1,25},{10,2},{18... | collective-permute-start | bytes 19976 | tf_op jit(solution)/shard_map/ppermute | solution.py:27
  49.0 4.3 collective-permute-start.7
  50.6 4.3 collective-permute-start.6
  57.3 5.6 %collective-permute-start.9 = (f32[5,1,8,16]{3,2,1,0:T(8,128)S(1)}, f32[5,1,8,16]{3,2,1,0:T(8,128)S(1)}, u32[]{:S(2)}, u32[]{:S(2)}) collective-permute-start(f32[5,1,8,16]{3,2,1,0:T(8,128)S(1)} %get-tuple-element.184), channel_id=1, source_target_pairs={{0,8},{8,16},{16,24},{24,0},{1,9},{9,17},{17,25},{25,1},{2,10},{10... | collective-permute-start | bytes 7688 | tf_op jit(solution)/shard_map/ppermute | solution.py:25
  58.4 4.6 %collective-permute-start.8 = (f32[5,1,8,16]{3,2,1,0:T(8,128)S(1)}, f32[5,1,8,16]{3,2,1,0:T(8,128)S(1)}, u32[]{:S(2)}, u32[]{:S(2)}) collective-permute-start(f32[5,1,8,16]{3,2,1,0:T(8,128)S(1)} %get-tuple-element.185), channel_id=1, source_target_pairs={{8,0},{16,8},{24,16},{0,24},{9,1},{17,9},{25,17},{1,25},{10,2},{18... | collective-permute-start | bytes 7688 | tf_op jit(solution)/shard_map/ppermute | solution.py:27
  63.0 3.9 collective-permute-start.11
  68.7 5.8 %collective-permute-start.13 = (f32[5,1,8,16]{3,2,1,0:T(8,128)S(1)}, f32[5,1,8,16]{3,2,1,0:T(8,128)S(1)}, u32[]{:S(2)}, u32[]{:S(2)}) collective-permute-start(f32[5,1,8,16]{3,2,1,0:T(8,128)S(1)} %get-tuple-element.182), channel_id=1, source_target_pairs={{0,8},{8,16},{16,24},{24,0},{1,9},{9,17},{17,25},{25,1},{2,10},{10... | collective-permute-start | bytes 7688 | tf_op jit(solution)/shard_map/ppermute | solution.py:25
  70.0 4.5 collective-permute-start.12
  74.6 3.9 collective-permute-start.15
  80.9 5.7 %collective-permute-start.17 = (f32[5,1,8,16]{3,2,1,0:T(8,128)S(1)}, f32[5,1,8,16]{3,2,1,0:T(8,128)S(1)}, u32[]{:S(2)}, u32[]{:S(2)}) collective-permute-start(f32[5,1,8,16]{3,2,1,0:T(8,128)S(1)} %get-tuple-element.180), channel_id=1, source_target_pairs={{0,8},{8,16},{16,24},{24,0},{1,9},{9,17},{17,25},{25,1},{2,10},{10... | collective-permute-start | bytes 7688 | tf_op jit(solution)/shard_map/ppermute | solution.py:25
  82.4 4.3 collective-permute-start.16
  86.7 25.9 %collective-permute-start.19 = (f32[5,10,1,16]{3,2,1,0:T(1,128)S(1)}, f32[5,10,1,16]{3,2,1,0:T(1,128)S(1)}, u32[]{:S(2)}, u32[]{:S(2)}) collective-permute-start(f32[5,10,1,16]{3,2,1,0:T(1,128)S(1)} %get-tuple-element.150), channel_id=1, source_target_pairs={{0,4},{4,0},{1,5},{5,1},{2,6},{6,2},{3,7},{7,3},{8,12},{12,8},{9,1... | collective-permute-start | bytes 9608 | tf_op jit(solution)/shard_map/ppermute | solution.py:25
  87.4 25.2 %collective-permute-start.18 = (f32[5,10,1,16]{3,2,1,0:T(1,128)S(1)}, f32[5,10,1,16]{3,2,1,0:T(1,128)S(1)}, u32[]{:S(2)}, u32[]{:S(2)}) collective-permute-start(f32[5,10,1,16]{3,2,1,0:T(1,128)S(1)} %get-tuple-element.151), channel_id=1, source_target_pairs={{4,0},{0,4},{5,1},{1,5},{6,2},{2,6},{7,3},{3,7},{12,8},{8,12},{13,... | collective-permute-start | bytes 9608 | tf_op jit(solution)/shard_map/ppermute | solution.py:27
  117.6 9.7 %collective-permute-start.20 = (f32[1,8,16,768]{3,2,1,0:T(8,128)S(1)}, f32[1,8,16,768]{3,2,1,0:T(8,128)S(1)}, u32[]{:S(2)}, u32[]{:S(2)}) collective-permute-start(f32[1,8,16,768]{3,2,1,0:T(8,128)S(1)} %get-tuple-element.60), channel_id=1, source_target_pairs={{0,8},{8,16},{16,24},{24,0},{1,9},{9,17},{17,25},{25,1},{2,10},{10... | collective-permute-start | bytes 1179656 | tf_op jit(solution)/shard_map/ppermute | solution.py:25
  117.6 12.4 %collective-permute-start.21 = (f32[1,8,16,768]{3,2,1,0:T(8,128)S(1)}, f32[1,8,16,768]{3,2,1,0:T(8,128)S(1)}, u32[]{:S(2)}, u32[]{:S(2)}) collective-permute-start(f32[1,8,16,768]{3,2,1,0:T(8,128)S(1)} %get-tuple-element.61), channel_id=1, source_target_pairs={{8,0},{16,8},{24,16},{0,24},{9,1},{17,9},{25,17},{1,25},{10,2},{18... | collective-permute-start | bytes 1179656 | tf_op jit(solution)/shard_map/ppermute | solution.py:27
  130.1 8.9 %collective-permute-start.22 = (f32[10,1,16,768]{3,2,1,0:T(8,128)S(1)}, f32[10,1,16,768]{3,2,1,0:T(8,128)S(1)}, u32[]{:S(2)}, u32[]{:S(2)}) collective-permute-start(f32[10,1,16,768]{3,2,1,0:T(8,128)S(1)} %get-tuple-element.42), channel_id=1, source_target_pairs={{0,4},{4,0},{1,5},{5,1},{2,6},{6,2},{3,7},{7,3},{8,12},{12,8},{9,1... | collective-permute-start | bytes 1474568 | tf_op jit(solution)/shard_map/ppermute | solution.py:25
  130.2 14.1 %collective-permute-start.23 = (f32[10,1,16,768]{3,2,1,0:T(8,128)S(1)}, f32[10,1,16,768]{3,2,1,0:T(8,128)S(1)}, u32[]{:S(2)}, u32[]{:S(2)}) collective-permute-start(f32[10,1,16,768]{3,2,1,0:T(8,128)S(1)} %get-tuple-element.43), channel_id=1, source_target_pairs={{4,0},{0,4},{5,1},{1,5},{6,2},{2,6},{7,3},{3,7},{12,8},{8,12},{13,... | collective-permute-start | bytes 1474568 | tf_op jit(solution)/shard_map/ppermute | solution.py:27
  179.5 6.7 %collective-permute-start.25 = (f32[5,1,8,16]{3,2,1,0:T(8,128)S(1)}, f32[5,1,8,16]{3,2,1,0:T(8,128)S(1)}, u32[]{:S(2)}, u32[]{:S(2)}) collective-permute-start(f32[5,1,8,16]{3,2,1,0:T(8,128)S(1)} %get-tuple-element.82), channel_id=1, source_target_pairs={{0,8},{8,16},{16,24},{24,0},{1,9},{9,17},{17,25},{25,1},{2,10},{10... | collective-permute-start | bytes 7688 | tf_op jit(solution)/shard_map/ppermute | solution.py:25
  180.5 5.6 %collective-permute-start.24 = (f32[5,1,8,16]{3,2,1,0:T(8,128)S(1)}, f32[5,1,8,16]{3,2,1,0:T(8,128)S(1)}, u32[]{:S(2)}, u32[]{:S(2)}) collective-permute-start(f32[5,1,8,16]{3,2,1,0:T(8,128)S(1)} %get-tuple-element.83), channel_id=1, source_target_pairs={{8,0},{16,8},{24,16},{0,24},{9,1},{17,9},{25,17},{1,25},{10,2},{18... | collective-permute-start | bytes 7688 | tf_op jit(solution)/shard_map/ppermute | solution.py:27
  186.2 6.0 %collective-permute-start.27 = (f32[5,10,1,16]{3,2,1,0:T(1,128)S(1)}, f32[5,10,1,16]{3,2,1,0:T(1,128)S(1)}, u32[]{:S(2)}, u32[]{:S(2)}) collective-permute-start(f32[5,10,1,16]{3,2,1,0:T(1,128)S(1)} %get-tuple-element.146), channel_id=1, source_target_pairs={{0,4},{4,0},{1,5},{5,1},{2,6},{6,2},{3,7},{7,3},{8,12},{12,8},{9,1... | collective-permute-start | bytes 9608 | tf_op jit(solution)/shard_map/ppermute | solution.py:25
  186.3 5.9 %collective-permute-start.26 = (f32[5,10,1,16]{3,2,1,0:T(1,128)S(1)}, f32[5,10,1,16]{3,2,1,0:T(1,128)S(1)}, u32[]{:S(2)}, u32[]{:S(2)}) collective-permute-start(f32[5,10,1,16]{3,2,1,0:T(1,128)S(1)} %get-tuple-element.147), channel_id=1, source_target_pairs={{4,0},{0,4},{5,1},{1,5},{6,2},{2,6},{7,3},{3,7},{12,8},{8,12},{13,... | collective-permute-start | bytes 9608 | tf_op jit(solution)/shard_map/ppermute | solution.py:27
  188.3 6.0 %collective-permute-start.29 = (f32[13,1,8,16]{3,2,1,0:T(8,128)S(1)}, f32[13,1,8,16]{3,2,1,0:T(8,128)S(1)}, u32[]{:S(2)}, u32[]{:S(2)}) collective-permute-start(f32[13,1,8,16]{3,2,1,0:T(8,128)S(1)} %get-tuple-element.88), channel_id=1, source_target_pairs={{0,8},{8,16},{16,24},{24,0},{1,9},{9,17},{17,25},{25,1},{2,10},{10... | collective-permute-start | bytes 19976 | tf_op jit(solution)/shard_map/ppermute | solution.py:25
  188.4 6.0 %collective-permute-start.28 = (f32[13,1,8,16]{3,2,1,0:T(8,128)S(1)}, f32[13,1,8,16]{3,2,1,0:T(8,128)S(1)}, u32[]{:S(2)}, u32[]{:S(2)}) collective-permute-start(f32[13,1,8,16]{3,2,1,0:T(8,128)S(1)} %get-tuple-element.89), channel_id=1, source_target_pairs={{8,0},{16,8},{24,16},{0,24},{9,1},{17,9},{25,17},{1,25},{10,2},{18... | collective-permute-start | bytes 19976 | tf_op jit(solution)/shard_map/ppermute | solution.py:27
  194.4 4.3 collective-permute-start.31
  194.6 4.9 %collective-permute-start.30 = (f32[13,10,1,16]{3,2,1,0:T(1,128)S(1)}, f32[13,10,1,16]{3,2,1,0:T(1,128)S(1)}, u32[]{:S(2)}, u32[]{:S(2)}) collective-permute-start(f32[13,10,1,16]{3,2,1,0:T(1,128)S(1)} %get-tuple-element.75), channel_id=1, source_target_pairs={{4,0},{0,4},{5,1},{1,5},{6,2},{2,6},{7,3},{3,7},{12,8},{8,12},{13,... | collective-permute-start | bytes 24968 | tf_op jit(solution)/shard_map/ppermute | solution.py:27
  202.8 5.6 %collective-permute-start.33 = (f32[5,1,8,16]{3,2,1,0:T(8,128)S(1)}, f32[5,1,8,16]{3,2,1,0:T(8,128)S(1)}, u32[]{:S(2)}, u32[]{:S(2)}) collective-permute-start(f32[5,1,8,16]{3,2,1,0:T(8,128)S(1)} %get-tuple-element.176), channel_id=1, source_target_pairs={{0,8},{8,16},{16,24},{24,0},{1,9},{9,17},{17,25},{25,1},{2,10},{10... | collective-permute-start | bytes 7688 | tf_op jit(solution)/shard_map/ppermute | solution.py:25
  202.9 5.6 %collective-permute-start.32 = (f32[5,1,8,16]{3,2,1,0:T(8,128)S(1)}, f32[5,1,8,16]{3,2,1,0:T(8,128)S(1)}, u32[]{:S(2)}, u32[]{:S(2)}) collective-permute-start(f32[5,1,8,16]{3,2,1,0:T(8,128)S(1)} %get-tuple-element.177), channel_id=1, source_target_pairs={{8,0},{16,8},{24,16},{0,24},{9,1},{17,9},{25,17},{1,25},{10,2},{18... | collective-permute-start | bytes 7688 | tf_op jit(solution)/shard_map/ppermute | solution.py:27
  214.8 5.7 %collective-permute-start.37 = (f32[5,1,8,16]{3,2,1,0:T(8,128)S(1)}, f32[5,1,8,16]{3,2,1,0:T(8,128)S(1)}, u32[]{:S(2)}, u32[]{:S(2)}) collective-permute-start(f32[5,1,8,16]{3,2,1,0:T(8,128)S(1)} %get-tuple-element.174), channel_id=1, source_target_pairs={{0,8},{8,16},{16,24},{24,0},{1,9},{9,17},{17,25},{25,1},{2,10},{10... | collective-permute-start | bytes 7688 | tf_op jit(solution)/shard_map/ppermute | solution.py:25
  216.0 4.5 %collective-permute-start.36 = (f32[5,1,8,16]{3,2,1,0:T(8,128)S(1)}, f32[5,1,8,16]{3,2,1,0:T(8,128)S(1)}, u32[]{:S(2)}, u32[]{:S(2)}) collective-permute-start(f32[5,1,8,16]{3,2,1,0:T(8,128)S(1)} %get-tuple-element.175), channel_id=1, source_target_pairs={{8,0},{16,8},{24,16},{0,24},{9,1},{17,9},{25,17},{1,25},{10,2},{18... | collective-permute-start | bytes 7688 | tf_op jit(solution)/shard_map/ppermute | solution.py:27
  221.3 4.0 collective-permute-start.38
  226.5 5.7 %collective-permute-start.41 = (f32[5,1,8,16]{3,2,1,0:T(8,128)S(1)}, f32[5,1,8,16]{3,2,1,0:T(8,128)S(1)}, u32[]{:S(2)}, u32[]{:S(2)}) collective-permute-start(f32[5,1,8,16]{3,2,1,0:T(8,128)S(1)} %get-tuple-element.172), channel_id=1, source_target_pairs={{0,8},{8,16},{16,24},{24,0},{1,9},{9,17},{17,25},{25,1},{2,10},{10... | collective-permute-start | bytes 7688 | tf_op jit(solution)/shard_map/ppermute | solution.py:25
  227.6 4.5 %collective-permute-start.40 = (f32[5,1,8,16]{3,2,1,0:T(8,128)S(1)}, f32[5,1,8,16]{3,2,1,0:T(8,128)S(1)}, u32[]{:S(2)}, u32[]{:S(2)}) collective-permute-start(f32[5,1,8,16]{3,2,1,0:T(8,128)S(1)} %get-tuple-element.173), channel_id=1, source_target_pairs={{8,0},{16,8},{24,16},{0,24},{9,1},{17,9},{25,17},{1,25},{10,2},{18... | collective-permute-start | bytes 7688 | tf_op jit(solution)/shard_map/ppermute | solution.py:27
  232.8 26.8 %collective-permute-start.43 = (f32[5,10,1,16]{3,2,1,0:T(1,128)}, f32[5,10,1,16]{3,2,1,0:T(1,128)}, u32[]{:S(2)}, u32[]{:S(2)}) collective-permute-start(f32[5,10,1,16]{3,2,1,0:T(1,128)} %get-tuple-element.134), channel_id=1, source_target_pairs={{0,4},{4,0},{1,5},{5,1},{2,6},{6,2},{3,7},{7,3},{8,12},{12,8},{9,1... | collective-permute-start | bytes 9608 | tf_op jit(solution)/shard_map/ppermute | solution.py:25
  234.2 25.5 %collective-permute-start.42 = (f32[5,10,1,16]{3,2,1,0:T(1,128)}, f32[5,10,1,16]{3,2,1,0:T(1,128)}, u32[]{:S(2)}, u32[]{:S(2)}) collective-permute-start(f32[5,10,1,16]{3,2,1,0:T(1,128)} %get-tuple-element.135), channel_id=1, source_target_pairs={{4,0},{0,4},{5,1},{1,5},{6,2},{2,6},{7,3},{3,7},{12,8},{8,12},{13,... | collective-permute-start | bytes 9608 | tf_op jit(solution)/shard_map/ppermute | solution.py:27
  267.8 9.7 %collective-permute-start.44 = (f32[1,8,16,768]{3,2,1,0:T(8,128)S(1)}, f32[1,8,16,768]{3,2,1,0:T(8,128)S(1)}, u32[]{:S(2)}, u32[]{:S(2)}) collective-permute-start(f32[1,8,16,768]{3,2,1,0:T(8,128)S(1)} %get-tuple-element.54), channel_id=1, source_target_pairs={{0,8},{8,16},{16,24},{24,0},{1,9},{9,17},{17,25},{25,1},{2,10},{10... | collective-permute-start | bytes 1179656 | tf_op jit(solution)/shard_map/ppermute | solution.py:25
  267.9 12.4 %collective-permute-start.45 = (f32[1,8,16,768]{3,2,1,0:T(8,128)S(1)}, f32[1,8,16,768]{3,2,1,0:T(8,128)S(1)}, u32[]{:S(2)}, u32[]{:S(2)}) collective-permute-start(f32[1,8,16,768]{3,2,1,0:T(8,128)S(1)} %get-tuple-element.55), channel_id=1, source_target_pairs={{8,0},{16,8},{24,16},{0,24},{9,1},{17,9},{25,17},{1,25},{10,2},{18... | collective-permute-start | bytes 1179656 | tf_op jit(solution)/shard_map/ppermute | solution.py:27
  280.4 8.9 %collective-permute-start.46 = (f32[10,1,16,768]{3,2,1,0:T(8,128)S(1)}, f32[10,1,16,768]{3,2,1,0:T(8,128)S(1)}, u32[]{:S(2)}, u32[]{:S(2)}) collective-permute-start(f32[10,1,16,768]{3,2,1,0:T(8,128)S(1)} %get-tuple-element.40), channel_id=1, source_target_pairs={{0,4},{4,0},{1,5},{5,1},{2,6},{6,2},{3,7},{7,3},{8,12},{12,8},{9,1... | collective-permute-start | bytes 1474568 | tf_op jit(solution)/shard_map/ppermute | solution.py:25
  280.5 14.1 %collective-permute-start.47 = (f32[10,1,16,768]{3,2,1,0:T(8,128)S(1)}, f32[10,1,16,768]{3,2,1,0:T(8,128)S(1)}, u32[]{:S(2)}, u32[]{:S(2)}) collective-permute-start(f32[10,1,16,768]{3,2,1,0:T(8,128)S(1)} %get-tuple-element.41), channel_id=1, source_target_pairs={{4,0},{0,4},{5,1},{1,5},{6,2},{2,6},{7,3},{3,7},{12,8},{8,12},{13,... | collective-permute-start | bytes 1474568 | tf_op jit(solution)/shard_map/ppermute | solution.py:27
  329.7 6.7 %collective-permute-start.49 = (f32[5,1,8,16]{3,2,1,0:T(8,128)S(1)}, f32[5,1,8,16]{3,2,1,0:T(8,128)S(1)}, u32[]{:S(2)}, u32[]{:S(2)}) collective-permute-start(f32[5,1,8,16]{3,2,1,0:T(8,128)S(1)} %get-tuple-element.80), channel_id=1, source_target_pairs={{0,8},{8,16},{16,24},{24,0},{1,9},{9,17},{17,25},{25,1},{2,10},{10... | collective-permute-start | bytes 7688 | tf_op jit(solution)/shard_map/ppermute | solution.py:25
  329.7 6.7 %collective-permute-start.48 = (f32[5,1,8,16]{3,2,1,0:T(8,128)S(1)}, f32[5,1,8,16]{3,2,1,0:T(8,128)S(1)}, u32[]{:S(2)}, u32[]{:S(2)}) collective-permute-start(f32[5,1,8,16]{3,2,1,0:T(8,128)S(1)} %get-tuple-element.81), channel_id=1, source_target_pairs={{8,0},{16,8},{24,16},{0,24},{9,1},{17,9},{25,17},{1,25},{10,2},{18... | collective-permute-start | bytes 7688 | tf_op jit(solution)/shard_map/ppermute | solution.py:27
  336.5 6.0 %collective-permute-start.51 = (f32[5,10,1,16]{3,2,1,0:T(1,128)S(1)}, f32[5,10,1,16]{3,2,1,0:T(1,128)S(1)}, u32[]{:S(2)}, u32[]{:S(2)}) collective-permute-start(f32[5,10,1,16]{3,2,1,0:T(1,128)S(1)} %get-tuple-element.130), channel_id=1, source_target_pairs={{0,4},{4,0},{1,5},{5,1},{2,6},{6,2},{3,7},{7,3},{8,12},{12,8},{9,1... | collective-permute-start | bytes 9608 | tf_op jit(solution)/shard_map/ppermute | solution.py:25
  336.5 5.9 %collective-permute-start.50 = (f32[5,10,1,16]{3,2,1,0:T(1,128)S(1)}, f32[5,10,1,16]{3,2,1,0:T(1,128)S(1)}, u32[]{:S(2)}, u32[]{:S(2)}) collective-permute-start(f32[5,10,1,16]{3,2,1,0:T(1,128)S(1)} %get-tuple-element.131), channel_id=1, source_target_pairs={{4,0},{0,4},{5,1},{1,5},{6,2},{2,6},{7,3},{3,7},{12,8},{8,12},{13,... | collective-permute-start | bytes 9608 | tf_op jit(solution)/shard_map/ppermute | solution.py:27
  338.6 6.0 %collective-permute-start.53 = (f32[13,1,8,16]{3,2,1,0:T(8,128)S(1)}, f32[13,1,8,16]{3,2,1,0:T(8,128)S(1)}, u32[]{:S(2)}, u32[]{:S(2)}) collective-permute-start(f32[13,1,8,16]{3,2,1,0:T(8,128)S(1)} %get-tuple-element.86), channel_id=1, source_target_pairs={{0,8},{8,16},{16,24},{24,0},{1,9},{9,17},{17,25},{25,1},{2,10},{10... | collective-permute-start | bytes 19976 | tf_op jit(solution)/shard_map/ppermute | solution.py:25
  338.6 6.0 %collective-permute-start.52 = (f32[13,1,8,16]{3,2,1,0:T(8,128)S(1)}, f32[13,1,8,16]{3,2,1,0:T(8,128)S(1)}, u32[]{:S(2)}, u32[]{:S(2)}) collective-permute-start(f32[13,1,8,16]{3,2,1,0:T(8,128)S(1)} %get-tuple-element.87), channel_id=1, source_target_pairs={{8,0},{16,8},{24,16},{0,24},{9,1},{17,9},{25,17},{1,25},{10,2},{18... | collective-permute-start | bytes 19976 | tf_op jit(solution)/shard_map/ppermute | solution.py:27
  344.7 4.3 collective-permute-start.55
  344.8 4.9 %collective-permute-start.54 = (f32[13,10,1,16]{3,2,1,0:T(1,128)S(1)}, f32[13,10,1,16]{3,2,1,0:T(1,128)S(1)}, u32[]{:S(2)}, u32[]{:S(2)}) collective-permute-start(f32[13,10,1,16]{3,2,1,0:T(1,128)S(1)} %get-tuple-element.71), channel_id=1, source_target_pairs={{4,0},{0,4},{5,1},{1,5},{6,2},{2,6},{7,3},{3,7},{12,8},{8,12},{13,... | collective-permute-start | bytes 24968 | tf_op jit(solution)/shard_map/ppermute | solution.py:27
  353.1 5.6 %collective-permute-start.57 = (f32[5,1,8,16]{3,2,1,0:T(8,128)S(1)}, f32[5,1,8,16]{3,2,1,0:T(8,128)S(1)}, u32[]{:S(2)}, u32[]{:S(2)}) collective-permute-start(f32[5,1,8,16]{3,2,1,0:T(8,128)S(1)} %get-tuple-element.168), channel_id=1, source_target_pairs={{0,8},{8,16},{16,24},{24,0},{1,9},{9,17},{17,25},{25,1},{2,10},{10... | collective-permute-start | bytes 7688 | tf_op jit(solution)/shard_map/ppermute | solution.py:25
  353.1 5.6 %collective-permute-start.56 = (f32[5,1,8,16]{3,2,1,0:T(8,128)S(1)}, f32[5,1,8,16]{3,2,1,0:T(8,128)S(1)}, u32[]{:S(2)}, u32[]{:S(2)}) collective-permute-start(f32[5,1,8,16]{3,2,1,0:T(8,128)S(1)} %get-tuple-element.169), channel_id=1, source_target_pairs={{8,0},{16,8},{24,16},{0,24},{9,1},{17,9},{25,17},{1,25},{10,2},{18... | collective-permute-start | bytes 7688 | tf_op jit(solution)/shard_map/ppermute | solution.py:27
  365.1 5.7 %collective-permute-start.61 = (f32[5,1,8,16]{3,2,1,0:T(8,128)S(1)}, f32[5,1,8,16]{3,2,1,0:T(8,128)S(1)}, u32[]{:S(2)}, u32[]{:S(2)}) collective-permute-start(f32[5,1,8,16]{3,2,1,0:T(8,128)S(1)} %get-tuple-element.166), channel_id=1, source_target_pairs={{0,8},{8,16},{16,24},{24,0},{1,9},{9,17},{17,25},{25,1},{2,10},{10... | collective-permute-start | bytes 7688 | tf_op jit(solution)/shard_map/ppermute | solution.py:25
  366.2 4.5 %collective-permute-start.60 = (f32[5,1,8,16]{3,2,1,0:T(8,128)S(1)}, f32[5,1,8,16]{3,2,1,0:T(8,128)S(1)}, u32[]{:S(2)}, u32[]{:S(2)}) collective-permute-start(f32[5,1,8,16]{3,2,1,0:T(8,128)S(1)} %get-tuple-element.167), channel_id=1, source_target_pairs={{8,0},{16,8},{24,16},{0,24},{9,1},{17,9},{25,17},{1,25},{10,2},{18... | collective-permute-start | bytes 7688 | tf_op jit(solution)/shard_map/ppermute | solution.py:27
  371.6 4.0 collective-permute-start.62
  376.8 5.6 %collective-permute-start.65 = (f32[5,1,8,16]{3,2,1,0:T(8,128)S(1)}, f32[5,1,8,16]{3,2,1,0:T(8,128)S(1)}, u32[]{:S(2)}, u32[]{:S(2)}) collective-permute-start(f32[5,1,8,16]{3,2,1,0:T(8,128)S(1)} %get-tuple-element.164), channel_id=1, source_target_pairs={{0,8},{8,16},{16,24},{24,0},{1,9},{9,17},{17,25},{25,1},{2,10},{10... | collective-permute-start | bytes 7688 | tf_op jit(solution)/shard_map/ppermute | solution.py:25
  377.9 4.5 %collective-permute-start.64 = (f32[5,1,8,16]{3,2,1,0:T(8,128)S(1)}, f32[5,1,8,16]{3,2,1,0:T(8,128)S(1)}, u32[]{:S(2)}, u32[]{:S(2)}) collective-permute-start(f32[5,1,8,16]{3,2,1,0:T(8,128)S(1)} %get-tuple-element.165), channel_id=1, source_target_pairs={{8,0},{16,8},{24,16},{0,24},{9,1},{17,9},{25,17},{1,25},{10,2},{18... | collective-permute-start | bytes 7688 | tf_op jit(solution)/shard_map/ppermute | solution.py:27
  383.1 27.1 %collective-permute-start.67 = (f32[5,10,1,16]{3,2,1,0:T(1,128)}, f32[5,10,1,16]{3,2,1,0:T(1,128)S(1)}, u32[]{:S(2)}, u32[]{:S(2)}) collective-permute-start(f32[5,10,1,16]{3,2,1,0:T(1,128)} %get-tuple-element.118), channel_id=1, source_target_pairs={{0,4},{4,0},{1,5},{5,1},{2,6},{6,2},{3,7},{7,3},{8,12},{12,8},{9,1... | collective-permute-start | bytes 9608 | tf_op jit(solution)/shard_map/ppermute | solution.py:25
  384.4 25.7 %collective-permute-start.66 = (f32[5,10,1,16]{3,2,1,0:T(1,128)}, f32[5,10,1,16]{3,2,1,0:T(1,128)S(1)}, u32[]{:S(2)}, u32[]{:S(2)}) collective-permute-start(f32[5,10,1,16]{3,2,1,0:T(1,128)} %get-tuple-element.119), channel_id=1, source_target_pairs={{4,0},{0,4},{5,1},{1,5},{6,2},{2,6},{7,3},{3,7},{12,8},{8,12},{13,... | collective-permute-start | bytes 9608 | tf_op jit(solution)/shard_map/ppermute | solution.py:27
  415.2 9.7 %collective-permute-start.68 = (f32[1,8,16,768]{3,2,1,0:T(8,128)S(1)}, f32[1,8,16,768]{3,2,1,0:T(8,128)S(1)}, u32[]{:S(2)}, u32[]{:S(2)}) collective-permute-start(f32[1,8,16,768]{3,2,1,0:T(8,128)S(1)} %get-tuple-element.48), channel_id=1, source_target_pairs={{0,8},{8,16},{16,24},{24,0},{1,9},{9,17},{17,25},{25,1},{2,10},{10... | collective-permute-start | bytes 1179656 | tf_op jit(solution)/shard_map/ppermute | solution.py:25
  415.2 12.0 %collective-permute-start.69 = (f32[1,8,16,768]{3,2,1,0:T(8,128)S(1)}, f32[1,8,16,768]{3,2,1,0:T(8,128)S(1)}, u32[]{:S(2)}, u32[]{:S(2)}) collective-permute-start(f32[1,8,16,768]{3,2,1,0:T(8,128)S(1)} %get-tuple-element.49), channel_id=1, source_target_pairs={{8,0},{16,8},{24,16},{0,24},{9,1},{17,9},{25,17},{1,25},{10,2},{18... | collective-permute-start | bytes 1179656 | tf_op jit(solution)/shard_map/ppermute | solution.py:27
  427.3 8.9 %collective-permute-start.70 = (f32[10,1,16,768]{3,2,1,0:T(8,128)S(1)}, f32[10,1,16,768]{3,2,1,0:T(8,128)S(1)}, u32[]{:S(2)}, u32[]{:S(2)}) collective-permute-start(f32[10,1,16,768]{3,2,1,0:T(8,128)S(1)} %get-tuple-element.38), channel_id=1, source_target_pairs={{0,4},{4,0},{1,5},{5,1},{2,6},{6,2},{3,7},{7,3},{8,12},{12,8},{9,1... | collective-permute-start | bytes 1474568 | tf_op jit(solution)/shard_map/ppermute | solution.py:25
  427.4 14.1 %collective-permute-start.71 = (f32[10,1,16,768]{3,2,1,0:T(8,128)S(1)}, f32[10,1,16,768]{3,2,1,0:T(8,128)S(1)}, u32[]{:S(2)}, u32[]{:S(2)}) collective-permute-start(f32[10,1,16,768]{3,2,1,0:T(8,128)S(1)} %get-tuple-element.39), channel_id=1, source_target_pairs={{4,0},{0,4},{5,1},{1,5},{6,2},{2,6},{7,3},{3,7},{12,8},{8,12},{13,... | collective-permute-start | bytes 1474568 | tf_op jit(solution)/shard_map/ppermute | solution.py:27
  (43 other events, 808.4 us)
where the time goes:
time: 457 us; the launch traced here: 450 us
  blocking collectives  117 us (26%)
  starting transfers between devices  109 us (24%)
  waiting for transfers between devices  106 us (23%)
  matrix products  63.9 us (14%)
  other arithmetic  31.8 us (7%)
  local copies, waits for them, and re-layouts  17.1 us (4%)
  between operations  5.41 us (1%)
    ppermute x36, starting transfers between devices, padded_2(): lax.ppermute(head, axis, [((i + 1) % count, i) for i in range(count)])  82.2 us
    ppermute x36, waiting for transfers between devices, padded_2(): lax.ppermute(tail, axis, [(i, (i + 1) % count) for i in range(count)])  72.4 us
    psum x3, blocking collectives, total_mass(): summed = lax.psum(local_sum, ('tx', 'ty'))  67.4 us
    psum x3, blocking collectives, on_device(): moments = lax.psum(local_moments, 'vel')  49.5 us
    dot_general x3, matrix products, on_device(): jnp.einsum('kv,xyzv->kxyz', moment_rows, distribution, precision=highest)  35.4 us
    ppermute x36, waiting for transfers between devices, padded_2(): lax.ppermute(head, axis, [((i + 1) % count, i) for i in range(count)])  33.4 us
    ppermute x36, starting transfers between devices, padded_2(): lax.ppermute(tail, axis, [(i, (i + 1) % count) for i in range(count)])  26.5 us
    dot_general x3, matrix products, on_device(): jnp.einsum('kxyz,kv->xyzv', macro_state, rows, precision=highest)  20.1 us
  transfers between devices with their start and end apart: 72, of which 44 were waited for; matrix products, arithmetic and copies ran while one was open for 3% of the time, Pallas kernels for 0%

commit v1 on v0

v1 whole, which is shorter than its diff:
```python
import functools

import jax
import jax.numpy as jnp
from jax import lax
from jax.experimental import pallas as pl
from jax.experimental.pallas import tpu as pltpu
from jax.sharding import PartitionSpec as P

ITERS = 3
MACRO_STEPS = 4

STEP_TIME = 0.1
COLLISION = 1.0
MACRO_TIME = 0.1
VISCOSITY = 1.0
CONDUCTION = 1.0

LANES = 128
MOMENTS = 14
PROWS = 16
KROWS = 48
f32 = jnp.float32
bf16 = jnp.bfloat16


def split(value):
    high = value.astype(bf16)
    return high, (value - high.astype(f32)).astype(bf16)


def dot(a, b, contract):
    return lax.dot_general(a, b, (contract, ((), ())), preferred_element_type=f32)


def local_moments(proj, plane):
    high, low = split(plane)
    both = dot(proj, high, ((1,), (1,)))
    return both[:PROWS] + both[PROWS:] + dot(proj[:PROWS], low, ((1,), (1,)))


def prepare_kernel(vel, wgt, h, mom, proj, wmat, coef, ysend, xup, xdown, rows, *, total):
    x = pl.program_id(0)
    planes = pl.num_programs(0)
    vx, vy, vz = vel[0:1, :], vel[1:2, :], vel[2:3, :]

    @pl.when(x == 0)
    def _():
        speed = vx * vx + vy * vy + vz * vz
        scale = wgt[...] / total
        one = jnp.ones_like(speed)
        zero = jnp.zeros_like(speed)
        table = [
            one,
            vx,
            vy,
            vz,
            2.0 / 3.0 * speed - 1.0,
            2.0 * (vx * vx - speed / 3.0),
            2.0 * (vy * vy - speed / 3.0),
            2.0 * (vz * vz - speed / 3.0),
            2.0 * vx * vy,
            2.0 * vx * vz,
            2.0 * vy * vz,
            vx * (speed - 2.5),
            vy * (speed - 2.5),
            vz * (speed - 2.5),
        ]
        for k, row in enumerate(table):
            rows[k : k + 1, :] = row * scale
        for k in range(MOMENTS, PROWS):
            rows[k : k + 1, :] = zero
        high, low = split(rows[0:PROWS, :])
        proj[0:PROWS, :] = high
        proj[PROWS : 2 * PROWS, :] = low
        along_x, along_y, along_z = (STEP_TIME * jnp.abs(v) for v in (vx, vy, vz))
        centre = (1.0 - STEP_TIME * COLLISION) - (along_x + along_y + along_z)
        for k, row in enumerate([centre, along_x, along_y, along_z, vy, vz, zero, zero]):
            coef[k : k + 1, :] = row
        basis = [one, 2.0 * vx, 2.0 * vy, 2.0 * vz, speed - 1.5]
        parts = [
            centre,
            jnp.where(vx > 0.0, along_x, 0.0),
            jnp.where(vx > 0.0, 0.0, along_x),
            jnp.where(vy > 0.0, along_y, 0.0),
            jnp.where(vy > 0.0, 0.0, along_y),
            jnp.where(vz > 0.0, along_z, 0.0),
            jnp.where(vz > 0.0, 0.0, along_z),
            STEP_TIME * COLLISION * one,
        ]
        for i, part in enumerate(parts):
            for k, row in enumerate(basis):
                rows[5 * i + k : 5 * i + k + 1, :] = part * row
        rows[40:41, :] = one
        rows[41:42, :] = basis[4]
        for k in range(42, KROWS):
            rows[k : k + 1, :] = zero
        high, low = split(rows[...])
        wmat[0:KROWS, :] = high
        wmat[KROWS : 2 * KROWS, :] = high
        wmat[2 * KROWS : 3 * KROWS, :] = low

    _, ny, nz, nv = h.shape
    plane = h[0].reshape(ny * nz, nv)
    out = local_moments(proj[...], plane)
    mom[pl.ds(x, MOMENTS, stride=planes), :] = out[:MOMENTS]
    ysend[0] = jnp.where(vy > 0.0, plane[(ny - 1) * nz :], plane[:nz])

    @pl.when(x == planes - 1)
    def _():
        xup[...] = h[0, :, :, : nv // 2]

    @pl.when(x == 0)
    def _():
        xdown[...] = h[0, :, :, nv // 2 :]


def prepare(initial, velocity, weights, total):
    nx, ny, nz, nv = initial.shape
    whole = lambda *shape: pl.BlockSpec(shape, lambda x: (0,) * len(shape))
    return pl.pallas_call(
        functools.partial(prepare_kernel, total=total),
        grid=(nx,),
        in_specs=[whole(3, nv), whole(1, nv), pl.BlockSpec((1, ny, nz, nv), lambda x: (x, 0, 0, 0))],
        out_specs=[
            whole(MOMENTS * nx, ny * nz),
            whole(2 * PROWS, nv),
            whole(3 * KROWS, nv),
            whole(8, nv),
            pl.BlockSpec((1, nz, nv), lambda x: (x, 0, 0)),
            whole(ny, nz, nv // 2),
            whole(ny, nz, nv // 2),
        ],
        out_shape=[
            jax.ShapeDtypeStruct((MOMENTS * nx, ny * nz), f32),
            jax.ShapeDtypeStruct((2 * PROWS, nv), bf16),
            jax.ShapeDtypeStruct((3 * KROWS, nv), bf16),
            jax.ShapeDtypeStruct((8, nv), f32),
            jax.ShapeDtypeStruct((nx, nz, nv), f32),
            jax.ShapeDtypeStruct((ny, nz, nv // 2), f32),
            jax.ShapeDtypeStruct((ny, nz, nv // 2), f32),
        ],
        scratch_shapes=[pltpu.VMEM((KROWS, nv), f32)],
        name="prepare",
    )(velocity, weights[None], initial)


def stream_kernel(h, yhalo, xbefore, xafter, coef, fluid, g):
    nx, ny, nz, nv = h.shape
    tiles = nv // LANES
    for j in range(tiles):
        lanes = slice(j * LANES, (j + 1) * LANES)
        forward_x = j < tiles // 2
        half = slice(lanes.start % (nv // 2), lanes.start % (nv // 2) + LANES)
        row = lambda k: jnp.broadcast_to(coef[k : k + 1, lanes], (nz, LANES))
        centre, along_x, along_y, along_z = (row(k) for k in range(4))
        up_z = row(5) > 0.0
        quarters = {(lanes.start * 4) // nv, ((lanes.stop - 1) * 4) // nv}
        signs = {q % 2 == 0 for q in quarters}
        up_y = row(4) > 0.0
        for x in range(nx):
            for y in range(ny):
                c = h[x, y, :, lanes]
                if forward_x:
                    ux = h[x - 1, y, :, lanes] if x > 0 else xbefore[y, :, half]
                else:
                    ux = h[x + 1, y, :, lanes] if x < nx - 1 else xafter[y, :, half]
                before = h[x, y - 1, :, lanes] if y > 0 else yhalo[x, :, lanes]
                after = h[x, y + 1, :, lanes] if y < ny - 1 else yhalo[x, :, lanes]
                if signs == {True}:
                    uy = before
                elif signs == {False}:
                    uy = after
                else:
                    uy = jnp.where(up_y, before, after)
                uz = jnp.where(up_z, pltpu.roll(c, 1, 0), pltpu.roll(c, nz - 1, 0))
                out = (centre * c + along_x * ux) + (along_y * uy + along_z * uz)
                g[x, y, :, lanes] = out * fluid[x, y]


def stream(h, yhalo, xbefore, xafter, coef, fluid):
    return pl.pallas_call(
        stream_kernel,
        out_shape=jax.ShapeDtypeStruct(h.shape, f32),
        name="stream",
        cost_estimate=pl.CostEstimate(flops=2_000_000, bytes_accessed=8_000_000, transcendentals=0),
    )(h, yhalo, xbefore, xafter, coef, fluid)


def macro_kernel(target, own, side, left, left_side, right, right_side, far, fluid, heat, mix, state_out, *, cells, nz, last):
    nx, width = fluid.shape

    def field(k):
        part = slice(k * nx, (k + 1) * nx)
        here = jnp.concatenate([left[part], own[part], right[part]], axis=0)
        there = jnp.concatenate([left_side[part], side[part], right_side[part]], axis=0)
        return jnp.concatenate([here, there], axis=1)

    rows, lanes = 3 * nx, 2 * width
    depth = lax.broadcasted_iota(jnp.int32, (rows, lanes), 1) % nz
    first, final = depth == 0, depth == nz - 1

    def shift(v, direction, offset):
        if direction == 0:
            return pltpu.roll(v, 1 if offset < 0 else rows - 1, 0)
        if direction == 1:
            return pltpu.roll(v, nz if offset < 0 else lanes - nz, 1)
        if offset < 0:
            return jnp.where(first, pltpu.roll(v, lanes - nz + 1, 1), pltpu.roll(v, 1, 1))
        return jnp.where(final, pltpu.roll(v, nz - 1, 1), pltpu.roll(v, lanes - 1, 1))

    def around(v, directions=(0, 1, 2)):
        return {d: (shift(v, d, 1), shift(v, d, -1)) for d in directions}

    def grad(pair):
        return (pair[0] - pair[1]) * 0.5

    def laplace(v, near):
        total = (near[0][0] + near[0][1]) + (near[1][0] + near[1][1]) + (near[2][0] + near[2][1])
        return total - 6.0 * v

    def slope(v, d):
        return grad(around(v, (d,))[d])

    state = [field(k) for k in range(5)]
    kinetic = state
    near = [None] + [around(state[k]) for k in range(1, 5)]
    stress = [field(5 + k) for k in range(9)]
    sums = [
        slope(stress[0], 0) + slope(stress[3], 1) + slope(stress[4], 2),
        slope(stress[3], 0) + slope(stress[1], 1) + slope(stress[5], 2),
        slope(stress[4], 0) + slope(stress[5], 1) + slope(stress[2], 2),
    ]
    flow = slope(stress[6], 0) + slope(stress[7], 1) + slope(stress[8], 2)
    sources = [-0.5 * (sums[i] + VISCOSITY * laplace(state[1 + i], near[1 + i])) for i in range(3)]
    sources.append(-(2.0 / 3.0) * (flow + CONDUCTION * laplace(state[4], near[4])))
    for step in range(MACRO_STEPS):
        if step:
            near = [None] + [around(state[k]) for k in range(1, 5)]
        near[0] = around(state[0])
        div = grad(near[1][0]) + grad(near[2][1]) + grad(near[3][2])
        rates = [-div]
        for i in range(3):
            rates.append(
                -0.5 * (grad(near[0][i]) + grad(near[4][i]))
                + 0.5 * VISCOSITY * laplace(state[1 + i], near[1 + i])
                + sources[i]
            )
        rates.append(-(2.0 / 3.0) * div + 2.0 / 3.0 * CONDUCTION * laplace(state[4], near[4]) + sources[3])
        state = [s + MACRO_TIME * r for s, r in zip(state, rates)]

    mass = far[...]
    for part in (own, side, left, left_side, right, right_side):
        mass = mass + part[0:nx]
    mass = jnp.sum(jnp.sum(mass, axis=0, keepdims=True), axis=1, keepdims=True)
    shift_all = jnp.broadcast_to(target[0] - mass / cells, (nx, width))
    is_fluid = fluid[...]

    def centre(v):
        return v[nx : 2 * nx, :width]

    def emit(k, value):
        mix[pl.ds(k, nx, stride=KROWS), :] = value

    change = [s - k for s, k in zip(state, kinetic)]
    for k in range(5):
        emit(k, centre(change[k]) * is_fluid)
        for d in range(3):
            emit(5 + 10 * d + k, centre(shift(change[k], d, -1)) * is_fluid)
            emit(10 + 10 * d + k, centre(shift(change[k], d, 1)) * is_fluid)
        emit(35 + k, centre(state[k]) * is_fluid)
    emit(40, shift_all * is_fluid)
    emit(41, heat[...] * (1.0 - is_fluid))
    for k in range(42, KROWS):
        emit(k, jnp.zeros((nx, width), f32))
    for k in range(5):
        value = centre(state[k])
        state_out[k] = value + shift_all if k == 0 else value


def macro(target, own, side, left, left_side, right, right_side, far, fluid, heat, cells, nz):
    nx, width = fluid.shape
    vmem = pl.BlockSpec(memory_space=pltpu.VMEM)
    return pl.pallas_call(
        functools.partial(macro_kernel, cells=cells, nz=nz, last=False),
        in_specs=[pl.BlockSpec(memory_space=pltpu.SMEM)] + [vmem] * 9,
        out_shape=[
            jax.ShapeDtypeStruct((KROWS * nx, width), f32),
            jax.ShapeDtypeStruct((5, nx, width), f32),
        ],
        name="macro",
    )(target, own, side, left, left_side, right, right_side, far, fluid, heat)


def update_kernel(g, mix, wmat, proj, coef, *outs, last):
    nx, ny, nz, nv = g.shape
    h = outs[0]
    half = nv // 2
    for x in range(nx):
        columns = mix[x * KROWS : (x + 1) * KROWS, :].T
        high, low = split(columns)
        lhs = jnp.concatenate([high, low, high], axis=1)
        add = dot(lhs, wmat[...], ((1,), (0,)))
        plane = g[x].reshape(ny * nz, nv) + add
        h[x] = plane.reshape(ny, nz, nv)
        if not last:
            mom, ysend, xup, xdown = outs[1:]
            out = local_moments(proj[...], plane)
            mom[pl.ds(x, MOMENTS, stride=nx), :] = out[:MOMENTS]
            ysend[x] = jnp.where(coef[4:5, :] > 0.0, plane[(ny - 1) * nz :], plane[:nz])
            if x == nx - 1:
                xup[...] = h[x, :, :, :half]
            if x == 0:
                xdown[...] = h[x, :, :, half:]


def update(g, mix, wmat, proj, coef, last):
    nx, ny, nz, nv = g.shape
    shapes = [jax.ShapeDtypeStruct(g.shape, f32)]
    if not last:
        shapes += [
            jax.ShapeDtypeStruct((MOMENTS * nx, ny * nz), f32),
            jax.ShapeDtypeStruct((nx, nz, nv), f32),
            jax.ShapeDtypeStruct((ny, nz, nv // 2), f32),
            jax.ShapeDtypeStruct((ny, nz, nv // 2), f32),
        ]
    return pl.pallas_call(
        functools.partial(update_kernel, last=last),
        out_shape=shapes,
        name="update",
    )(g, mix, wmat, proj, coef)


def ring(value, axis, step):
    count = lax.axis_size(axis)
    return lax.ppermute(value, axis, [(i, (i + step) % count) for i in range(count)])


def on_device(initial, velocity, weights, wall, wall_temp, mass_target):
    nx, ny, nz, nv = initial.shape
    width = ny * nz
    n_tx, n_ty, n_vel = (lax.axis_size(a) for a in ("tx", "ty", "vel"))
    if n_ty != 2 or n_tx < 3 or nx <= MACRO_STEPS or width != LANES or n_vel & (n_vel - 1):
        raise ValueError("unsupported sizes")
    cells = float(nx * width * n_tx * n_ty)
    top = n_vel // 2

    def plane_pair(value, flip_y, flip_v):
        pairs = []
        for y in range(n_ty):
            for v in range(n_vel):
                pairs.append((y * n_vel + v, (y ^ flip_y) * n_vel + (v ^ flip_v)))
        return lax.ppermute(value, ("ty", "vel"), pairs)

    fluid = jnp.where(wall == 1, 0.0, 1.0).astype(f32)
    fluid_rows = fluid.reshape(nx, width)
    heat = wall_temp.reshape(nx, width)
    fluid_cells = jnp.broadcast_to(fluid[..., None], (nx, ny, nz, LANES))
    target = mass_target[None]
    mom, proj, wmat, coef, ysend, xup, xdown = prepare(initial, velocity, weights, float(nv * n_vel))
    h = initial
    for iteration in range(ITERS):
        last = iteration == ITERS - 1
        bit = 1
        while bit < top:
            mom = mom + plane_pair(mom, 0, bit)
            bit *= 2
        own = mom + plane_pair(mom, 0, top)
        side = plane_pair(mom, 1, 0) + plane_pair(mom, 1, top)
        left, left_side = ring(own, "tx", 1), ring(side, "tx", 1)
        right, right_side = ring(own, "tx", -1), ring(side, "tx", -1)
        sums = own[0:nx] + side[0:nx]
        far = sum([ring(sums, "tx", d) for d in range(2, n_tx - 1)], jnp.zeros_like(sums))
        yhalo = ring(ysend, "ty", 1)
        xbefore, xafter = ring(xup, "tx", 1), ring(xdown, "tx", -1)
        g = stream(h, yhalo, xbefore, xafter, coef, fluid_cells)
        mix, state = macro(target, own, side, left, left_side, right, right_side, far, fluid_rows, heat, cells, nz)
        outs = update(g, mix, wmat, proj, coef, last)
        h = outs[0]
        if not last:
            mom, ysend, xup, xdown = outs[1:]
    return h, state.reshape(5, nx, ny, nz)


def solution(mesh):
    placed = (
        P("tx", "ty", None, "vel"),
        P(None, "vel"),
        P("vel"),
        P("tx", "ty", None),
        P("tx", "ty", None),
        P(),
    )
    return jax.shard_map(
        on_device,
        mesh=mesh,
        in_specs=placed,
        out_specs=(P("tx", "ty", None, "vel"), P(None, "tx", "ty", None)),
        check_vma=False,
    )
```

time: 457 us -> 141 us (0.31); the launches traced: 450 us -> 141 us
  blocking collectives: 117 us -> 0 us
  waiting for transfers between devices: 106 us -> 27.7 us
  matrix products: 63.9 us -> 0 us
  starting transfers between devices: 109 us -> 53.1 us
  Pallas kernels: 0 us -> 46.8 us
  other arithmetic: 31.8 us -> 2.55 us
  local copies, waits for them, and re-layouts: 17.1 us -> 8.66 us
    psum x6 -> x0, blocking collectives: 117 us -> none  [the longest x3 67.4 us: total_mass(): summed = lax.psum(local_sum, ('tx', 'ty'))]
    ppermute x72 -> x36, waiting for transfers between devices: 106 us -> 27.7 us  [the longest x24 21.6 us: ring(): lax.ppermute(value, axis, [(i, (i + step) % count) for i in range(count)])]
    dot_general x9 -> x0, matrix products: 63.9 us -> none  [the longest x3 35.4 us: on_device(): jnp.einsum('kv,xyzv->kxyz', moment_rows, distribution, precision=highest)]
    ppermute x72 -> x36, starting transfers between devices: 109 us -> 53.1 us  [the longest x24 41.2 us: ring(): lax.ppermute(value, axis, [(i, (i + step) % count) for i in range(count)])]
    pallas_call x0 -> x10, Pallas kernels: none -> 46.8 us  [the longest x3 15.9 us: update(): pl.pallas_call(functools.partial(update_kernel, last=last), out_shape=sha...]
    slice x49 -> x0, local copies, waits for them, and re-layouts: 13.4 us -> none  [the longest x6 3.83 us: on_device(): fields = jnp.concatenate([moments[5:14], moments[1:5]])]
    mul x31 -> x0, other arithmetic: 9.75 us -> none  [the longest x30 8.9 us: differences(): (shifted(direction, 1) - shifted(direction, -1)) * 0.5]
    add x30 -> x12, other arithmetic: 8.85 us -> 2.55 us  [the longest x3 2.48 us: on_device(): mom = mom + plane_pair(mom, 0, bit)]
  transfers between devices with their start and end apart: 72 -> 36, of which waited for: 44 -> 17; matrix products, arithmetic and copies ran while one was open for 3% -> 2% of each run, Pallas kernels for 0% -> 6%
where the time goes in v1:
time: 141 us
  starting transfers between devices  53.1 us (38%)
  Pallas kernels  46.8 us (33%)
  waiting for transfers between devices  27.7 us (20%)
  local copies, waits for them, and re-layouts  8.66 us (6%)
  other arithmetic  2.55 us (2%)
  between operations  1.66 us (1%)
    ppermute x24, starting transfers between devices, ring(): lax.ppermute(value, axis, [(i, (i + step) % count) for i in range(count)])  41.2 us
    ppermute x24, waiting for transfers between devices, ring(): lax.ppermute(value, axis, [(i, (i + step) % count) for i in range(count)])  21.6 us
    pallas_call x3, Pallas kernels, update(): pl.pallas_call(functools.partial(update_kernel, last=last), out_shape=sha...  15.9 us
    pallas_call x3, Pallas kernels, stream(): pl.pallas_call(stream_kernel, out_shape=jax.ShapeDtypeStruct(h.shape, f32...  15.9 us
    ppermute x12, starting transfers between devices, plane_pair(): return lax.ppermute(value, ('ty', 'vel'), pairs)  11.9 us
    pallas_call x3, Pallas kernels, macro(): pl.pallas_call(functools.partial(macro_kernel, cells=cells, nz=nz, last=F...  8.37 us
    pallas_call x1, Pallas kernels, prepare(): pl.pallas_call(functools.partial(prepare_kernel, total=total), grid=(nx,)...  6.63 us
    ppermute x12, waiting for transfers between devices, plane_pair(): return lax.ppermute(value, ('ty', 'vel'), pairs)  6.1 us
  transfers between devices with their start and end apart: 36, of which 17 were waited for; matrix products, arithmetic and copies ran while one was open for 2% of the time, Pallas kernels for 6%

profile of v1, /device:TPU:0, one launch (start us, length us, event | category | flops | bytes accessed | tf_op | source)
XLA Modules:
  0.0 140.5 jit_solution(8009080610829692037)
XLA Ops:
  0.7 1.3 broadcast_in_dim.20.wgt
  1.9 6.6 %prepare.1 = (f32[112,128]{1,0:T(8,128)}, bf16[32,768]{1,0:T(8,128)(2,1)}, bf16[144,768]{1,0:T(8,128)(2,1)}, f32[8,768]{1,0:T(8,128)}, f32[8,16,768]{2,1,0:T(8,1...) custom-call(f32[3,768]{1,0:T(4,128)} %vel.1, f32[1,768]{1,0:T(1,128)} %broadcast_in_dim.20.wgt, f32[8,8,16,768]{3,2,1,0:T(8,128)} %h.3), custom_call_target="tpu_custom_call" | custom-call | tf_op jit(solution)/shard_map/prepare/pallas_call | solution.py:121
  8.6 0.5 collective-permute-start.3
  9.1 1.1 collective-permute-done.3
  10.2 0.8 add.36
  11.0 2.9 %collective-permute-start.5 = (f32[112,128]{1,0:T(8,128)S(1)}, f32[112,128]{1,0:T(8,128)S(1)}, u32[]{:S(2)}, u32[]{:S(2)}) collective-permute-start(f32[112,128]{1,0:T(8,128)S(1)} %add.36), channel_id=1, source_target_pairs={{0,4},{1,5},{2,6},{3,7},{4,0},{5,1},{6,2},{7,3},{8,12},{9,13},{10,... | collective-permute-start | bytes 172040 | tf_op jit(solution)/shard_map/ppermute | solution.py:353
  13.9 1.4 %collective-permute-start.6 = (f32[112,128]{1,0:T(8,128)S(1)}, f32[112,128]{1,0:T(8,128)S(1)}, u32[]{:S(2)}, u32[]{:S(2)}) collective-permute-start(f32[112,128]{1,0:T(8,128)S(1)} %add.36), channel_id=1, source_target_pairs={{0,6},{1,7},{2,4},{3,5},{4,2},{5,3},{6,0},{7,1},{8,14},{9,15},{10,... | collective-permute-start | bytes 172040 | tf_op jit(solution)/shard_map/ppermute | solution.py:353
  15.4 2.0 %collective-permute-start = (f32[8,16,768]{2,1,0:T(8,128)}, f32[8,16,768]{2,1,0:T(8,128)S(1)}, u32[]{:S(2)}, u32[]{:S(2)}) collective-permute-start(f32[8,16,768]{2,1,0:T(8,128)} %get-tuple-element.23), channel_id=1, source_target_pairs={{0,4},{4,0},{1,5},{5,1},{2,6},{6,2},{3,7},{7,3},{8,12},{12,8},{9,1... | collective-permute-start | bytes 1179656 | tf_op jit(solution)/shard_map/ppermute | solution.py:336
  17.4 2.1 %collective-permute-done.6 = f32[112,128]{1,0:T(8,128)S(1)} collective-permute-done((f32[112,128]{1,0:T(8,128)S(1)}, f32[112,128]{1,0:T(8,128)S(1)}, u32[]{:S(2)}, u32[]{:S(2)}) %collective-permute-start.6) | collective-permute-done | bytes 57376 | tf_op jit(solution)/shard_map/ppermute | solution.py:353
  19.5 3.7 %collective-permute-start.10 = (f32[112,128]{1,0:T(8,128)S(1)}, f32[112,128]{1,0:T(8,128)S(1)}, u32[]{:S(2)}, u32[]{:S(2)}) collective-permute-start(f32[112,128]{1,0:T(8,128)S(1)} %add.38.side), channel_id=1, source_target_pairs={{0,24},{8,0},{16,8},{24,16},{1,25},{9,1},{17,9},{25,17},{2,26},{10... | collective-permute-start | bytes 172040 | tf_op jit(solution)/shard_map/ppermute | solution.py:336
  23.2 1.1 collective-permute-start.11
  24.2 3.4 %collective-permute-start.1 = (f32[8,16,384]{2,1,0:T(8,128)}, f32[8,16,384]{2,1,0:T(8,128)S(1)}, u32[]{:S(2)}, u32[]{:S(2)}) collective-permute-start(f32[8,16,384]{2,1,0:T(8,128)} %get-tuple-element.24), channel_id=1, source_target_pairs={{0,8},{8,16},{16,24},{24,0},{1,9},{9,17},{17,25},{25,1},{2,10},{10... | collective-permute-start | bytes 589832 | tf_op jit(solution)/shard_map/ppermute | solution.py:336
  27.6 0.6 collective-permute-done.11.far
  28.2 3.4 %collective-permute-start.2 = (f32[8,16,384]{2,1,0:T(8,128)}, f32[8,16,384]{2,1,0:T(8,128)S(1)}, u32[]{:S(2)}, u32[]{:S(2)}) collective-permute-start(f32[8,16,384]{2,1,0:T(8,128)} %get-tuple-element.25), channel_id=1, source_target_pairs={{0,24},{8,0},{16,8},{24,16},{1,25},{9,1},{17,9},{25,17},{2,26},{10... | collective-permute-start | bytes 589832 | tf_op jit(solution)/shard_map/ppermute | solution.py:336
  31.6 3.8 %collective-permute-start.9 = (f32[112,128]{1,0:T(8,128)S(1)}, f32[112,128]{1,0:T(8,128)S(1)}, u32[]{:S(2)}, u32[]{:S(2)}) collective-permute-start(f32[112,128]{1,0:T(8,128)S(1)} %add.37.own), channel_id=1, source_target_pairs={{0,24},{8,0},{16,8},{24,16},{1,25},{9,1},{17,9},{25,17},{2,26},{10... | collective-permute-start | bytes 172040 | tf_op jit(solution)/shard_map/ppermute | solution.py:336
  35.5 0.7 reshape.14.fluid
  36.1 0.7 reshape.15.heat
  38.5 2.8 %macro.3 = (f32[384,128]{1,0:T(8,128)}, f32[5,8,128]{2,1,0:T(8,128)}) custom-call(f32[1]{0:T(128)} %bitcast.1.target, f32[112,128]{1,0:T(8,128)} %copy-done.6, f32[112,128]{1,0:T(8,128)} %copy-done.3, f32[112,128]{1,0:T(8,128)} %copy-done.21, f32[112,128]{1,0:T(8,128)} %copy-done.16, f32[112,128]{1,0:T(8,128)} %copy-done.24, f32[112,128]{1,0:T(8,128)} %copy-done.15, ...), custom_call_target="tpu_custom_call" | custom-call | tf_op jit(solution)/shard_map/macro/pallas_call | solution.py:284
  41.4 1.0 broadcast_in_dim.23.fluid
  42.4 5.3 %stream.3.g = f32[8,8,16,768]{3,2,1,0:T(8,128)} custom-call(f32[8,8,16,768]{3,2,1,0:T(8,128)} %h.3, f32[8,16,768]{2,1,0:T(8,128)} %copy-done.1, f32[8,16,384]{2,1,0:T(8,128)} %copy-done.13, f32[8,16,384]{2,1,0:T(8,128)} %copy-done.14, f32[8,768]{1,0:T(8,128)} %get-tuple-element.26.coef, f32[8,8,16,128]{3,2,1,0:T(8,128)} %broadcast_in_dim.23.fluid), custom_call_target="tpu_custom_call" | custom-call | flops 2000000 | bytes 8000000 | tf_op jit(solution)/shard_map/stream/pallas_call | solution.py:182
  47.7 5.5 %update.3 = (f32[8,8,16,768]{3,2,1,0:T(8,128)}, f32[112,128]{1,0:T(8,128)}, f32[8,16,768]{2,1,0:T(8,128)}, f32[8,16,384]{2,1,0:T(8,128)}, f32[8,16,384]{2,1,0:T(8,128)}) custom-call(f32[8,8,16,768]{3,2,1,0:T(8,128)} %stream.3.g, f32[384,128]{1,0:T(8,128)} %get-tuple-element.28.mix, bf16[144,768]{1,0:T(8,128)(2,1)} %get-tuple-element.29.wmat, ...), custom_call_target="tpu_custom_call" | custom-call | tf_op jit(solution)/shard_map/update/pallas_call | solution.py:327
  53.2 1.4 %collective-permute-done.15 = f32[112,128]{1,0:T(8,128)S(1)} collective-permute-done((f32[112,128]{1,0:T(8,128)}, f32[112,128]{1,0:T(8,128)S(1)}, u32[]{:S(2)}, u32[]{:S(2)}) %collective-permute-start.15) | collective-permute-done | bytes 57376 | tf_op jit(solution)/shard_map/ppermute | solution.py:353
  54.7 0.8 add.40
  55.5 1.3 collective-permute-start.16
  56.8 0.6 collective-permute-start.17
  57.4 1.5 %collective-permute-start.18 = (f32[112,128]{1,0:T(8,128)S(1)}, f32[112,128]{1,0:T(8,128)S(1)}, u32[]{:S(2)}, u32[]{:S(2)}) collective-permute-start(f32[112,128]{1,0:T(8,128)S(1)} %add.40), channel_id=1, source_target_pairs={{0,6},{1,7},{2,4},{3,5},{4,2},{5,3},{6,0},{7,1},{8,14},{9,15},{10,... | collective-permute-start | bytes 172040 | tf_op jit(solution)/shard_map/ppermute | solution.py:353
  59.0 0.7 collective-permute-start.12
  59.7 1.2 collective-permute-start.13
  60.8 2.7 %collective-permute-start.14 = (f32[8,16,384]{2,1,0:T(8,128)}, f32[8,16,384]{2,1,0:T(8,128)S(1)}, u32[]{:S(2)}, u32[]{:S(2)}) collective-permute-start(f32[8,16,384]{2,1,0:T(8,128)} %get-tuple-element.34), channel_id=1, source_target_pairs={{0,24},{8,0},{16,8},{24,16},{1,25},{9,1},{17,9},{25,17},{2,26},{10... | collective-permute-start | bytes 589832 | tf_op jit(solution)/shard_map/ppermute | solution.py:336
  63.9 3.4 %collective-permute-start.20 = (f32[112,128]{1,0:T(8,128)S(1)}, f32[112,128]{1,0:T(8,128)S(1)}, u32[]{:S(2)}, u32[]{:S(2)}) collective-permute-start(f32[112,128]{1,0:T(8,128)S(1)} %add.42.side), channel_id=1, source_target_pairs={{0,8},{8,16},{16,24},{24,0},{1,9},{9,17},{17,25},{25,1},{2,10},{10... | collective-permute-start | bytes 172040 | tf_op jit(solution)/shard_map/ppermute | solution.py:336
  67.3 5.2 %collective-permute-done.23.far = f32[8,128]{1,0:T(8,128)S(1)} collective-permute-done((f32[8,128]{1,0:T(8,128)S(1)}, f32[8,128]{1,0:T(8,128)S(1)}, u32[]{:S(2)}, u32[]{:S(2)}) %collective-permute-start.23) | collective-permute-done | bytes 4128 | tf_op jit(solution)/shard_map/ppermute | solution.py:336
  72.5 0.7 collective-permute-done.20.left_side
  73.2 1.4 collective-permute-start.19
  74.5 2.1 %collective-permute-done.22.right_side = f32[112,128]{1,0:T(8,128)S(1)} collective-permute-done((f32[112,128]{1,0:T(8,128)S(1)}, f32[112,128]{1,0:T(8,128)S(1)}, u32[]{:S(2)}, u32[]{:S(2)}) %collective-permute-start.22) | collective-permute-done | bytes 57376 | tf_op jit(solution)/shard_map/ppermute | solution.py:336
  76.7 1.9 %collective-permute-start.21 = (f32[112,128]{1,0:T(8,128)S(1)}, f32[112,128]{1,0:T(8,128)S(1)}, u32[]{:S(2)}, u32[]{:S(2)}) collective-permute-start(f32[112,128]{1,0:T(8,128)S(1)} %add.41.own), channel_id=1, source_target_pairs={{0,24},{8,0},{16,8},{24,16},{1,25},{9,1},{17,9},{25,17},{2,26},{10... | collective-permute-start | bytes 172040 | tf_op jit(solution)/shard_map/ppermute | solution.py:336
  78.6 0.8 collective-permute-done.19.left
  79.5 1.4 %collective-permute-done.21.right = f32[112,128]{1,0:T(8,128)S(1)} collective-permute-done((f32[112,128]{1,0:T(8,128)S(1)}, f32[112,128]{1,0:T(8,128)S(1)}, u32[]{:S(2)}, u32[]{:S(2)}) %collective-permute-start.21) | collective-permute-done | bytes 57376 | tf_op jit(solution)/shard_map/ppermute | solution.py:336
  80.9 0.6 copy-done.26
  81.5 2.8 %macro.4 = (f32[384,128]{1,0:T(8,128)}, f32[5,8,128]{2,1,0:T(8,128)}) custom-call(f32[1]{0:T(128)} %bitcast.2.target, f32[112,128]{1,0:T(8,128)} %copy-done.5, f32[112,128]{1,0:T(8,128)} %copy-done.8, f32[112,128]{1,0:T(8,128)} %copy-done.23, f32[112,128]{1,0:T(8,128)} %copy-done.18, f32[112,128]{1,0:T(8,128)} %copy-done.26, f32[112,128]{1,0:T(8,128)} %copy-done.20, ...), custom_call_target="tpu_custom_call" | custom-call | tf_op jit(solution)/shard_map/macro/pallas_call | solution.py:284
  84.3 0.6 copy-done.10
  85.2 5.3 %stream.4.g = f32[8,8,16,768]{3,2,1,0:T(8,128)} custom-call(f32[8,8,16,768]{3,2,1,0:T(8,128)} %get-tuple-element.31.h, f32[8,16,768]{2,1,0:T(8,128)} %copy-done.2, f32[8,16,384]{2,1,0:T(8,128)} %copy-done.10, f32[8,16,384]{2,1,0:T(8,128)} %copy-done.12, f32[8,768]{1,0:T(8,128)} %get-tuple-element.26.coef, f32[8,8,16,128]{3,2,1,0:T(8,128)} %broadcast_in_dim.23.fluid), custom_call_target="tpu_custom_call" | custom-call | flops 2000000 | bytes 8000000 | tf_op jit(solution)/shard_map/stream/pallas_call | solution.py:182
  90.5 5.5 %update.4 = (f32[8,8,16,768]{3,2,1,0:T(8,128)}, f32[112,128]{1,0:T(8,128)}, f32[8,16,768]{2,1,0:T(8,128)}, f32[8,16,384]{2,1,0:T(8,128)}, f32[8,16,384]{2,1,0:T(8,128)}) custom-call(f32[8,8,16,768]{3,2,1,0:T(8,128)} %stream.4.g, f32[384,128]{1,0:T(8,128)} %get-tuple-element.36.mix, bf16[144,768]{1,0:T(8,128)(2,1)} %get-tuple-element.29.wmat, ...), custom_call_target="tpu_custom_call" | custom-call | tf_op jit(solution)/shard_map/update/pallas_call | solution.py:327
  96.0 1.4 %collective-permute-done.27 = f32[112,128]{1,0:T(8,128)S(1)} collective-permute-done((f32[112,128]{1,0:T(8,128)}, f32[112,128]{1,0:T(8,128)S(1)}, u32[]{:S(2)}, u32[]{:S(2)}) %collective-permute-start.27) | collective-permute-done | bytes 57376 | tf_op jit(solution)/shard_map/ppermute | solution.py:353
  97.4 0.8 add.44
  98.3 1.4 %collective-permute-start.28 = (f32[112,128]{1,0:T(8,128)S(1)}, f32[112,128]{1,0:T(8,128)S(1)}, u32[]{:S(2)}, u32[]{:S(2)}) collective-permute-start(f32[112,128]{1,0:T(8,128)S(1)} %add.44), channel_id=1, source_target_pairs={{0,2},{1,3},{2,0},{3,1},{4,6},{5,7},{6,4},{7,5},{8,10},{9,11},{10,... | collective-permute-start | bytes 172040 | tf_op jit(solution)/shard_map/ppermute | solution.py:353
  99.7 1.6 %collective-permute-start.29 = (f32[112,128]{1,0:T(8,128)S(1)}, f32[112,128]{1,0:T(8,128)S(1)}, u32[]{:S(2)}, u32[]{:S(2)}) collective-permute-start(f32[112,128]{1,0:T(8,128)S(1)} %add.44), channel_id=1, source_target_pairs={{0,4},{1,5},{2,6},{3,7},{4,0},{5,1},{6,2},{7,3},{8,12},{9,13},{10,... | collective-permute-start | bytes 172040 | tf_op jit(solution)/shard_map/ppermute | solution.py:353
  101.8 1.4 %collective-permute-start.24 = (f32[8,16,768]{2,1,0:T(8,128)}, f32[8,16,768]{2,1,0:T(8,128)S(1)}, u32[]{:S(2)}, u32[]{:S(2)}) collective-permute-start(f32[8,16,768]{2,1,0:T(8,128)} %get-tuple-element.38), channel_id=1, source_target_pairs={{0,4},{4,0},{1,5},{5,1},{2,6},{6,2},{3,7},{7,3},{8,12},{12,8},{9,1... | collective-permute-start | bytes 1179656 | tf_op jit(solution)/shard_map/ppermute | solution.py:336
  103.2 0.6 collective-permute-start.25
  103.8 3.2 %collective-permute-start.26 = (f32[8,16,384]{2,1,0:T(8,128)}, f32[8,16,384]{2,1,0:T(8,128)S(1)}, u32[]{:S(2)}, u32[]{:S(2)}) collective-permute-start(f32[8,16,384]{2,1,0:T(8,128)} %get-tuple-element.40), channel_id=1, source_target_pairs={{0,24},{8,0},{16,8},{24,16},{1,25},{9,1},{17,9},{25,17},{2,26},{10... | collective-permute-start | bytes 589832 | tf_op jit(solution)/shard_map/ppermute | solution.py:336
  107.1 0.5 collective-permute-start.35
  107.6 3.3 %collective-permute-start.32 = (f32[112,128]{1,0:T(8,128)S(1)}, f32[112,128]{1,0:T(8,128)S(1)}, u32[]{:S(2)}, u32[]{:S(2)}) collective-permute-start(f32[112,128]{1,0:T(8,128)S(1)} %add.46.side), channel_id=1, source_target_pairs={{0,8},{8,16},{16,24},{24,0},{1,9},{9,17},{17,25},{25,1},{2,10},{10... | collective-permute-start | bytes 172040 | tf_op jit(solution)/shard_map/ppermute | solution.py:336
  110.9 5.3 %collective-permute-done.35.far = f32[8,128]{1,0:T(8,128)S(1)} collective-permute-done((f32[8,128]{1,0:T(8,128)S(1)}, f32[8,128]{1,0:T(8,128)S(1)}, u32[]{:S(2)}, u32[]{:S(2)}) %collective-permute-start.35) | collective-permute-done | bytes 4128 | tf_op jit(solution)/shard_map/ppermute | solution.py:336
  116.2 0.7 collective-permute-done.32.left_side
  116.9 1.4 collective-permute-start.31
  118.2 2.1 %collective-permute-done.34.right_side = f32[112,128]{1,0:T(8,128)S(1)} collective-permute-done((f32[112,128]{1,0:T(8,128)S(1)}, f32[112,128]{1,0:T(8,128)S(1)}, u32[]{:S(2)}, u32[]{:S(2)}) %collective-permute-start.34) | collective-permute-done | bytes 57376 | tf_op jit(solution)/shard_map/ppermute | solution.py:336
  120.4 1.9 %collective-permute-start.33 = (f32[112,128]{1,0:T(8,128)S(1)}, f32[112,128]{1,0:T(8,128)S(1)}, u32[]{:S(2)}, u32[]{:S(2)}) collective-permute-start(f32[112,128]{1,0:T(8,128)S(1)} %add.45.own), channel_id=1, source_target_pairs={{0,24},{8,0},{16,8},{24,16},{1,25},{9,1},{17,9},{25,17},{2,26},{10... | collective-permute-start | bytes 172040 | tf_op jit(solution)/shard_map/ppermute | solution.py:336
  122.3 0.8 collective-permute-done.31.left
  123.1 1.4 %collective-permute-done.33.right = f32[112,128]{1,0:T(8,128)S(1)} collective-permute-done((f32[112,128]{1,0:T(8,128)S(1)}, f32[112,128]{1,0:T(8,128)S(1)}, u32[]{:S(2)}, u32[]{:S(2)}) %collective-permute-start.33) | collective-permute-done | bytes 57376 | tf_op jit(solution)/shard_map/ppermute | solution.py:336
  124.6 0.6 copy-done.25
  125.2 2.8 %macro.5 = (f32[384,128]{1,0:T(8,128)}, f32[5,8,128]{2,1,0:T(8,128)}) custom-call(f32[1]{0:T(128)} %bitcast.3.target, f32[112,128]{1,0:T(8,128)} %copy-done.4, f32[112,128]{1,0:T(8,128)} %copy-done.7, f32[112,128]{1,0:T(8,128)} %copy-done.22, f32[112,128]{1,0:T(8,128)} %copy-done.17, f32[112,128]{1,0:T(8,128)} %copy-done.25, f32[112,128]{1,0:T(8,128)} %copy-done.19, ...), custom_call_target="tpu_custom_call" | custom-call | tf_op jit(solution)/shard_map/macro/pallas_call | solution.py:284
  128.0 1.5 %reshape.16 = f32[5,8,8,16]{3,2,1,0:T(8,128)} reshape(f32[5,8,128]{2,1,0:T(8,128)} %get-tuple-element.43) | data formatting | bytes 40960 | tf_op jit(solution)/shard_map/reshape | solution.py:382
  129.5 0.6 copy-done.9
  130.4 5.3 %stream.5.g = f32[8,8,16,768]{3,2,1,0:T(8,128)} custom-call(f32[8,8,16,768]{3,2,1,0:T(8,128)} %get-tuple-element.37.h, f32[8,16,768]{2,1,0:T(8,128)} %copy-done, f32[8,16,384]{2,1,0:T(8,128)} %copy-done.9, f32[8,16,384]{2,1,0:T(8,128)} %copy-done.11, f32[8,768]{1,0:T(8,128)} %get-tuple-element.26.coef, f32[8,8,16,128]{3,2,1,0:T(8,128)} %broadcast_in_dim.23.fluid), custom_call_target="tpu_custom_call" | custom-call | flops 2000000 | bytes 8000000 | tf_op jit(solution)/shard_map/stream/pallas_call | solution.py:182
  135.7 4.9 %update.5 = f32[8,8,16,768]{3,2,1,0:T(8,128)} custom-call(f32[8,8,16,768]{3,2,1,0:T(8,128)} %stream.5.g, f32[384,128]{1,0:T(8,128)} %get-tuple-element.42.mix, bf16[144,768]{1,0:T(8,128)(2,1)} %get-tuple-element.29.wmat, bf16[32,768]{1,0:T(8,128)(2,1)} %get-tuple-element.30.proj, f32[8,768]{1,0:T(8,128)} %get-tuple-element.26.coef), custom_call_target="tpu_custom_call" | custom-call | tf_op jit(solution)/shard_map/update/pallas_call | solution.py:327
  (100 shorter events, 2.7 us)
Async XLA Ops:
  0.6 34.8 %copy-start.28 = (s32[8,8,16]{2,1,0:T(8,128)S(1)}, s32[8,8,16]{2,1,0:T(8,128)}, u32[]{:S(2)}) copy-start(s32[8,8,16]{2,1,0:T(8,128)} %param.9) | copy-start | bytes 12292
  0.6 35.5 %copy-start.27 = (f32[8,8,16]{2,1,0:T(8,128)S(1)}, f32[8,8,16]{2,1,0:T(8,128)}, u32[]{:S(2)}) copy-start(f32[8,8,16]{2,1,0:T(8,128)} %param.10) | copy-start | bytes 12292
  8.6 1.6 %collective-permute-start.3 = (f32[112,128]{1,0:T(8,128)}, f32[112,128]{1,0:T(8,128)S(1)}, u32[]{:S(2)}, u32[]{:S(2)}) collective-permute-start(f32[112,128]{1,0:T(8,128)} %get-tuple-element.27), channel_id=1, source_target_pairs={{0,1},{1,0},{2,3},{3,2},{4,5},{5,4},{6,7},{7,6},{8,9},{9,8},{10,11... | collective-permute-start | bytes 172040 | tf_op jit(solution)/shard_map/ppermute | solution.py:353
  11.0 6.3 %collective-permute-start.5 = (f32[112,128]{1,0:T(8,128)S(1)}, f32[112,128]{1,0:T(8,128)S(1)}, u32[]{:S(2)}, u32[]{:S(2)}) collective-permute-start(f32[112,128]{1,0:T(8,128)S(1)} %add.36), channel_id=1, source_target_pairs={{0,4},{1,5},{2,6},{3,7},{4,0},{5,1},{6,2},{7,3},{8,12},{9,13},{10,... | collective-permute-start | bytes 172040 | tf_op jit(solution)/shard_map/ppermute | solution.py:353
  13.9 5.6 %collective-permute-start.6 = (f32[112,128]{1,0:T(8,128)S(1)}, f32[112,128]{1,0:T(8,128)S(1)}, u32[]{:S(2)}, u32[]{:S(2)}) collective-permute-start(f32[112,128]{1,0:T(8,128)S(1)} %add.36), channel_id=1, source_target_pairs={{0,6},{1,7},{2,4},{3,5},{4,2},{5,3},{6,0},{7,1},{8,14},{9,15},{10,... | collective-permute-start | bytes 172040 | tf_op jit(solution)/shard_map/ppermute | solution.py:353
  15.3 7.8 %collective-permute-start.4 = (f32[112,128]{1,0:T(8,128)S(1)}, f32[112,128]{1,0:T(8,128)S(1)}, u32[]{:S(2)}, u32[]{:S(2)}) collective-permute-start(f32[112,128]{1,0:T(8,128)S(1)} %add.36), channel_id=1, source_target_pairs={{0,2},{1,3},{2,0},{3,1},{4,6},{5,7},{6,4},{7,5},{8,10},{9,11},{10,... | collective-permute-start | bytes 172040 | tf_op jit(solution)/shard_map/ppermute | solution.py:353
  15.4 25.9 %collective-permute-start = (f32[8,16,768]{2,1,0:T(8,128)}, f32[8,16,768]{2,1,0:T(8,128)S(1)}, u32[]{:S(2)}, u32[]{:S(2)}) collective-permute-start(f32[8,16,768]{2,1,0:T(8,128)} %get-tuple-element.23), channel_id=1, source_target_pairs={{0,4},{4,0},{1,5},{5,1},{2,6},{6,2},{3,7},{7,3},{8,12},{12,8},{9,1... | collective-permute-start | bytes 1179656 | tf_op jit(solution)/shard_map/ppermute | solution.py:336
  19.5 18.5 %copy-start.3 = (f32[112,128]{1,0:T(8,128)}, f32[112,128]{1,0:T(8,128)S(1)}, u32[]{:S(2)}) copy-start(f32[112,128]{1,0:T(8,128)S(1)} %add.38.side) | copy-start | bytes 172036
  19.5 12.1 %collective-permute-start.10 = (f32[112,128]{1,0:T(8,128)S(1)}, f32[112,128]{1,0:T(8,128)S(1)}, u32[]{:S(2)}, u32[]{:S(2)}) collective-permute-start(f32[112,128]{1,0:T(8,128)S(1)} %add.38.side), channel_id=1, source_target_pairs={{0,24},{8,0},{16,8},{24,16},{1,25},{9,1},{17,9},{25,17},{2,26},{10... | collective-permute-start | bytes 172040 | tf_op jit(solution)/shard_map/ppermute | solution.py:336
  23.1 8.5 %collective-permute-start.8 = (f32[112,128]{1,0:T(8,128)S(1)}, f32[112,128]{1,0:T(8,128)S(1)}, u32[]{:S(2)}, u32[]{:S(2)}) collective-permute-start(f32[112,128]{1,0:T(8,128)S(1)} %add.38.side), channel_id=1, source_target_pairs={{0,8},{8,16},{16,24},{24,0},{1,9},{9,17},{17,25},{25,1},{2,10},{10... | collective-permute-start | bytes 172040 | tf_op jit(solution)/shard_map/ppermute | solution.py:336
  23.1 14.8 %copy-start.6 = (f32[112,128]{1,0:T(8,128)}, f32[112,128]{1,0:T(8,128)S(1)}, u32[]{:S(2)}) copy-start(f32[112,128]{1,0:T(8,128)S(1)} %add.37.own) | copy-start | bytes 172036
  23.2 5.0 %collective-permute-start.11 = (f32[8,128]{1,0:T(8,128)S(1)}, f32[8,128]{1,0:T(8,128)S(1)}, u32[]{:S(2)}, u32[]{:S(2)}) collective-permute-start(f32[8,128]{1,0:T(8,128)S(1)} %slice_add_fusion.2), channel_id=1, source_target_pairs={{0,16},{8,24},{16,0},{24,8},{1,17},{9,25},{17,1},{25,9},{2,18},{10... | collective-permute-start | bytes 12296 | tf_op jit(solution)/shard_map/ppermute | solution.py:336
  24.2 17.1 %collective-permute-start.1 = (f32[8,16,384]{2,1,0:T(8,128)}, f32[8,16,384]{2,1,0:T(8,128)S(1)}, u32[]{:S(2)}, u32[]{:S(2)}) collective-permute-start(f32[8,16,384]{2,1,0:T(8,128)} %get-tuple-element.24), channel_id=1, source_target_pairs={{0,8},{8,16},{16,24},{24,0},{1,9},{9,17},{17,25},{25,1},{2,10},{10... | collective-permute-start | bytes 589832 | tf_op jit(solution)/shard_map/ppermute | solution.py:336
  28.2 9.8 %copy-start.29 = (f32[8,128]{1,0:T(8,128)}, f32[8,128]{1,0:T(8,128)S(1)}, u32[]{:S(2)}) copy-start(f32[8,128]{1,0:T(8,128)S(1)} %collective-permute-done.11.far) | copy-start | bytes 12292
  28.2 13.1 %collective-permute-start.2 = (f32[8,16,384]{2,1,0:T(8,128)}, f32[8,16,384]{2,1,0:T(8,128)S(1)}, u32[]{:S(2)}, u32[]{:S(2)}) collective-permute-start(f32[8,16,384]{2,1,0:T(8,128)} %get-tuple-element.25), channel_id=1, source_target_pairs={{0,24},{8,0},{16,8},{24,16},{1,25},{9,1},{17,9},{25,17},{2,26},{10... | collective-permute-start | bytes 589832 | tf_op jit(solution)/shard_map/ppermute | solution.py:336
  31.6 6.3 %copy-start.15 = (f32[112,128]{1,0:T(8,128)}, f32[112,128]{1,0:T(8,128)S(1)}, u32[]{:S(2)}) copy-start(f32[112,128]{1,0:T(8,128)S(1)} %collective-permute-done.10.right_side) | copy-start | bytes 172036
  31.6 6.1 %collective-permute-start.7 = (f32[112,128]{1,0:T(8,128)S(1)}, f32[112,128]{1,0:T(8,128)S(1)}, u32[]{:S(2)}, u32[]{:S(2)}) collective-permute-start(f32[112,128]{1,0:T(8,128)S(1)} %add.37.own), channel_id=1, source_target_pairs={{0,8},{8,16},{16,24},{24,0},{1,9},{9,17},{17,25},{25,1},{2,10},{10... | collective-permute-start | bytes 172040 | tf_op jit(solution)/shard_map/ppermute | solution.py:336
  31.6 6.3 %copy-start.16 = (f32[112,128]{1,0:T(8,128)}, f32[112,128]{1,0:T(8,128)S(1)}, u32[]{:S(2)}) copy-start(f32[112,128]{1,0:T(8,128)S(1)} %collective-permute-done.8.left_side) | copy-start | bytes 172036
  31.6 6.3 %collective-permute-start.9 = (f32[112,128]{1,0:T(8,128)S(1)}, f32[112,128]{1,0:T(8,128)S(1)}, u32[]{:S(2)}, u32[]{:S(2)}) collective-permute-start(f32[112,128]{1,0:T(8,128)S(1)} %add.37.own), channel_id=1, source_target_pairs={{0,24},{8,0},{16,8},{24,16},{1,25},{9,1},{17,9},{25,17},{2,26},{10... | collective-permute-start | bytes 172040 | tf_op jit(solution)/shard_map/ppermute | solution.py:336
  41.3 1.1 copy-start.13
  41.3 1.1 copy-start.14
  41.4 1.0 copy-start.1
  53.2 1.5 %collective-permute-start.15 = (f32[112,128]{1,0:T(8,128)}, f32[112,128]{1,0:T(8,128)S(1)}, u32[]{:S(2)}, u32[]{:S(2)}) collective-permute-start(f32[112,128]{1,0:T(8,128)} %get-tuple-element.35), channel_id=1, source_target_pairs={{0,1},{1,0},{2,3},{3,2},{4,5},{5,4},{6,7},{7,6},{8,9},{9,8},{10,11... | collective-permute-start | bytes 172040 | tf_op jit(solution)/shard_map/ppermute | solution.py:353
  55.5 5.4 %collective-permute-start.16 = (f32[112,128]{1,0:T(8,128)S(1)}, f32[112,128]{1,0:T(8,128)S(1)}, u32[]{:S(2)}, u32[]{:S(2)}) collective-permute-start(f32[112,128]{1,0:T(8,128)S(1)} %add.40), channel_id=1, source_target_pairs={{0,2},{1,3},{2,0},{3,1},{4,6},{5,7},{6,4},{7,5},{8,10},{9,11},{10,... | collective-permute-start | bytes 172040 | tf_op jit(solution)/shard_map/ppermute | solution.py:353
  56.8 6.7 %collective-permute-start.17 = (f32[112,128]{1,0:T(8,128)S(1)}, f32[112,128]{1,0:T(8,128)S(1)}, u32[]{:S(2)}, u32[]{:S(2)}) collective-permute-start(f32[112,128]{1,0:T(8,128)S(1)} %add.40), channel_id=1, source_target_pairs={{0,4},{1,5},{2,6},{3,7},{4,0},{5,1},{6,2},{7,3},{8,12},{9,13},{10,... | collective-permute-start | bytes 172040 | tf_op jit(solution)/shard_map/ppermute | solution.py:353
  57.4 6.1 %collective-permute-start.18 = (f32[112,128]{1,0:T(8,128)S(1)}, f32[112,128]{1,0:T(8,128)S(1)}, u32[]{:S(2)}, u32[]{:S(2)}) collective-permute-start(f32[112,128]{1,0:T(8,128)S(1)} %add.40), channel_id=1, source_target_pairs={{0,6},{1,7},{2,4},{3,5},{4,2},{5,3},{6,0},{7,1},{8,14},{9,15},{10,... | collective-permute-start | bytes 172040 | tf_op jit(solution)/shard_map/ppermute | solution.py:353
  59.0 25.3 %collective-permute-start.12 = (f32[8,16,768]{2,1,0:T(8,128)}, f32[8,16,768]{2,1,0:T(8,128)S(1)}, u32[]{:S(2)}, u32[]{:S(2)}) collective-permute-start(f32[8,16,768]{2,1,0:T(8,128)} %get-tuple-element.32), channel_id=1, source_target_pairs={{0,4},{4,0},{1,5},{5,1},{2,6},{6,2},{3,7},{7,3},{8,12},{12,8},{9,1... | collective-permute-start | bytes 1179656 | tf_op jit(solution)/shard_map/ppermute | solution.py:336
  59.7 24.6 %collective-permute-start.13 = (f32[8,16,384]{2,1,0:T(8,128)}, f32[8,16,384]{2,1,0:T(8,128)S(1)}, u32[]{:S(2)}, u32[]{:S(2)}) collective-permute-start(f32[8,16,384]{2,1,0:T(8,128)} %get-tuple-element.33), channel_id=1, source_target_pairs={{0,8},{8,16},{16,24},{24,0},{1,9},{9,17},{17,25},{25,1},{2,10},{10... | collective-permute-start | bytes 589832 | tf_op jit(solution)/shard_map/ppermute | solution.py:336
  60.8 23.4 %collective-permute-start.14 = (f32[8,16,384]{2,1,0:T(8,128)}, f32[8,16,384]{2,1,0:T(8,128)S(1)}, u32[]{:S(2)}, u32[]{:S(2)}) collective-permute-start(f32[8,16,384]{2,1,0:T(8,128)} %get-tuple-element.34), channel_id=1, source_target_pairs={{0,24},{8,0},{16,8},{24,16},{1,25},{9,1},{17,9},{25,17},{2,26},{10... | collective-permute-start | bytes 589832 | tf_op jit(solution)/shard_map/ppermute | solution.py:336
  63.5 17.4 %copy-start.5 = (f32[112,128]{1,0:T(8,128)}, f32[112,128]{1,0:T(8,128)S(1)}, u32[]{:S(2)}) copy-start(f32[112,128]{1,0:T(8,128)S(1)} %add.41.own) | copy-start | bytes 172036
  63.6 17.3 %copy-start.8 = (f32[112,128]{1,0:T(8,128)}, f32[112,128]{1,0:T(8,128)S(1)}, u32[]{:S(2)}) copy-start(f32[112,128]{1,0:T(8,128)S(1)} %add.42.side) | copy-start | bytes 172036
  63.6 8.9 %collective-permute-start.23 = (f32[8,128]{1,0:T(8,128)S(1)}, f32[8,128]{1,0:T(8,128)S(1)}, u32[]{:S(2)}, u32[]{:S(2)}) collective-permute-start(f32[8,128]{1,0:T(8,128)S(1)} %slice_add_fusion.1), channel_id=1, source_target_pairs={{0,16},{8,24},{16,0},{24,8},{1,17},{9,25},{17,1},{25,9},{2,18},{10... | collective-permute-start | bytes 12296 | tf_op jit(solution)/shard_map/ppermute | solution.py:336
  63.9 9.2 %collective-permute-start.20 = (f32[112,128]{1,0:T(8,128)S(1)}, f32[112,128]{1,0:T(8,128)S(1)}, u32[]{:S(2)}, u32[]{:S(2)}) collective-permute-start(f32[112,128]{1,0:T(8,128)S(1)} %add.42.side), channel_id=1, source_target_pairs={{0,8},{8,16},{16,24},{24,0},{1,9},{9,17},{17,25},{25,1},{2,10},{10... | collective-permute-start | bytes 172040 | tf_op jit(solution)/shard_map/ppermute | solution.py:336
  72.5 8.4 %copy-start.31 = (f32[8,128]{1,0:T(8,128)}, f32[8,128]{1,0:T(8,128)S(1)}, u32[]{:S(2)}) copy-start(f32[8,128]{1,0:T(8,128)S(1)} %collective-permute-done.23.far) | copy-start | bytes 12292
  72.5 4.2 %collective-permute-start.22 = (f32[112,128]{1,0:T(8,128)S(1)}, f32[112,128]{1,0:T(8,128)S(1)}, u32[]{:S(2)}, u32[]{:S(2)}) collective-permute-start(f32[112,128]{1,0:T(8,128)S(1)} %add.42.side), channel_id=1, source_target_pairs={{0,24},{8,0},{16,8},{24,16},{1,25},{9,1},{17,9},{25,17},{2,26},{10... | collective-permute-start | bytes 172040 | tf_op jit(solution)/shard_map/ppermute | solution.py:336
  73.2 7.7 %copy-start.18 = (f32[112,128]{1,0:T(8,128)}, f32[112,128]{1,0:T(8,128)S(1)}, u32[]{:S(2)}) copy-start(f32[112,128]{1,0:T(8,128)S(1)} %collective-permute-done.20.left_side) | copy-start | bytes 172036
  73.2 6.3 %collective-permute-start.19 = (f32[112,128]{1,0:T(8,128)S(1)}, f32[112,128]{1,0:T(8,128)S(1)}, u32[]{:S(2)}, u32[]{:S(2)}) collective-permute-start(f32[112,128]{1,0:T(8,128)S(1)} %add.41.own), channel_id=1, source_target_pairs={{0,8},{8,16},{16,24},{24,0},{1,9},{9,17},{17,25},{25,1},{2,10},{10... | collective-permute-start | bytes 172040 | tf_op jit(solution)/shard_map/ppermute | solution.py:336
  76.7 4.2 %copy-start.20 = (f32[112,128]{1,0:T(8,128)}, f32[112,128]{1,0:T(8,128)S(1)}, u32[]{:S(2)}) copy-start(f32[112,128]{1,0:T(8,128)S(1)} %collective-permute-done.22.right_side) | copy-start | bytes 172036
  76.7 4.2 %collective-permute-start.21 = (f32[112,128]{1,0:T(8,128)S(1)}, f32[112,128]{1,0:T(8,128)S(1)}, u32[]{:S(2)}, u32[]{:S(2)}) collective-permute-start(f32[112,128]{1,0:T(8,128)S(1)} %add.41.own), channel_id=1, source_target_pairs={{0,24},{8,0},{16,8},{24,16},{1,25},{9,1},{17,9},{25,17},{2,26},{10... | collective-permute-start | bytes 172040 | tf_op jit(solution)/shard_map/ppermute | solution.py:336
  79.4 1.5 %copy-start.23 = (f32[112,128]{1,0:T(8,128)}, f32[112,128]{1,0:T(8,128)S(1)}, u32[]{:S(2)}) copy-start(f32[112,128]{1,0:T(8,128)S(1)} %collective-permute-done.19.left) | copy-start | bytes 172036
  84.3 0.7 copy-start.10
  84.3 0.7 copy-start.12
  84.3 0.9 copy-start.2
  96.0 1.5 %collective-permute-start.27 = (f32[112,128]{1,0:T(8,128)}, f32[112,128]{1,0:T(8,128)S(1)}, u32[]{:S(2)}, u32[]{:S(2)}) collective-permute-start(f32[112,128]{1,0:T(8,128)} %get-tuple-element.41), channel_id=1, source_target_pairs={{0,1},{1,0},{2,3},{3,2},{4,5},{5,4},{6,7},{7,6},{8,9},{9,8},{10,11... | collective-permute-start | bytes 172040 | tf_op jit(solution)/shard_map/ppermute | solution.py:353
  98.3 5.5 %collective-permute-start.28 = (f32[112,128]{1,0:T(8,128)S(1)}, f32[112,128]{1,0:T(8,128)S(1)}, u32[]{:S(2)}, u32[]{:S(2)}) collective-permute-start(f32[112,128]{1,0:T(8,128)S(1)} %add.44), channel_id=1, source_target_pairs={{0,2},{1,3},{2,0},{3,1},{4,6},{5,7},{6,4},{7,5},{8,10},{9,11},{10,... | collective-permute-start | bytes 172040 | tf_op jit(solution)/shard_map/ppermute | solution.py:353
  99.7 7.3 %collective-permute-start.29 = (f32[112,128]{1,0:T(8,128)S(1)}, f32[112,128]{1,0:T(8,128)S(1)}, u32[]{:S(2)}, u32[]{:S(2)}) collective-permute-start(f32[112,128]{1,0:T(8,128)S(1)} %add.44), channel_id=1, source_target_pairs={{0,4},{1,5},{2,6},{3,7},{4,0},{5,1},{6,2},{7,3},{8,12},{9,13},{10,... | collective-permute-start | bytes 172040 | tf_op jit(solution)/shard_map/ppermute | solution.py:353
  101.3 5.7 %collective-permute-start.30 = (f32[112,128]{1,0:T(8,128)S(1)}, f32[112,128]{1,0:T(8,128)S(1)}, u32[]{:S(2)}, u32[]{:S(2)}) collective-permute-start(f32[112,128]{1,0:T(8,128)S(1)} %add.44), channel_id=1, source_target_pairs={{0,6},{1,7},{2,4},{3,5},{4,2},{5,3},{6,0},{7,1},{8,14},{9,15},{10,... | collective-permute-start | bytes 172040 | tf_op jit(solution)/shard_map/ppermute | solution.py:353
  101.8 27.8 %collective-permute-start.24 = (f32[8,16,768]{2,1,0:T(8,128)}, f32[8,16,768]{2,1,0:T(8,128)S(1)}, u32[]{:S(2)}, u32[]{:S(2)}) collective-permute-start(f32[8,16,768]{2,1,0:T(8,128)} %get-tuple-element.38), channel_id=1, source_target_pairs={{0,4},{4,0},{1,5},{5,1},{2,6},{6,2},{3,7},{7,3},{8,12},{12,8},{9,1... | collective-permute-start | bytes 1179656 | tf_op jit(solution)/shard_map/ppermute | solution.py:336
  103.2 26.3 %collective-permute-start.25 = (f32[8,16,384]{2,1,0:T(8,128)}, f32[8,16,384]{2,1,0:T(8,128)S(1)}, u32[]{:S(2)}, u32[]{:S(2)}) collective-permute-start(f32[8,16,384]{2,1,0:T(8,128)} %get-tuple-element.39), channel_id=1, source_target_pairs={{0,8},{8,16},{16,24},{24,0},{1,9},{9,17},{17,25},{25,1},{2,10},{10... | collective-permute-start | bytes 589832 | tf_op jit(solution)/shard_map/ppermute | solution.py:336
  103.8 25.7 %collective-permute-start.26 = (f32[8,16,384]{2,1,0:T(8,128)}, f32[8,16,384]{2,1,0:T(8,128)S(1)}, u32[]{:S(2)}, u32[]{:S(2)}) collective-permute-start(f32[8,16,384]{2,1,0:T(8,128)} %get-tuple-element.40), channel_id=1, source_target_pairs={{0,24},{8,0},{16,8},{24,16},{1,25},{9,1},{17,9},{25,17},{2,26},{10... | collective-permute-start | bytes 589832 | tf_op jit(solution)/shard_map/ppermute | solution.py:336
  107.0 17.5 %copy-start.4 = (f32[112,128]{1,0:T(8,128)}, f32[112,128]{1,0:T(8,128)S(1)}, u32[]{:S(2)}) copy-start(f32[112,128]{1,0:T(8,128)S(1)} %add.45.own) | copy-start | bytes 172036
  107.0 17.5 %copy-start.7 = (f32[112,128]{1,0:T(8,128)}, f32[112,128]{1,0:T(8,128)S(1)}, u32[]{:S(2)}) copy-start(f32[112,128]{1,0:T(8,128)S(1)} %add.46.side) | copy-start | bytes 172036
  107.1 9.1 %collective-permute-start.35 = (f32[8,128]{1,0:T(8,128)S(1)}, f32[8,128]{1,0:T(8,128)S(1)}, u32[]{:S(2)}, u32[]{:S(2)}) collective-permute-start(f32[8,128]{1,0:T(8,128)S(1)} %slice_add_fusion), channel_id=1, source_target_pairs={{0,16},{8,24},{16,0},{24,8},{1,17},{9,25},{17,1},{25,9},{2,18},{10... | collective-permute-start | bytes 12296 | tf_op jit(solution)/shard_map/ppermute | solution.py:336
  107.6 9.2 %collective-permute-start.32 = (f32[112,128]{1,0:T(8,128)S(1)}, f32[112,128]{1,0:T(8,128)S(1)}, u32[]{:S(2)}, u32[]{:S(2)}) collective-permute-start(f32[112,128]{1,0:T(8,128)S(1)} %add.46.side), channel_id=1, source_target_pairs={{0,8},{8,16},{16,24},{24,0},{1,9},{9,17},{17,25},{25,1},{2,10},{10... | collective-permute-start | bytes 172040 | tf_op jit(solution)/shard_map/ppermute | solution.py:336
  116.2 8.4 %copy-start.30 = (f32[8,128]{1,0:T(8,128)}, f32[8,128]{1,0:T(8,128)S(1)}, u32[]{:S(2)}) copy-start(f32[8,128]{1,0:T(8,128)S(1)} %collective-permute-done.35.far) | copy-start | bytes 12292
  116.2 4.2 %collective-permute-start.34 = (f32[112,128]{1,0:T(8,128)S(1)}, f32[112,128]{1,0:T(8,128)S(1)}, u32[]{:S(2)}, u32[]{:S(2)}) collective-permute-start(f32[112,128]{1,0:T(8,128)S(1)} %add.46.side), channel_id=1, source_target_pairs={{0,24},{8,0},{16,8},{24,16},{1,25},{9,1},{17,9},{25,17},{2,26},{10... | collective-permute-start | bytes 172040 | tf_op jit(solution)/shard_map/ppermute | solution.py:336
  116.8 7.7 %copy-start.17 = (f32[112,128]{1,0:T(8,128)}, f32[112,128]{1,0:T(8,128)S(1)}, u32[]{:S(2)}) copy-start(f32[112,128]{1,0:T(8,128)S(1)} %collective-permute-done.32.left_side) | copy-start | bytes 172036
  116.9 6.3 %collective-permute-start.31 = (f32[112,128]{1,0:T(8,128)S(1)}, f32[112,128]{1,0:T(8,128)S(1)}, u32[]{:S(2)}, u32[]{:S(2)}) collective-permute-start(f32[112,128]{1,0:T(8,128)S(1)} %add.45.own), channel_id=1, source_target_pairs={{0,8},{8,16},{16,24},{24,0},{1,9},{9,17},{17,25},{25,1},{2,10},{10... | collective-permute-start | bytes 172040 | tf_op jit(solution)/shard_map/ppermute | solution.py:336
  120.4 4.2 %copy-start.19 = (f32[112,128]{1,0:T(8,128)}, f32[112,128]{1,0:T(8,128)S(1)}, u32[]{:S(2)}) copy-start(f32[112,128]{1,0:T(8,128)S(1)} %collective-permute-done.34.right_side) | copy-start | bytes 172036
  120.4 4.2 %collective-permute-start.33 = (f32[112,128]{1,0:T(8,128)S(1)}, f32[112,128]{1,0:T(8,128)S(1)}, u32[]{:S(2)}, u32[]{:S(2)}) collective-permute-start(f32[112,128]{1,0:T(8,128)S(1)} %add.45.own), channel_id=1, source_target_pairs={{0,24},{8,0},{16,8},{24,16},{1,25},{9,1},{17,9},{25,17},{2,26},{10... | collective-permute-start | bytes 172040 | tf_op jit(solution)/shard_map/ppermute | solution.py:336
  123.1 1.5 %copy-start.22 = (f32[112,128]{1,0:T(8,128)}, f32[112,128]{1,0:T(8,128)S(1)}, u32[]{:S(2)}) copy-start(f32[112,128]{1,0:T(8,128)S(1)} %collective-permute-done.31.left) | copy-start | bytes 172036
  129.5 0.7 copy-start.9
  129.5 0.8 copy-start.11
  129.5 0.8 copy-start
  (4 other events, 2.5 us)

commit v2 on v1

--- a/solution.py
+++ b/solution.py
@@ -6,6 +6,7 @@
 from jax.experimental import pallas as pl
 from jax.experimental.pallas import tpu as pltpu
 from jax.sharding import PartitionSpec as P
+
 
 ITERS = 3
 MACRO_STEPS = 4
@@ -142,59 +143,90 @@
         ],
         scratch_shapes=[pltpu.VMEM((KROWS, nv), f32)],
         name="prepare",
+        compiler_params=pltpu.CompilerParams(vmem_limit_bytes=8 << 20),
     )(velocity, weights[None], initial)
 
 
-def stream_kernel(h, yhalo, xbefore, xafter, coef, fluid, g):
+def y_direction(lanes, nv):
+    quarters = {(lanes.start * 4) // nv, ((lanes.stop - 1) * 4) // nv}
+    return {q % 2 == 0 for q in quarters}
+
+
+def stream_kernel(h, coef, fluid, g):
     nx, ny, nz, nv = h.shape
     tiles = nv // LANES
     for j in range(tiles):
         lanes = slice(j * LANES, (j + 1) * LANES)
         forward_x = j < tiles // 2
-        half = slice(lanes.start % (nv // 2), lanes.start % (nv // 2) + LANES)
         row = lambda k: jnp.broadcast_to(coef[k : k + 1, lanes], (nz, LANES))
         centre, along_x, along_y, along_z = (row(k) for k in range(4))
         up_z = row(5) > 0.0
-        quarters = {(lanes.start * 4) // nv, ((lanes.stop - 1) * 4) // nv}
-        signs = {q % 2 == 0 for q in quarters}
         up_y = row(4) > 0.0
+        signs = y_direction(lanes, nv)
+        zero = jnp.zeros((nz, LANES), f32)
         for x in range(nx):
             for y in range(ny):
                 c = h[x, y, :, lanes]
-                if forward_x:
-                    ux = h[x - 1, y, :, lanes] if x > 0 else xbefore[y, :, half]
-                else:
-                    ux = h[x + 1, y, :, lanes] if x < nx - 1 else xafter[y, :, half]
-                before = h[x, y - 1, :, lanes] if y > 0 else yhalo[x, :, lanes]
-                after = h[x, y + 1, :, lanes] if y < ny - 1 else yhalo[x, :, lanes]
+                beside = x - 1 if forward_x else x + 1
+                ux = h[beside, y, :, lanes] if 0 <= beside < nx else None
+                before = h[x, y - 1, :, lanes] if y > 0 else None
+                after = h[x, y + 1, :, lanes] if y < ny - 1 else None
                 if signs == {True}:
                     uy = before
                 elif signs == {False}:
                     uy = after
                 else:
-                    uy = jnp.where(up_y, before, after)
+                    uy = jnp.where(up_y, zero if before is None else before, zero if after is None else after)
                 uz = jnp.where(up_z, pltpu.roll(c, 1, 0), pltpu.roll(c, nz - 1, 0))
-                out = (centre * c + along_x * ux) + (along_y * uy + along_z * uz)
+                out = centre * c + along_z * uz
+                if ux is not None:
+                    out = out + along_x * ux
+                if uy is not None:
+                    out = out + along_y * uy
                 g[x, y, :, lanes] = out * fluid[x, y]
 
 
-def stream(h, yhalo, xbefore, xafter, coef, fluid):
+def stream(h, coef, fluid):
     return pl.pallas_call(
         stream_kernel,
         out_shape=jax.ShapeDtypeStruct(h.shape, f32),
         name="stream",
-        cost_estimate=pl.CostEstimate(flops=2_000_000, bytes_accessed=8_000_000, transcendentals=0),
-    )(h, yhalo, xbefore, xafter, coef, fluid)
-
-
-def macro_kernel(target, own, side, left, left_side, right, right_side, far, fluid, heat, mix, state_out, *, cells, nz, last):
+        compiler_params=pltpu.CompilerParams(vmem_limit_bytes=12 << 20),
+    )(h, coef, fluid)
+
+
+def join_kernel(mom, across, beside, corner, both, mass):
+    rows = mom.shape[0]
+    nx = mass.shape[0]
+    own = mom[...] + across[...]
+    side = beside[...] + corner[...]
+    both[0:rows, :] = own
+    both[rows:, :] = side
+    mass[...] = own[0:nx] + side[0:nx]
+
+
+def join(mom, across, beside, corner, nx):
+    rows, width = mom.shape
+    return pl.pallas_call(
+        join_kernel,
+        out_shape=[
+            jax.ShapeDtypeStruct((2 * rows, width), f32),
+            jax.ShapeDtypeStruct((nx, width), f32),
+        ],
+        name="join",
+        compiler_params=pltpu.CompilerParams(vmem_limit_bytes=4 << 20),
+    )(mom, across, beside, corner)
+
+
+def macro_kernel(mid, left, right, fluid, heat, mix, state_out, mass_out, *, nz):
     nx, width = fluid.shape
 
     def field(k):
-        part = slice(k * nx, (k + 1) * nx)
-        here = jnp.concatenate([left[part], own[part], right[part]], axis=0)
-        there = jnp.concatenate([left_side[part], side[part], right_side[part]], axis=0)
-        return jnp.concatenate([here, there], axis=1)
+        halves = []
+        for start in (k * nx, (MOMENTS + k) * nx):
+            part = slice(start, start + nx)
+            halves.append(jnp.concatenate([left[part], mid[part], right[part]], axis=0))
+        return jnp.concatenate(halves, axis=1)
 
     rows, lanes = 3 * nx, 2 * width
     depth = lax.broadcasted_iota(jnp.int32, (rows, lanes), 1) % nz
@@ -249,11 +281,11 @@
         rates.append(-(2.0 / 3.0) * div + 2.0 / 3.0 * CONDUCTION * laplace(state[4], near[4]) + sources[3])
         state = [s + MACRO_TIME * r for s, r in zip(state, rates)]
 
-    mass = far[...]
-    for part in (own, side, left, left_side, right, right_side):
-        mass = mass + part[0:nx]
-    mass = jnp.sum(jnp.sum(mass, axis=0, keepdims=True), axis=1, keepdims=True)
-    shift_all = jnp.broadcast_to(target[0] - mass / cells, (nx, width))
+    mass = None
+    for part in (mid, left, right):
+        for start in (0, MOMENTS * nx):
+            mass = part[start : start + nx] if mass is None else mass + part[start : start + nx]
+    mass_out[...] = mass
     is_fluid = fluid[...]
 
     def centre(v):
@@ -269,66 +301,107 @@
             emit(5 + 10 * d + k, centre(shift(change[k], d, -1)) * is_fluid)
             emit(10 + 10 * d + k, centre(shift(change[k], d, 1)) * is_fluid)
         emit(35 + k, centre(state[k]) * is_fluid)
-    emit(40, shift_all * is_fluid)
+    emit(40, is_fluid)
     emit(41, heat[...] * (1.0 - is_fluid))
     for k in range(42, KROWS):
         emit(k, jnp.zeros((nx, width), f32))
     for k in range(5):
-        value = centre(state[k])
-        state_out[k] = value + shift_all if k == 0 else value
-
-
-def macro(target, own, side, left, left_side, right, right_side, far, fluid, heat, cells, nz):
+        state_out[k] = centre(state[k])
+
+
+def macro(mid, left, right, fluid, heat, nz):
     nx, width = fluid.shape
-    vmem = pl.BlockSpec(memory_space=pltpu.VMEM)
     return pl.pallas_call(
-        functools.partial(macro_kernel, cells=cells, nz=nz, last=False),
-        in_specs=[pl.BlockSpec(memory_space=pltpu.SMEM)] + [vmem] * 9,
+        functools.partial(macro_kernel, nz=nz),
         out_shape=[
             jax.ShapeDtypeStruct((KROWS * nx, width), f32),
             jax.ShapeDtypeStruct((5, nx, width), f32),
+            jax.ShapeDtypeStruct((nx, width), f32),
         ],
         name="macro",
-    )(target, own, side, left, left_side, right, right_side, far, fluid, heat)
-
-
-def update_kernel(g, mix, wmat, proj, coef, *outs, last):
+        compiler_params=pltpu.CompilerParams(vmem_limit_bytes=8 << 20),
+    )(mid, left, right, fluid, heat)
+
+
+def update_kernel(target, g, mix, wmat, proj, coef, fluid, yhalo, xbefore, xafter, mass, far, *refs, last, cells):
     nx, ny, nz, nv = g.shape
-    h = outs[0]
     half = nv // 2
+    if last:
+        state, h, fields = refs
+    else:
+        h, mom, ysend, xup, xdown = refs
+    total = mass[...] + far[...]
+    total = jnp.sum(jnp.sum(total, axis=0, keepdims=True), axis=1, keepdims=True)
+    offset = target[0] - total / cells
+    is_offset = lax.broadcasted_iota(jnp.int32, (KROWS, ny * nz), 0) == 40
+    scale = jnp.where(is_offset, jnp.broadcast_to(offset, (KROWS, ny * nz)), 1.0)
+    if last:
+        for k in range(5):
+            value = state[k] + jnp.broadcast_to(offset, (nx, ny * nz)) if k == 0 else state[k]
+            for y in range(ny):
+                fields[pl.ds(k * nx * ny + y, nx, stride=ny), :] = value[:, y * nz : (y + 1) * nz]
+    along_x, along_y = coef[1:2, :], coef[2:3, :]
+    upward = coef[4:5, :] > 0.0
+    first_y = jnp.where(upward, along_y, 0.0)
+    final_y = jnp.where(upward, 0.0, along_y)
     for x in range(nx):
-        columns = mix[x * KROWS : (x + 1) * KROWS, :].T
+        columns = (mix[x * KROWS : (x + 1) * KROWS, :] * scale).T
         high, low = split(columns)
         lhs = jnp.concatenate([high, low, high], axis=1)
         add = dot(lhs, wmat[...], ((1,), (0,)))
-        plane = g[x].reshape(ny * nz, nv) + add
+        pieces = []
+        for y in range(ny):
+            piece = g[x, y] + add[y * nz : (y + 1) * nz]
+            outer = None
+            if y == 0:
+                outer = first_y * yhalo[x]
+            if y == ny - 1:
+                outer = final_y * yhalo[x]
+            if x == 0:
+                edge = jnp.concatenate([along_x[:, :half] * xbefore[y], jnp.zeros((nz, half), f32)], axis=1)
+                outer = edge if outer is None else outer + edge
+            if x == nx - 1:
+                edge = jnp.concatenate([jnp.zeros((nz, half), f32), along_x[:, half:] * xafter[y]], axis=1)
+                outer = edge if outer is None else outer + edge
+            if outer is not None:
+                piece = piece + outer * jnp.concatenate([fluid[x, y]] * (nv // LANES), axis=1)
+            pieces.append(piece)
+        plane = jnp.concatenate(pieces, axis=0)
         h[x] = plane.reshape(ny, nz, nv)
         if not last:
-            mom, ysend, xup, xdown = outs[1:]
             out = local_moments(proj[...], plane)
             mom[pl.ds(x, MOMENTS, stride=nx), :] = out[:MOMENTS]
-            ysend[x] = jnp.where(coef[4:5, :] > 0.0, plane[(ny - 1) * nz :], plane[:nz])
+            ysend[x] = jnp.where(upward, plane[(ny - 1) * nz :], plane[:nz])
             if x == nx - 1:
                 xup[...] = h[x, :, :, :half]
             if x == 0:
                 xdown[...] = h[x, :, :, half:]
 
 
-def update(g, mix, wmat, proj, coef, last):
+def update(target, g, mix, wmat, proj, coef, fluid, halos, mass, far, state, cells):
     nx, ny, nz, nv = g.shape
+    last = state is not None
     shapes = [jax.ShapeDtypeStruct(g.shape, f32)]
-    if not last:
+    if last:
+        shapes.append(jax.ShapeDtypeStruct((5 * nx * ny, nz), f32))
+    else:
         shapes += [
             jax.ShapeDtypeStruct((MOMENTS * nx, ny * nz), f32),
             jax.ShapeDtypeStruct((nx, nz, nv), f32),
             jax.ShapeDtypeStruct((ny, nz, nv // 2), f32),
             jax.ShapeDtypeStruct((ny, nz, nv // 2), f32),
         ]
+    operands = [target, g, mix, wmat, proj, coef, fluid, *halos, mass, far]
+    if last:
+        operands.append(state)
+    vmem = pl.BlockSpec(memory_space=pltpu.VMEM)
     return pl.pallas_call(
-        functools.partial(update_kernel, last=last),
+        functools.partial(update_kernel, last=last, cells=cells),
+        in_specs=[pl.BlockSpec(memory_space=pltpu.SMEM)] + [vmem] * (len(operands) - 1),
         out_shape=shapes,
         name="update",
-    )(g, mix, wmat, proj, coef)
+        compiler_params=pltpu.CompilerParams(vmem_limit_bytes=14 << 20),
+    )(*operands)
 
 
 def ring(value, axis, step):
@@ -365,21 +438,29 @@
         while bit < top:
             mom = mom + plane_pair(mom, 0, bit)
             bit *= 2
-        own = mom + plane_pair(mom, 0, top)
-        side = plane_pair(mom, 1, 0) + plane_pair(mom, 1, top)
-        left, left_side = ring(own, "tx", 1), ring(side, "tx", 1)
-        right, right_side = ring(own, "tx", -1), ring(side, "tx", -1)
-        sums = own[0:nx] + side[0:nx]
-        far = sum([ring(sums, "tx", d) for d in range(2, n_tx - 1)], jnp.zeros_like(sums))
+        across = plane_pair(mom, 0, top)
+        beside = plane_pair(mom, 1, 0)
+        corner = plane_pair(mom, 1, top)
         yhalo = ring(ysend, "ty", 1)
-        xbefore, xafter = ring(xup, "tx", 1), ring(xdown, "tx", -1)
-        g = stream(h, yhalo, xbefore, xafter, coef, fluid_cells)
-        mix, state = macro(target, own, side, left, left_side, right, right_side, far, fluid_rows, heat, cells, nz)
-        outs = update(g, mix, wmat, proj, coef, last)
+        xbefore = ring(xup, "tx", 1)
+        xafter = ring(xdown, "tx", -1)
+        both, sums = join(mom, across, beside, corner, nx)
+        left = ring(both, "tx", 1)
+        right = ring(both, "tx", -1)
+        far = None
+        for d in range(2, n_tx - 1):
+            part = ring(sums, "tx", d)
+            far = part if far is None else far + part
+        if far is None:
+            far = jnp.zeros_like(sums)
+        g = stream(h, coef, fluid_cells)
+        mix, state, mass = macro(both, left, right, fluid_rows, heat, nz)
+        halos = (yhalo, xbefore, xafter)
+        outs = update(target, g, mix, wmat, proj, coef, fluid_cells, halos, mass, far, state if last else None, cells)
         h = outs[0]
         if not last:
             mom, ysend, xup, xdown = outs[1:]
-    return h, state.reshape(5, nx, ny, nz)
+    return h, outs[1].reshape(5, nx, ny, nz)
 
 
 def solution(mesh):

time: 141 us -> 94.1 us (0.67)
  Pallas kernels: 46.8 us -> 21.8 us
  starting transfers between devices: 53.1 us -> 40.9 us
  waiting for transfers between devices: 27.7 us -> 21.1 us
  other arithmetic: 2.55 us -> 0.63 us
    ppermute x24 -> x18, waiting for transfers between devices: 21.6 us -> 9.19 us  [ring(): lax.ppermute(value, axis, [(i, (i + step) % count) for i in range(count)])]
    ppermute x24 -> x18, starting transfers between devices: 41.2 us -> 28.8 us  [ring(): lax.ppermute(value, axis, [(i, (i + step) % count) for i in range(count)])]
    pallas_call x3, Pallas kernels: 15.9 us -> 3.99 us  [stream(): pl.pallas_call(stream_kernel, out_shape=jax.ShapeDtypeStruct(h.shape, f32...]
    pallas_call x6 -> x9, Pallas kernels: 24.3 us -> 13.9 us  [the longest x3 7.88 us: update(): pl.pallas_call(functools.partial(update_kernel, last=last, cells=cells),...]
    ppermute x12, waiting for transfers between devices: 6.1 us -> 11.9 us  [plane_pair(): return lax.ppermute(value, ('ty', 'vel'), pairs)]
    pallas_call x1, Pallas kernels: 6.63 us -> 3.9 us  [prepare(): pl.pallas_call(functools.partial(prepare_kernel, total=total), grid=(nx,)...]
    add x3, other arithmetic: 2.48 us -> 0.02 us  [on_device(): mom = mom + plane_pair(mom, 0, bit)]
    reshape x1 -> x0, local copies, waits for them, and re-layouts: 1.5 us -> none  [on_device(): return (h, state.reshape(5, nx, ny, nz))]
  transfers between devices with their start and end apart: 36 -> 30, of which waited for: 17 -> 11; matrix products, arithmetic and copies ran while one was open for 2% -> 5% of each run, Pallas kernels for 6% -> 11%
where the time goes in v2:
time: 94.1 us; the launch traced here: 93.6 us
  starting transfers between devices  40.9 us (43%)
  Pallas kernels  21.8 us (23%)
  waiting for transfers between devices  21.1 us (22%)
  local copies, waits for them, and re-layouts  7.75 us (8%)
  between operations  1.44 us (2%)
    ppermute x18, starting transfers between devices, ring(): lax.ppermute(value, axis, [(i, (i + step) % count) for i in range(count)])  28.8 us
    ppermute x12, starting transfers between devices, plane_pair(): return lax.ppermute(value, ('ty', 'vel'), pairs)  12.1 us
    ppermute x12, waiting for transfers between devices, plane_pair(): return lax.ppermute(value, ('ty', 'vel'), pairs)  11.9 us
    ppermute x18, waiting for transfers between devices, ring(): lax.ppermute(value, axis, [(i, (i + step) % count) for i in range(count)])  9.19 us
    pallas_call x3, Pallas kernels, update(): pl.pallas_call(functools.partial(update_kernel, last=last, cells=cells),...  7.88 us
    pallas_call x3, Pallas kernels, macro(): pl.pallas_call(functools.partial(macro_kernel, nz=nz), out_shape=[jax.Sha...  5.35 us
    pallas_call x3, Pallas kernels, stream(): pl.pallas_call(stream_kernel, out_shape=jax.ShapeDtypeStruct(h.shape, f32...  3.99 us
    pallas_call x1, Pallas kernels, prepare(): pl.pallas_call(functools.partial(prepare_kernel, total=total), grid=(nx,)...  3.9 us
  transfers between devices with their start and end apart: 30, of which 11 were waited for; matrix products, arithmetic and copies ran while one was open for 5% of the time, Pallas kernels for 11%

profile of v2, /device:TPU:0, one launch (start us, length us, event | category | flops | bytes accessed | tf_op | source)
XLA Modules:
  0.0 93.6 jit_solution(16728465281429792141)
XLA Ops:
  0.6 0.7 broadcast_in_dim.21.wgt
  1.3 1.9 %copy-done = f32[8,8,16,768]{3,2,1,0:T(8,128)S(1)} copy-done((f32[8,8,16,768]{3,2,1,0:T(8,128)S(1)}, f32[8,8,16,768]{3,2,1,0:T(8,128)}, u32[]{:S(2)}) %copy-start) | copy-done | bytes 3145752
  3.2 0.7 copy-done.6
  3.9 3.9 %prepare.1 = (f32[112,128]{1,0:T(8,128)S(1)}, bf16[32,768]{1,0:T(8,128)(2,1)S(1)}, bf16[144,768]{1,0:T(8,128)(2,1)S(1)}, f32[8,768]{1,0:T(8,128)S(1)}, f32[8,16,...) custom-call(f32[3,768]{1,0:T(4,128)S(1)} %copy-done.6, f32[1,768]{1,0:T(1,128)S(1)} %broadcast_in_dim.21.wgt, ...), custom_call_target="tpu_custom_call" | custom-call | tf_op jit(solution)/shard_map/prepare/pallas_call | solution.py:122
  7.8 0.5 collective-permute-start
  8.3 0.9 collective-permute-done
  9.2 3.8 %collective-permute-start.3 = (f32[112,128]{1,0:T(8,128)S(1)}, f32[112,128]{1,0:T(8,128)S(1)}, u32[]{:S(2)}, u32[]{:S(2)}) collective-permute-start(f32[112,128]{1,0:T(8,128)S(1)} %add.9.mom), channel_id=1, source_target_pairs={{0,6},{1,7},{2,4},{3,5},{4,2},{5,3},{6,0},{7,1},{8,14},{9,15},{10,... | collective-permute-start | bytes 172040 | tf_op jit(solution)/shard_map/ppermute | solution.py:426
  13.1 0.5 collective-permute-start.2
  13.6 0.1 collective-permute-start.1
  13.7 1.9 %collective-permute-start.6 = (f32[8,16,768]{2,1,0:T(8,128)}, f32[8,16,768]{2,1,0:T(8,128)}, u32[]{:S(2)}, u32[]{:S(2)}) collective-permute-start(f32[8,16,768]{2,1,0:T(8,128)} %get-tuple-element.40), channel_id=1, source_target_pairs={{0,4},{4,0},{1,5},{5,1},{2,6},{6,2},{3,7},{7,3},{8,12},{12,8},{9,1... | collective-permute-start | bytes 1179656 | tf_op jit(solution)/shard_map/ppermute | solution.py:409
  15.6 0.0 collective-permute-done.3.corner
  15.6 2.2 %collective-permute-done.2.beside = f32[112,128]{1,0:T(8,128)S(1)} collective-permute-done((f32[112,128]{1,0:T(8,128)S(1)}, f32[112,128]{1,0:T(8,128)S(1)}, u32[]{:S(2)}, u32[]{:S(2)}) %collective-permute-start.2) | collective-permute-done | bytes 57376 | tf_op jit(solution)/shard_map/ppermute | solution.py:426
  17.9 0.6 join.3
  18.5 3.6 %collective-permute-start.5 = (f32[224,128]{1,0:T(8,128)S(1)}, f32[224,128]{1,0:T(8,128)S(1)}, u32[]{:S(2)}, u32[]{:S(2)}) collective-permute-start(f32[224,128]{1,0:T(8,128)S(1)} %get-tuple-element.36.mid), channel_id=1, source_target_pairs={{0,24},{8,0},{16,8},{24,16},{1,25},{9,1},{17,9},{25,17},{2,26},{10... | collective-permute-start | bytes 344072 | tf_op jit(solution)/shard_map/ppermute | solution.py:409
  22.1 0.0 collective-permute-start.7
  22.1 3.8 %collective-permute-start.8 = (f32[8,16,384]{2,1,0:T(8,128)}, f32[8,16,384]{2,1,0:T(8,128)}, u32[]{:S(2)}, u32[]{:S(2)}) collective-permute-start(f32[8,16,384]{2,1,0:T(8,128)} %get-tuple-element.42), channel_id=1, source_target_pairs={{0,24},{8,0},{16,8},{24,16},{1,25},{9,1},{17,9},{25,17},{2,26},{10... | collective-permute-start | bytes 589832 | tf_op jit(solution)/shard_map/ppermute | solution.py:409
  25.9 0.0 collective-permute-start.4
  25.9 0.0 collective-permute-done.5.right
  25.9 0.6 copy-done.2
  26.5 0.6 collective-permute-start.9
  27.1 0.6 compare_select_fusion
  28.4 1.4 %reshape.15.heat = f32[8,128]{1,0:T(8,128)} reshape(f32[8,8,16]{2,1,0:T(8,128)} %param.10) | data formatting | bytes 8192 | tf_op jit(solution)/shard_map/reshape | solution.py:430
  29.8 1.4 %reshape.14.fluid = f32[8,128]{1,0:T(8,128)} reshape(f32[8,8,16]{2,1,0:T(8,128)} %compare_select_fusion) | data formatting | bytes 8192 | tf_op jit(solution)/shard_map/reshape | solution.py:429
  31.2 0.9 %broadcast_in_dim.24.fluid = f32[8,8,16,128]{3,2,1,0:T(8,128)S(1)} broadcast(f32[8,8,16]{2,1,0:T(8,128)} %compare_select_fusion), dimensions={0,1,2} | broadcast | bytes 528384 | tf_op jit(solution)/shard_map/broadcast_in_dim | solution.py:431
  32.2 0.0 copy-start.3
  32.2 1.3 %stream.3.g = f32[8,8,16,768]{3,2,1,0:T(8,128)S(1)} custom-call(f32[8,8,16,768]{3,2,1,0:T(8,128)S(1)} %copy-done.1, f32[8,768]{1,0:T(8,128)S(1)} %get-tuple-element.34.coef, f32[8,8,16,128]{3,2,1,0:T(8,128)S(1)} %broadcast_in_dim.24.fluid), custom_call_target="tpu_custom_call" | custom-call | tf_op jit(solution)/shard_map/stream/pallas_call | solution.py:190
  33.5 2.8 %collective-permute-done.4.left = f32[224,128]{1,0:T(8,128)} collective-permute-done((f32[224,128]{1,0:T(8,128)S(1)}, f32[224,128]{1,0:T(8,128)}, u32[]{:S(2)}, u32[]{:S(2)}) %collective-permute-start.4) | collective-permute-done | bytes 114720 | tf_op jit(solution)/shard_map/ppermute | solution.py:409
  36.4 2.6 %macro.3 = (f32[384,128]{1,0:T(8,128)S(1)}, f32[5,8,128]{2,1,0:T(8,128)}, f32[8,128]{1,0:T(8,128)S(1)}) custom-call(f32[224,128]{1,0:T(8,128)S(1)} %get-tuple-element.36.mid, f32[224,128]{1,0:T(8,128)} %collective-permute-done.4.left, f32[224,128]{1,0:T(8,128)S(1)} %copy-done.3, f32[8,128]{1,0:T(8,128)S(1)} %copy-done.5, f32[8,128]{1,0:T(8,128)S(1)} %copy-done.4), custom_call_target="tpu_custom_call" | custom-call | tf_op jit(solution)/shard_map/macro/pallas_call | solution.py:314
  38.9 0.0 collective-permute-done.9.far
  38.9 0.0 collective-permute-done.7.xbefore
  38.9 3.0 %update.3 = (f32[8,8,16,768]{3,2,1,0:T(8,128)S(1)}, f32[112,128]{1,0:T(8,128)S(1)}, f32[8,16,768]{2,1,0:T(8,128)S(1)}, f32[8,16,384]{2,1,0:T(8,128)S(1)}, f32[8,16,384]{2,1,0:T(8,128)S(1)}) custom-call(f32[1]{0:T(128)} %bitcast.2.target, f32[8,8,16,768]{3,2,1,0:T(8,128)S(1)} %stream.3.g, f32[384,128]{1,0:T(8,128)S(1)} %get-tuple-element.37.mix, ...), custom_call_target="tpu_custom_call" | custom-call | tf_op jit(solution)/shard_map/update/pallas_call | solution.py:398
  42.0 1.4 %collective-permute-start.16 = (f32[8,16,768]{2,1,0:T(8,128)S(1)}, f32[8,16,768]{2,1,0:T(8,128)S(1)}, u32[]{:S(2)}, u32[]{:S(2)}) collective-permute-start(f32[8,16,768]{2,1,0:T(8,128)S(1)} %get-tuple-element.49), channel_id=1, source_target_pairs={{0,4},{4,0},{1,5},{5,1},{2,6},{6,2},{3,7},{7,3},{8,12},{12,8},{9,1... | collective-permute-start | bytes 1179656 | tf_op jit(solution)/shard_map/ppermute | solution.py:409
  43.4 1.2 %collective-permute-done.10 = f32[112,128]{1,0:T(8,128)S(1)} collective-permute-done((f32[112,128]{1,0:T(8,128)S(1)}, f32[112,128]{1,0:T(8,128)S(1)}, u32[]{:S(2)}, u32[]{:S(2)}) %collective-permute-start.10) | collective-permute-done | bytes 57376 | tf_op jit(solution)/shard_map/ppermute | solution.py:426
  44.7 1.4 %collective-permute-start.13 = (f32[112,128]{1,0:T(8,128)S(1)}, f32[112,128]{1,0:T(8,128)S(1)}, u32[]{:S(2)}, u32[]{:S(2)}) collective-permute-start(f32[112,128]{1,0:T(8,128)S(1)} %add.10.mom), channel_id=1, source_target_pairs={{0,6},{1,7},{2,4},{3,5},{4,2},{5,3},{6,0},{7,1},{8,14},{9,15},{10,... | collective-permute-start | bytes 172040 | tf_op jit(solution)/shard_map/ppermute | solution.py:426
  46.1 0.8 collective-permute-start.17
  46.8 3.1 %collective-permute-start.18 = (f32[8,16,384]{2,1,0:T(8,128)S(1)}, f32[8,16,384]{2,1,0:T(8,128)S(1)}, u32[]{:S(2)}, u32[]{:S(2)}) collective-permute-start(f32[8,16,384]{2,1,0:T(8,128)S(1)} %get-tuple-element.51), channel_id=1, source_target_pairs={{0,24},{8,0},{16,8},{24,16},{1,25},{9,1},{17,9},{25,17},{2,26},{10... | collective-permute-start | bytes 589832 | tf_op jit(solution)/shard_map/ppermute | solution.py:409
  49.9 0.7 collective-permute-start.12
  50.5 1.5 %collective-permute-start.11 = (f32[112,128]{1,0:T(8,128)S(1)}, f32[112,128]{1,0:T(8,128)S(1)}, u32[]{:S(2)}, u32[]{:S(2)}) collective-permute-start(f32[112,128]{1,0:T(8,128)S(1)} %add.10.mom), channel_id=1, source_target_pairs={{0,2},{1,3},{2,0},{3,1},{4,6},{5,7},{6,4},{7,5},{8,10},{9,11},{10,... | collective-permute-start | bytes 172040 | tf_op jit(solution)/shard_map/ppermute | solution.py:426
  52.0 2.0 %collective-permute-done.12.beside = f32[112,128]{1,0:T(8,128)S(1)} collective-permute-done((f32[112,128]{1,0:T(8,128)S(1)}, f32[112,128]{1,0:T(8,128)S(1)}, u32[]{:S(2)}, u32[]{:S(2)}) %collective-permute-start.12) | collective-permute-done | bytes 57376 | tf_op jit(solution)/shard_map/ppermute | solution.py:426
  54.1 0.7 collective-permute-done.11.across
  54.7 0.6 collective-permute-start.15
  55.3 1.5 %collective-permute-start.14 = (f32[224,128]{1,0:T(8,128)S(1)}, f32[224,128]{1,0:T(8,128)S(1)}, u32[]{:S(2)}, u32[]{:S(2)}) collective-permute-start(f32[224,128]{1,0:T(8,128)S(1)} %get-tuple-element.47.mid), channel_id=1, source_target_pairs={{0,8},{8,16},{16,24},{24,0},{1,9},{9,17},{17,25},{25,1},{2,10},{10... | collective-permute-start | bytes 344072 | tf_op jit(solution)/shard_map/ppermute | solution.py:409
  56.8 3.0 %collective-permute-done.15.right = f32[224,128]{1,0:T(8,128)S(1)} collective-permute-done((f32[224,128]{1,0:T(8,128)S(1)}, f32[224,128]{1,0:T(8,128)S(1)}, u32[]{:S(2)}, u32[]{:S(2)}) %collective-permute-start.15) | collective-permute-done | bytes 114720 | tf_op jit(solution)/shard_map/ppermute | solution.py:409
  59.9 3.0 %collective-permute-start.19 = (f32[8,128]{1,0:T(8,128)S(1)}, f32[8,128]{1,0:T(8,128)S(1)}, u32[]{:S(2)}, u32[]{:S(2)}) collective-permute-start(f32[8,128]{1,0:T(8,128)S(1)} %get-tuple-element.53), channel_id=1, source_target_pairs={{0,16},{8,24},{16,0},{24,8},{1,17},{9,25},{17,1},{25,9},{2,18},{10... | collective-permute-start | bytes 12296 | tf_op jit(solution)/shard_map/ppermute | solution.py:409
  62.9 1.3 %stream.4.g = f32[8,8,16,768]{3,2,1,0:T(8,128)S(1)} custom-call(f32[8,8,16,768]{3,2,1,0:T(8,128)S(1)} %get-tuple-element.45.h, f32[8,768]{1,0:T(8,128)S(1)} %get-tuple-element.34.coef, f32[8,8,16,128]{3,2,1,0:T(8,128)S(1)} %broadcast_in_dim.24.fluid), custom_call_target="tpu_custom_call" | custom-call | tf_op jit(solution)/shard_map/stream/pallas_call | solution.py:190
  64.2 1.7 %macro.4 = (f32[384,128]{1,0:T(8,128)S(1)}, f32[5,8,128]{2,1,0:T(8,128)}, f32[8,128]{1,0:T(8,128)S(1)}) custom-call(f32[224,128]{1,0:T(8,128)S(1)} %get-tuple-element.47.mid, f32[224,128]{1,0:T(8,128)S(1)} %collective-permute-done.14.left, f32[224,128]{1,0:T(8,128)S(1)} %collective-permute-done.15.right, f32[8,128]{1,0:T(8,128)S(1)} %copy-done.5, ...), custom_call_target="tpu_custom_call" | custom-call | tf_op jit(solution)/shard_map/macro/pallas_call | solution.py:314
  65.9 1.9 %update.4 = (f32[8,8,16,768]{3,2,1,0:T(8,128)S(1)}, f32[112,128]{1,0:T(8,128)S(1)}, f32[8,16,768]{2,1,0:T(8,128)S(1)}, f32[8,16,384]{2,1,0:T(8,128)S(1)}, f32[8,16,384]{2,1,0:T(8,128)S(1)}) custom-call(f32[1]{0:T(128)} %bitcast.3.target, f32[8,8,16,768]{3,2,1,0:T(8,128)S(1)} %stream.4.g, f32[384,128]{1,0:T(8,128)S(1)} %get-tuple-element.48.mix, ...), custom_call_target="tpu_custom_call" | custom-call | tf_op jit(solution)/shard_map/update/pallas_call | solution.py:398
  67.8 0.7 collective-permute-start.26
  68.5 1.2 %collective-permute-done.20 = f32[112,128]{1,0:T(8,128)S(1)} collective-permute-done((f32[112,128]{1,0:T(8,128)S(1)}, f32[112,128]{1,0:T(8,128)S(1)}, u32[]{:S(2)}, u32[]{:S(2)}) %collective-permute-start.20) | collective-permute-done | bytes 57376 | tf_op jit(solution)/shard_map/ppermute | solution.py:426
  69.7 1.6 %collective-permute-start.23 = (f32[112,128]{1,0:T(8,128)S(1)}, f32[112,128]{1,0:T(8,128)S(1)}, u32[]{:S(2)}, u32[]{:S(2)}) collective-permute-start(f32[112,128]{1,0:T(8,128)S(1)} %add.11.mom), channel_id=1, source_target_pairs={{0,6},{1,7},{2,4},{3,5},{4,2},{5,3},{6,0},{7,1},{8,14},{9,15},{10,... | collective-permute-start | bytes 172040 | tf_op jit(solution)/shard_map/ppermute | solution.py:426
  71.3 1.4 %collective-permute-start.27 = (f32[8,16,384]{2,1,0:T(8,128)S(1)}, f32[8,16,384]{2,1,0:T(8,128)S(1)}, u32[]{:S(2)}, u32[]{:S(2)}) collective-permute-start(f32[8,16,384]{2,1,0:T(8,128)S(1)} %get-tuple-element.59), channel_id=1, source_target_pairs={{0,8},{8,16},{16,24},{24,0},{1,9},{9,17},{17,25},{25,1},{2,10},{10... | collective-permute-start | bytes 589832 | tf_op jit(solution)/shard_map/ppermute | solution.py:409
  72.7 2.4 %collective-permute-start.28 = (f32[8,16,384]{2,1,0:T(8,128)S(1)}, f32[8,16,384]{2,1,0:T(8,128)S(1)}, u32[]{:S(2)}, u32[]{:S(2)}) collective-permute-start(f32[8,16,384]{2,1,0:T(8,128)S(1)} %get-tuple-element.60), channel_id=1, source_target_pairs={{0,24},{8,0},{16,8},{24,16},{1,25},{9,1},{17,9},{25,17},{2,26},{10... | collective-permute-start | bytes 589832 | tf_op jit(solution)/shard_map/ppermute | solution.py:409
  75.1 1.4 %collective-permute-start.22 = (f32[112,128]{1,0:T(8,128)S(1)}, f32[112,128]{1,0:T(8,128)S(1)}, u32[]{:S(2)}, u32[]{:S(2)}) collective-permute-start(f32[112,128]{1,0:T(8,128)S(1)} %add.11.mom), channel_id=1, source_target_pairs={{0,4},{1,5},{2,6},{3,7},{4,0},{5,1},{6,2},{7,3},{8,12},{9,13},{10,... | collective-permute-start | bytes 172040 | tf_op jit(solution)/shard_map/ppermute | solution.py:426
  76.5 0.5 collective-permute-start.21
  77.1 2.7 %collective-permute-done.22.beside = f32[112,128]{1,0:T(8,128)S(1)} collective-permute-done((f32[112,128]{1,0:T(8,128)S(1)}, f32[112,128]{1,0:T(8,128)S(1)}, u32[]{:S(2)}, u32[]{:S(2)}) %collective-permute-start.22) | collective-permute-done | bytes 57376 | tf_op jit(solution)/shard_map/ppermute | solution.py:426
  79.7 1.0 %collective-permute-done.21.across = f32[112,128]{1,0:T(8,128)S(1)} collective-permute-done((f32[112,128]{1,0:T(8,128)S(1)}, f32[112,128]{1,0:T(8,128)S(1)}, u32[]{:S(2)}, u32[]{:S(2)}) %collective-permute-start.21) | collective-permute-done | bytes 57376 | tf_op jit(solution)/shard_map/ppermute | solution.py:426
  80.7 0.8 collective-permute-start.25
  81.5 1.3 %collective-permute-start.24 = (f32[224,128]{1,0:T(8,128)S(1)}, f32[224,128]{1,0:T(8,128)S(1)}, u32[]{:S(2)}, u32[]{:S(2)}) collective-permute-start(f32[224,128]{1,0:T(8,128)S(1)} %get-tuple-element.56.mid), channel_id=1, source_target_pairs={{0,8},{8,16},{16,24},{24,0},{1,9},{9,17},{17,25},{25,1},{2,10},{10... | collective-permute-start | bytes 344072 | tf_op jit(solution)/shard_map/ppermute | solution.py:409
  82.8 3.3 %collective-permute-done.25.right = f32[224,128]{1,0:T(8,128)S(1)} collective-permute-done((f32[224,128]{1,0:T(8,128)S(1)}, f32[224,128]{1,0:T(8,128)S(1)}, u32[]{:S(2)}, u32[]{:S(2)}) %collective-permute-start.25) | collective-permute-done | bytes 114720 | tf_op jit(solution)/shard_map/ppermute | solution.py:409
  86.1 2.0 %collective-permute-start.29 = (f32[8,128]{1,0:T(8,128)S(1)}, f32[8,128]{1,0:T(8,128)S(1)}, u32[]{:S(2)}, u32[]{:S(2)}) collective-permute-start(f32[8,128]{1,0:T(8,128)S(1)} %get-tuple-element.62), channel_id=1, source_target_pairs={{0,16},{8,24},{16,0},{24,8},{1,17},{9,25},{17,1},{25,9},{2,18},{10... | collective-permute-start | bytes 12296 | tf_op jit(solution)/shard_map/ppermute | solution.py:409
  88.1 1.3 %stream.5.g = f32[8,8,16,768]{3,2,1,0:T(8,128)S(1)} custom-call(f32[8,8,16,768]{3,2,1,0:T(8,128)S(1)} %get-tuple-element.54.h, f32[8,768]{1,0:T(8,128)S(1)} %get-tuple-element.34.coef, f32[8,8,16,128]{3,2,1,0:T(8,128)S(1)} %broadcast_in_dim.24.fluid), custom_call_target="tpu_custom_call" | custom-call | tf_op jit(solution)/shard_map/stream/pallas_call | solution.py:190
  89.5 1.1 %macro.5 = (f32[384,128]{1,0:T(8,128)S(1)}, f32[5,8,128]{2,1,0:T(8,128)S(1)}, f32[8,128]{1,0:T(8,128)S(1)}) custom-call(f32[224,128]{1,0:T(8,128)S(1)} %get-tuple-element.56.mid, f32[224,128]{1,0:T(8,128)S(1)} %collective-permute-done.24.left, f32[224,128]{1,0:T(8,128)S(1)} %collective-permute-done.25.right, f32[8,128]{1,0:T(8,128)S(1)} %copy-done.5, ...), custom_call_target="tpu_custom_call" | custom-call | tf_op jit(solution)/shard_map/macro/pallas_call | solution.py:314
  90.6 0.0 collective-permute-done.29.far
  90.6 3.0 %update.5 = (f32[8,8,16,768]{3,2,1,0:T(8,128)}, f32[320,16]{1,0:T(8,128)}) custom-call(f32[1]{0:T(128)} %bitcast.4.target, f32[8,8,16,768]{3,2,1,0:T(8,128)S(1)} %stream.5.g, f32[384,128]{1,0:T(8,128)S(1)} %get-tuple-element.57.mix, bf16[144,768]{1,0:T(8,128)(2,1)S(1)} %get-tuple-element.38.wmat, bf16[32,768]{1,0:T(8,128)(2,1)S(1)} %get-tuple-element.39.proj, ...), custom_call_target="tpu_custom_call" | custom-call | tf_op jit(solution)/shard_map/update/pallas_call | solution.py:398
  (33 shorter events, 0.1 us)
Async XLA Ops:
  1.3 1.9 %copy-start = (f32[8,8,16,768]{3,2,1,0:T(8,128)S(1)}, f32[8,8,16,768]{3,2,1,0:T(8,128)}, u32[]{:S(2)}) copy-start(f32[8,8,16,768]{3,2,1,0:T(8,128)} %h.3) | copy-start | bytes 9437188
  3.2 0.7 copy-start.6
  3.9 23.2 %copy-start.7 = (s32[8,8,16]{2,1,0:T(8,128)S(1)}, s32[8,8,16]{2,1,0:T(8,128)}, u32[]{:S(2)}) copy-start(s32[8,8,16]{2,1,0:T(8,128)} %param.9) | copy-start | bytes 12292
  3.9 28.3 %copy-start.1 = (f32[8,8,16,768]{3,2,1,0:T(8,128)S(1)}, f32[8,8,16,768]{3,2,1,0:T(8,128)}, u32[]{:S(2)}) copy-start(f32[8,8,16,768]{3,2,1,0:T(8,128)} %h.3) | copy-start | bytes 9437188
  7.8 1.4 %collective-permute-start = (f32[112,128]{1,0:T(8,128)S(1)}, f32[112,128]{1,0:T(8,128)S(1)}, u32[]{:S(2)}, u32[]{:S(2)}) collective-permute-start(f32[112,128]{1,0:T(8,128)S(1)} %get-tuple-element.35), channel_id=1, source_target_pairs={{0,1},{1,0},{2,3},{3,2},{4,5},{5,4},{6,7},{7,6},{8,9},{9,8},{10,11... | collective-permute-start | bytes 172040 | tf_op jit(solution)/shard_map/ppermute | solution.py:426
  9.2 6.4 %collective-permute-start.3 = (f32[112,128]{1,0:T(8,128)S(1)}, f32[112,128]{1,0:T(8,128)S(1)}, u32[]{:S(2)}, u32[]{:S(2)}) collective-permute-start(f32[112,128]{1,0:T(8,128)S(1)} %add.9.mom), channel_id=1, source_target_pairs={{0,6},{1,7},{2,4},{3,5},{4,2},{5,3},{6,0},{7,1},{8,14},{9,15},{10,... | collective-permute-start | bytes 172040 | tf_op jit(solution)/shard_map/ppermute | solution.py:426
  13.1 4.8 %collective-permute-start.2 = (f32[112,128]{1,0:T(8,128)S(1)}, f32[112,128]{1,0:T(8,128)S(1)}, u32[]{:S(2)}, u32[]{:S(2)}) collective-permute-start(f32[112,128]{1,0:T(8,128)S(1)} %add.9.mom), channel_id=1, source_target_pairs={{0,4},{1,5},{2,6},{3,7},{4,0},{5,1},{6,2},{7,3},{8,12},{9,13},{10,... | collective-permute-start | bytes 172040 | tf_op jit(solution)/shard_map/ppermute | solution.py:426
  13.6 4.3 %collective-permute-start.1 = (f32[112,128]{1,0:T(8,128)S(1)}, f32[112,128]{1,0:T(8,128)S(1)}, u32[]{:S(2)}, u32[]{:S(2)}) collective-permute-start(f32[112,128]{1,0:T(8,128)S(1)} %add.9.mom), channel_id=1, source_target_pairs={{0,2},{1,3},{2,0},{3,1},{4,6},{5,7},{6,4},{7,5},{8,10},{9,11},{10,... | collective-permute-start | bytes 172040 | tf_op jit(solution)/shard_map/ppermute | solution.py:426
  13.7 25.2 %collective-permute-start.6 = (f32[8,16,768]{2,1,0:T(8,128)}, f32[8,16,768]{2,1,0:T(8,128)}, u32[]{:S(2)}, u32[]{:S(2)}) collective-permute-start(f32[8,16,768]{2,1,0:T(8,128)} %get-tuple-element.40), channel_id=1, source_target_pairs={{0,4},{4,0},{1,5},{5,1},{2,6},{6,2},{3,7},{7,3},{8,12},{12,8},{9,1... | collective-permute-start | bytes 1179656 | tf_op jit(solution)/shard_map/ppermute | solution.py:409
  18.5 7.4 %collective-permute-start.5 = (f32[224,128]{1,0:T(8,128)S(1)}, f32[224,128]{1,0:T(8,128)S(1)}, u32[]{:S(2)}, u32[]{:S(2)}) collective-permute-start(f32[224,128]{1,0:T(8,128)S(1)} %get-tuple-element.36.mid), channel_id=1, source_target_pairs={{0,24},{8,0},{16,8},{24,16},{1,25},{9,1},{17,9},{25,17},{2,26},{10... | collective-permute-start | bytes 344072 | tf_op jit(solution)/shard_map/ppermute | solution.py:409
  22.1 16.9 %collective-permute-start.7 = (f32[8,16,384]{2,1,0:T(8,128)}, f32[8,16,384]{2,1,0:T(8,128)}, u32[]{:S(2)}, u32[]{:S(2)}) collective-permute-start(f32[8,16,384]{2,1,0:T(8,128)} %get-tuple-element.41), channel_id=1, source_target_pairs={{0,8},{8,16},{16,24},{24,0},{1,9},{9,17},{17,25},{25,1},{2,10},{10... | collective-permute-start | bytes 589832 | tf_op jit(solution)/shard_map/ppermute | solution.py:409
  22.1 16.9 %collective-permute-start.8 = (f32[8,16,384]{2,1,0:T(8,128)}, f32[8,16,384]{2,1,0:T(8,128)}, u32[]{:S(2)}, u32[]{:S(2)}) collective-permute-start(f32[8,16,384]{2,1,0:T(8,128)} %get-tuple-element.42), channel_id=1, source_target_pairs={{0,24},{8,0},{16,8},{24,16},{1,25},{9,1},{17,9},{25,17},{2,26},{10... | collective-permute-start | bytes 589832 | tf_op jit(solution)/shard_map/ppermute | solution.py:409
  25.9 10.5 %collective-permute-start.4 = (f32[224,128]{1,0:T(8,128)S(1)}, f32[224,128]{1,0:T(8,128)}, u32[]{:S(2)}, u32[]{:S(2)}) collective-permute-start(f32[224,128]{1,0:T(8,128)S(1)} %get-tuple-element.36.mid), channel_id=1, source_target_pairs={{0,8},{8,16},{16,24},{24,0},{1,9},{9,17},{17,25},{25,1},{2,10},{10... | collective-permute-start | bytes 344072 | tf_op jit(solution)/shard_map/ppermute | solution.py:409
  25.9 0.6 copy-start.2
  26.5 12.4 %collective-permute-start.9 = (f32[8,128]{1,0:T(8,128)}, f32[8,128]{1,0:T(8,128)}, u32[]{:S(2)}, u32[]{:S(2)}) collective-permute-start(f32[8,128]{1,0:T(8,128)} %get-tuple-element.44), channel_id=1, source_target_pairs={{0,16},{8,24},{16,0},{24,8},{1,17},{9,25},{17,1},{25,9},{2,18},{10... | collective-permute-start | bytes 12296 | tf_op jit(solution)/shard_map/ppermute | solution.py:409
  32.2 4.2 %copy-start.3 = (f32[224,128]{1,0:T(8,128)S(1)}, f32[224,128]{1,0:T(8,128)}, u32[]{:S(2)}) copy-start(f32[224,128]{1,0:T(8,128)} %copy-done.2) | copy-start | bytes 344068
  32.2 4.2 %copy-start.4 = (f32[8,128]{1,0:T(8,128)S(1)}, f32[8,128]{1,0:T(8,128)}, u32[]{:S(2)}) copy-start(f32[8,128]{1,0:T(8,128)} %reshape.15.heat) | copy-start | bytes 12292
  32.2 4.2 %copy-start.5 = (f32[8,128]{1,0:T(8,128)S(1)}, f32[8,128]{1,0:T(8,128)}, u32[]{:S(2)}) copy-start(f32[8,128]{1,0:T(8,128)} %reshape.14.fluid) | copy-start | bytes 12292
  42.0 23.9 %collective-permute-start.16 = (f32[8,16,768]{2,1,0:T(8,128)S(1)}, f32[8,16,768]{2,1,0:T(8,128)S(1)}, u32[]{:S(2)}, u32[]{:S(2)}) collective-permute-start(f32[8,16,768]{2,1,0:T(8,128)S(1)} %get-tuple-element.49), channel_id=1, source_target_pairs={{0,4},{4,0},{1,5},{5,1},{2,6},{6,2},{3,7},{7,3},{8,12},{12,8},{9,1... | collective-permute-start | bytes 1179656 | tf_op jit(solution)/shard_map/ppermute | solution.py:409
  43.4 1.2 %collective-permute-start.10 = (f32[112,128]{1,0:T(8,128)S(1)}, f32[112,128]{1,0:T(8,128)S(1)}, u32[]{:S(2)}, u32[]{:S(2)}) collective-permute-start(f32[112,128]{1,0:T(8,128)S(1)} %get-tuple-element.46), channel_id=1, source_target_pairs={{0,1},{1,0},{2,3},{3,2},{4,5},{5,4},{6,7},{7,6},{8,9},{9,8},{10,11... | collective-permute-start | bytes 172040 | tf_op jit(solution)/shard_map/ppermute | solution.py:426
  44.7 5.9 %collective-permute-start.13 = (f32[112,128]{1,0:T(8,128)S(1)}, f32[112,128]{1,0:T(8,128)S(1)}, u32[]{:S(2)}, u32[]{:S(2)}) collective-permute-start(f32[112,128]{1,0:T(8,128)S(1)} %add.10.mom), channel_id=1, source_target_pairs={{0,6},{1,7},{2,4},{3,5},{4,2},{5,3},{6,0},{7,1},{8,14},{9,15},{10,... | collective-permute-start | bytes 172040 | tf_op jit(solution)/shard_map/ppermute | solution.py:426
  46.1 19.8 %collective-permute-start.17 = (f32[8,16,384]{2,1,0:T(8,128)S(1)}, f32[8,16,384]{2,1,0:T(8,128)S(1)}, u32[]{:S(2)}, u32[]{:S(2)}) collective-permute-start(f32[8,16,384]{2,1,0:T(8,128)S(1)} %get-tuple-element.50), channel_id=1, source_target_pairs={{0,8},{8,16},{16,24},{24,0},{1,9},{9,17},{17,25},{25,1},{2,10},{10... | collective-permute-start | bytes 589832 | tf_op jit(solution)/shard_map/ppermute | solution.py:409
  46.8 19.1 %collective-permute-start.18 = (f32[8,16,384]{2,1,0:T(8,128)S(1)}, f32[8,16,384]{2,1,0:T(8,128)S(1)}, u32[]{:S(2)}, u32[]{:S(2)}) collective-permute-start(f32[8,16,384]{2,1,0:T(8,128)S(1)} %get-tuple-element.51), channel_id=1, source_target_pairs={{0,24},{8,0},{16,8},{24,16},{1,25},{9,1},{17,9},{25,17},{2,26},{10... | collective-permute-start | bytes 589832 | tf_op jit(solution)/shard_map/ppermute | solution.py:409
  49.9 4.2 %collective-permute-start.12 = (f32[112,128]{1,0:T(8,128)S(1)}, f32[112,128]{1,0:T(8,128)S(1)}, u32[]{:S(2)}, u32[]{:S(2)}) collective-permute-start(f32[112,128]{1,0:T(8,128)S(1)} %add.10.mom), channel_id=1, source_target_pairs={{0,4},{1,5},{2,6},{3,7},{4,0},{5,1},{6,2},{7,3},{8,12},{9,13},{10,... | collective-permute-start | bytes 172040 | tf_op jit(solution)/shard_map/ppermute | solution.py:426
  50.5 4.2 %collective-permute-start.11 = (f32[112,128]{1,0:T(8,128)S(1)}, f32[112,128]{1,0:T(8,128)S(1)}, u32[]{:S(2)}, u32[]{:S(2)}) collective-permute-start(f32[112,128]{1,0:T(8,128)S(1)} %add.10.mom), channel_id=1, source_target_pairs={{0,2},{1,3},{2,0},{3,1},{4,6},{5,7},{6,4},{7,5},{8,10},{9,11},{10,... | collective-permute-start | bytes 172040 | tf_op jit(solution)/shard_map/ppermute | solution.py:426
  54.7 5.1 %collective-permute-start.15 = (f32[224,128]{1,0:T(8,128)S(1)}, f32[224,128]{1,0:T(8,128)S(1)}, u32[]{:S(2)}, u32[]{:S(2)}) collective-permute-start(f32[224,128]{1,0:T(8,128)S(1)} %get-tuple-element.47.mid), channel_id=1, source_target_pairs={{0,24},{8,0},{16,8},{24,16},{1,25},{9,1},{17,9},{25,17},{2,26},{10... | collective-permute-start | bytes 344072 | tf_op jit(solution)/shard_map/ppermute | solution.py:409
  55.3 8.9 %collective-permute-start.14 = (f32[224,128]{1,0:T(8,128)S(1)}, f32[224,128]{1,0:T(8,128)S(1)}, u32[]{:S(2)}, u32[]{:S(2)}) collective-permute-start(f32[224,128]{1,0:T(8,128)S(1)} %get-tuple-element.47.mid), channel_id=1, source_target_pairs={{0,8},{8,16},{16,24},{24,0},{1,9},{9,17},{17,25},{25,1},{2,10},{10... | collective-permute-start | bytes 344072 | tf_op jit(solution)/shard_map/ppermute | solution.py:409
  59.9 6.0 %collective-permute-start.19 = (f32[8,128]{1,0:T(8,128)S(1)}, f32[8,128]{1,0:T(8,128)S(1)}, u32[]{:S(2)}, u32[]{:S(2)}) collective-permute-start(f32[8,128]{1,0:T(8,128)S(1)} %get-tuple-element.53), channel_id=1, source_target_pairs={{0,16},{8,24},{16,0},{24,8},{1,17},{9,25},{17,1},{25,9},{2,18},{10... | collective-permute-start | bytes 12296 | tf_op jit(solution)/shard_map/ppermute | solution.py:409
  67.8 22.8 %collective-permute-start.26 = (f32[8,16,768]{2,1,0:T(8,128)S(1)}, f32[8,16,768]{2,1,0:T(8,128)S(1)}, u32[]{:S(2)}, u32[]{:S(2)}) collective-permute-start(f32[8,16,768]{2,1,0:T(8,128)S(1)} %get-tuple-element.58), channel_id=1, source_target_pairs={{0,4},{4,0},{1,5},{5,1},{2,6},{6,2},{3,7},{7,3},{8,12},{12,8},{9,1... | collective-permute-start | bytes 1179656 | tf_op jit(solution)/shard_map/ppermute | solution.py:409
  68.5 1.2 %collective-permute-start.20 = (f32[112,128]{1,0:T(8,128)S(1)}, f32[112,128]{1,0:T(8,128)S(1)}, u32[]{:S(2)}, u32[]{:S(2)}) collective-permute-start(f32[112,128]{1,0:T(8,128)S(1)} %get-tuple-element.55), channel_id=1, source_target_pairs={{0,1},{1,0},{2,3},{3,2},{4,5},{5,4},{6,7},{7,6},{8,9},{9,8},{10,11... | collective-permute-start | bytes 172040 | tf_op jit(solution)/shard_map/ppermute | solution.py:426
  69.7 6.8 %collective-permute-start.23 = (f32[112,128]{1,0:T(8,128)S(1)}, f32[112,128]{1,0:T(8,128)S(1)}, u32[]{:S(2)}, u32[]{:S(2)}) collective-permute-start(f32[112,128]{1,0:T(8,128)S(1)} %add.11.mom), channel_id=1, source_target_pairs={{0,6},{1,7},{2,4},{3,5},{4,2},{5,3},{6,0},{7,1},{8,14},{9,15},{10,... | collective-permute-start | bytes 172040 | tf_op jit(solution)/shard_map/ppermute | solution.py:426
  71.3 19.3 %collective-permute-start.27 = (f32[8,16,384]{2,1,0:T(8,128)S(1)}, f32[8,16,384]{2,1,0:T(8,128)S(1)}, u32[]{:S(2)}, u32[]{:S(2)}) collective-permute-start(f32[8,16,384]{2,1,0:T(8,128)S(1)} %get-tuple-element.59), channel_id=1, source_target_pairs={{0,8},{8,16},{16,24},{24,0},{1,9},{9,17},{17,25},{25,1},{2,10},{10... | collective-permute-start | bytes 589832 | tf_op jit(solution)/shard_map/ppermute | solution.py:409
  72.7 17.9 %collective-permute-start.28 = (f32[8,16,384]{2,1,0:T(8,128)S(1)}, f32[8,16,384]{2,1,0:T(8,128)S(1)}, u32[]{:S(2)}, u32[]{:S(2)}) collective-permute-start(f32[8,16,384]{2,1,0:T(8,128)S(1)} %get-tuple-element.60), channel_id=1, source_target_pairs={{0,24},{8,0},{16,8},{24,16},{1,25},{9,1},{17,9},{25,17},{2,26},{10... | collective-permute-start | bytes 589832 | tf_op jit(solution)/shard_map/ppermute | solution.py:409
  75.1 4.6 %collective-permute-start.22 = (f32[112,128]{1,0:T(8,128)S(1)}, f32[112,128]{1,0:T(8,128)S(1)}, u32[]{:S(2)}, u32[]{:S(2)}) collective-permute-start(f32[112,128]{1,0:T(8,128)S(1)} %add.11.mom), channel_id=1, source_target_pairs={{0,4},{1,5},{2,6},{3,7},{4,0},{5,1},{6,2},{7,3},{8,12},{9,13},{10,... | collective-permute-start | bytes 172040 | tf_op jit(solution)/shard_map/ppermute | solution.py:426
  76.5 4.2 %collective-permute-start.21 = (f32[112,128]{1,0:T(8,128)S(1)}, f32[112,128]{1,0:T(8,128)S(1)}, u32[]{:S(2)}, u32[]{:S(2)}) collective-permute-start(f32[112,128]{1,0:T(8,128)S(1)} %add.11.mom), channel_id=1, source_target_pairs={{0,2},{1,3},{2,0},{3,1},{4,6},{5,7},{6,4},{7,5},{8,10},{9,11},{10,... | collective-permute-start | bytes 172040 | tf_op jit(solution)/shard_map/ppermute | solution.py:426
  80.7 5.4 %collective-permute-start.25 = (f32[224,128]{1,0:T(8,128)S(1)}, f32[224,128]{1,0:T(8,128)S(1)}, u32[]{:S(2)}, u32[]{:S(2)}) collective-permute-start(f32[224,128]{1,0:T(8,128)S(1)} %get-tuple-element.56.mid), channel_id=1, source_target_pairs={{0,24},{8,0},{16,8},{24,16},{1,25},{9,1},{17,9},{25,17},{2,26},{10... | collective-permute-start | bytes 344072 | tf_op jit(solution)/shard_map/ppermute | solution.py:409
  81.5 7.9 %collective-permute-start.24 = (f32[224,128]{1,0:T(8,128)S(1)}, f32[224,128]{1,0:T(8,128)S(1)}, u32[]{:S(2)}, u32[]{:S(2)}) collective-permute-start(f32[224,128]{1,0:T(8,128)S(1)} %get-tuple-element.56.mid), channel_id=1, source_target_pairs={{0,8},{8,16},{16,24},{24,0},{1,9},{9,17},{17,25},{25,1},{2,10},{10... | collective-permute-start | bytes 344072 | tf_op jit(solution)/shard_map/ppermute | solution.py:409
  86.1 4.5 %collective-permute-start.29 = (f32[8,128]{1,0:T(8,128)S(1)}, f32[8,128]{1,0:T(8,128)S(1)}, u32[]{:S(2)}, u32[]{:S(2)}) collective-permute-start(f32[8,128]{1,0:T(8,128)S(1)} %get-tuple-element.62), channel_id=1, source_target_pairs={{0,16},{8,24},{16,0},{24,8},{1,17},{9,25},{17,1},{25,9},{2,18},{10... | collective-permute-start | bytes 12296 | tf_op jit(solution)/shard_map/ppermute | solution.py:409

commit v3 on v2

--- a/solution.py
+++ b/solution.py
@@ -40,99 +40,98 @@
     return both[:PROWS] + both[PROWS:] + dot(proj[:PROWS], low, ((1,), (1,)))
 
 
-def prepare_kernel(vel, wgt, h, mom, proj, wmat, coef, ysend, xup, xdown, rows, *, total):
-    x = pl.program_id(0)
-    planes = pl.num_programs(0)
+def prepare_kernel(
+    vel_far, wgt_far, target_far, source, h, mom, proj, wmat, coef, ysend, xup, xdown, goal, rows, vel, wgt, target, arrived, *, total
+):
+    planes, ny, nz, nv = source.shape
+    order = [planes - 1, *range(planes - 1)]
+    copies = [pltpu.make_async_copy(source.at[x], h.at[x], arrived.at[x]) for x in range(planes)]
+    small = [
+        pltpu.make_async_copy(far, near, arrived.at[planes + i])
+        for i, (far, near) in enumerate([(vel_far, vel), (wgt_far, wgt), (target_far, target)])
+    ]
+    for copy in small:
+        copy.start()
+    for x in order:
+        copies[x].start()
+    for copy in small:
+        copy.wait()
+    goal[...] = jnp.full(goal.shape, target[0], f32)
     vx, vy, vz = vel[0:1, :], vel[1:2, :], vel[2:3, :]
 
-    @pl.when(x == 0)
-    def _():
-        speed = vx * vx + vy * vy + vz * vz
-        scale = wgt[...] / total
-        one = jnp.ones_like(speed)
-        zero = jnp.zeros_like(speed)
-        table = [
-            one,
-            vx,
-            vy,
-            vz,
-            2.0 / 3.0 * speed - 1.0,
-            2.0 * (vx * vx - speed / 3.0),
-            2.0 * (vy * vy - speed / 3.0),
-            2.0 * (vz * vz - speed / 3.0),
-            2.0 * vx * vy,
-            2.0 * vx * vz,
-            2.0 * vy * vz,
-            vx * (speed - 2.5),
-            vy * (speed - 2.5),
-            vz * (speed - 2.5),
-        ]
-        for k, row in enumerate(table):
-            rows[k : k + 1, :] = row * scale
-        for k in range(MOMENTS, PROWS):
-            rows[k : k + 1, :] = zero
-        high, low = split(rows[0:PROWS, :])
-        proj[0:PROWS, :] = high
-        proj[PROWS : 2 * PROWS, :] = low
-        along_x, along_y, along_z = (STEP_TIME * jnp.abs(v) for v in (vx, vy, vz))
-        centre = (1.0 - STEP_TIME * COLLISION) - (along_x + along_y + along_z)
-        for k, row in enumerate([centre, along_x, along_y, along_z, vy, vz, zero, zero]):
-            coef[k : k + 1, :] = row
-        basis = [one, 2.0 * vx, 2.0 * vy, 2.0 * vz, speed - 1.5]
-        parts = [
-            centre,
-            jnp.where(vx > 0.0, along_x, 0.0),
-            jnp.where(vx > 0.0, 0.0, along_x),
-            jnp.where(vy > 0.0, along_y, 0.0),
-            jnp.where(vy > 0.0, 0.0, along_y),
-            jnp.where(vz > 0.0, along_z, 0.0),
-            jnp.where(vz > 0.0, 0.0, along_z),
-            STEP_TIME * COLLISION * one,
-        ]
-        for i, part in enumerate(parts):
-            for k, row in enumerate(basis):
-                rows[5 * i + k : 5 * i + k + 1, :] = part * row
-        rows[40:41, :] = one
-        rows[41:42, :] = basis[4]
-        for k in range(42, KROWS):
-            rows[k : k + 1, :] = zero
-        high, low = split(rows[...])
-        wmat[0:KROWS, :] = high
-        wmat[KROWS : 2 * KROWS, :] = high
-        wmat[2 * KROWS : 3 * KROWS, :] = low
-
-    _, ny, nz, nv = h.shape
-    plane = h[0].reshape(ny * nz, nv)
-    out = local_moments(proj[...], plane)
-    mom[pl.ds(x, MOMENTS, stride=planes), :] = out[:MOMENTS]
-    ysend[0] = jnp.where(vy > 0.0, plane[(ny - 1) * nz :], plane[:nz])
-
-    @pl.when(x == planes - 1)
-    def _():
-        xup[...] = h[0, :, :, : nv // 2]
-
-    @pl.when(x == 0)
-    def _():
-        xdown[...] = h[0, :, :, nv // 2 :]
-
-
-def prepare(initial, velocity, weights, total):
+    speed = vx * vx + vy * vy + vz * vz
+    scale = wgt[...].reshape(1, nv) / total
+    one = jnp.ones_like(speed)
+    zero = jnp.zeros_like(speed)
+    table = [
+        one,
+        vx,
+        vy,
+        vz,
+        2.0 / 3.0 * speed - 1.0,
+        2.0 * (vx * vx - speed / 3.0),
+        2.0 * (vy * vy - speed / 3.0),
+        2.0 * (vz * vz - speed / 3.0),
+        2.0 * vx * vy,
+        2.0 * vx * vz,
+        2.0 * vy * vz,
+        vx * (speed - 2.5),
+        vy * (speed - 2.5),
+        vz * (speed - 2.5),
+    ]
+    for k, row in enumerate(table):
+        rows[k : k + 1, :] = row * scale
+    for k in range(MOMENTS, PROWS):
+        rows[k : k + 1, :] = zero
+    high, low = split(rows[0:PROWS, :])
+    proj[0:PROWS, :] = high
+    proj[PROWS : 2 * PROWS, :] = low
+    along_x, along_y, along_z = (STEP_TIME * jnp.abs(v) for v in (vx, vy, vz))
+    centre = (1.0 - STEP_TIME * COLLISION) - (along_x + along_y + along_z)
+    for k, row in enumerate([centre, along_x, along_y, along_z, vy, vz, zero, zero]):
+        coef[k : k + 1, :] = row
+    basis = [one, 2.0 * vx, 2.0 * vy, 2.0 * vz, speed - 1.5]
+    parts = [
+        centre,
+        jnp.where(vx > 0.0, along_x, 0.0),
+        jnp.where(vx > 0.0, 0.0, along_x),
+        jnp.where(vy > 0.0, along_y, 0.0),
+        jnp.where(vy > 0.0, 0.0, along_y),
+        jnp.where(vz > 0.0, along_z, 0.0),
+        jnp.where(vz > 0.0, 0.0, along_z),
+        STEP_TIME * COLLISION * one,
+    ]
+    for i, part in enumerate(parts):
+        for k, row in enumerate(basis):
+            rows[5 * i + k : 5 * i + k + 1, :] = part * row
+    rows[40:41, :] = one
+    rows[41:42, :] = basis[4]
+    for k in range(42, KROWS):
+        rows[k : k + 1, :] = zero
+    high, low = split(rows[...])
+    wmat[0:KROWS, :] = high
+    wmat[KROWS : 2 * KROWS, :] = high
+    wmat[2 * KROWS : 3 * KROWS, :] = low
+
+    for x in order:
+        copies[x].wait()
+        plane = h[x].reshape(ny * nz, nv)
+        out = local_moments(proj[...], plane)
+        mom[pl.ds(x, MOMENTS, stride=planes), :] = out[:MOMENTS]
+        ysend[x] = jnp.where(vy > 0.0, plane[(ny - 1) * nz :], plane[:nz])
+        if x == planes - 1:
+            xup[...] = h[x, :, :, : nv // 2]
+        if x == 0:
+            xdown[...] = h[x, :, :, nv // 2 :]
+
+
+def prepare(initial, velocity, weights, target, total):
     nx, ny, nz, nv = initial.shape
-    whole = lambda *shape: pl.BlockSpec(shape, lambda x: (0,) * len(shape))
     return pl.pallas_call(
         functools.partial(prepare_kernel, total=total),
-        grid=(nx,),
-        in_specs=[whole(3, nv), whole(1, nv), pl.BlockSpec((1, ny, nz, nv), lambda x: (x, 0, 0, 0))],
-        out_specs=[
-            whole(MOMENTS * nx, ny * nz),
-            whole(2 * PROWS, nv),
-            whole(3 * KROWS, nv),
-            whole(8, nv),
-            pl.BlockSpec((1, nz, nv), lambda x: (x, 0, 0)),
-            whole(ny, nz, nv // 2),
-            whole(ny, nz, nv // 2),
-        ],
+        in_specs=[pl.BlockSpec(memory_space=pltpu.HBM)] * 4,
         out_shape=[
+            jax.ShapeDtypeStruct(initial.shape, f32),
             jax.ShapeDtypeStruct((MOMENTS * nx, ny * nz), f32),
             jax.ShapeDtypeStruct((2 * PROWS, nv), bf16),
             jax.ShapeDtypeStruct((3 * KROWS, nv), bf16),
@@ -140,11 +139,47 @@
             jax.ShapeDtypeStruct((nx, nz, nv), f32),
             jax.ShapeDtypeStruct((ny, nz, nv // 2), f32),
             jax.ShapeDtypeStruct((ny, nz, nv // 2), f32),
+            jax.ShapeDtypeStruct((8, LANES), f32),
         ],
-        scratch_shapes=[pltpu.VMEM((KROWS, nv), f32)],
+        scratch_shapes=[
+            pltpu.VMEM((KROWS, nv), f32),
+            pltpu.VMEM(velocity.shape, f32),
+            pltpu.VMEM(weights.shape, f32),
+            pltpu.SMEM((1,), f32),
+            pltpu.SemaphoreType.DMA((nx + 3,)),
+        ],
         name="prepare",
-        compiler_params=pltpu.CompilerParams(vmem_limit_bytes=8 << 20),
-    )(velocity, weights[None], initial)
+        compiler_params=pltpu.CompilerParams(vmem_limit_bytes=12 << 20),
+    )(*(pltpu.with_memory_space_constraint(v, pltpu.HBM) for v in (velocity, weights)), target, pltpu.with_memory_space_constraint(initial, pltpu.HBM))
+
+
+def walls_kernel(wall, wall_temp, rows, heat, cells):
+    nx, ny, nz = wall.shape
+    square = (nz, nz)
+    same = lax.broadcasted_iota(jnp.int32, square, 0) == lax.broadcasted_iota(jnp.int32, square, 1)
+    for x in range(nx):
+        open_cells = jnp.where(wall[x] == 1, 0.0, 1.0)
+        temps = wall_temp[x]
+        for y in range(ny):
+            part = slice(y * nz, (y + 1) * nz)
+            rows[x : x + 1, part] = open_cells[y : y + 1]
+            heat[x : x + 1, part] = temps[y : y + 1]
+            spread = jnp.where(same, jnp.broadcast_to(open_cells[y : y + 1], square), 0.0)
+            cells[x, y] = jnp.broadcast_to(jnp.sum(spread, axis=1, keepdims=True), (nz, LANES))
+
+
+def walls(wall, wall_temp):
+    nx, ny, nz = wall.shape
+    return pl.pallas_call(
+        walls_kernel,
+        out_shape=[
+            jax.ShapeDtypeStruct((nx, ny * nz), f32),
+            jax.ShapeDtypeStruct((nx, ny * nz), f32),
+            jax.ShapeDtypeStruct((nx, ny, nz, LANES), f32),
+        ],
+        name="walls",
+        compiler_params=pltpu.CompilerParams(vmem_limit_bytes=6 << 20),
+    )(wall, wall_temp)
 
 
 def y_direction(lanes, nv):
@@ -327,12 +362,13 @@
     nx, ny, nz, nv = g.shape
     half = nv // 2
     if last:
-        state, h, fields = refs
+        state, result, fields, h, sent = refs
+        copies = [pltpu.make_async_copy(h.at[x], result.at[x], sent.at[x]) for x in range(nx)]
     else:
         h, mom, ysend, xup, xdown = refs
     total = mass[...] + far[...]
     total = jnp.sum(jnp.sum(total, axis=0, keepdims=True), axis=1, keepdims=True)
-    offset = target[0] - total / cells
+    offset = target[0:1, 0:1] - total / cells
     is_offset = lax.broadcasted_iota(jnp.int32, (KROWS, ny * nz), 0) == 40
     scale = jnp.where(is_offset, jnp.broadcast_to(offset, (KROWS, ny * nz)), 1.0)
     if last:
@@ -368,7 +404,10 @@
             pieces.append(piece)
         plane = jnp.concatenate(pieces, axis=0)
         h[x] = plane.reshape(ny, nz, nv)
-        if not last:
+        if last:
+            if x:
+                copies[x - 1].start()
+        else:
             out = local_moments(proj[...], plane)
             mom[pl.ds(x, MOMENTS, stride=nx), :] = out[:MOMENTS]
             ysend[x] = jnp.where(upward, plane[(ny - 1) * nz :], plane[:nz])
@@ -376,6 +415,10 @@
                 xup[...] = h[x, :, :, :half]
             if x == 0:
                 xdown[...] = h[x, :, :, half:]
+    if last:
+        copies[nx - 1].start()
+        for copy in copies:
+            copy.wait()
 
 
 def update(target, g, mix, wmat, proj, coef, fluid, halos, mass, far, state, cells):
@@ -397,8 +440,10 @@
     vmem = pl.BlockSpec(memory_space=pltpu.VMEM)
     return pl.pallas_call(
         functools.partial(update_kernel, last=last, cells=cells),
-        in_specs=[pl.BlockSpec(memory_space=pltpu.SMEM)] + [vmem] * (len(operands) - 1),
+        in_specs=[vmem] * len(operands),
         out_shape=shapes,
+        out_specs=[pl.BlockSpec(memory_space=pltpu.HBM), vmem] if last else [vmem] * len(shapes),
+        scratch_shapes=[pltpu.VMEM(g.shape, f32), pltpu.SemaphoreType.DMA((nx,))] if last else [],
         name="update",
         compiler_params=pltpu.CompilerParams(vmem_limit_bytes=14 << 20),
     )(*operands)
@@ -425,13 +470,9 @@
                 pairs.append((y * n_vel + v, (y ^ flip_y) * n_vel + (v ^ flip_v)))
         return lax.ppermute(value, ("ty", "vel"), pairs)
 
-    fluid = jnp.where(wall == 1, 0.0, 1.0).astype(f32)
-    fluid_rows = fluid.reshape(nx, width)
-    heat = wall_temp.reshape(nx, width)
-    fluid_cells = jnp.broadcast_to(fluid[..., None], (nx, ny, nz, LANES))
-    target = mass_target[None]
-    mom, proj, wmat, coef, ysend, xup, xdown = prepare(initial, velocity, weights, float(nv * n_vel))
-    h = initial
+    h, mom, proj, wmat, coef, ysend, xup, xdown, target = prepare(
+        initial, velocity, weights, mass_target[None], float(nv * n_vel)
+    )
     for iteration in range(ITERS):
         last = iteration == ITERS - 1
         bit = 1
@@ -453,6 +494,8 @@
             far = part if far is None else far + part
         if far is None:
             far = jnp.zeros_like(sums)
+        if iteration == 0:
+            fluid_rows, heat, fluid_cells = walls(wall, wall_temp)
         g = stream(h, coef, fluid_cells)
         mix, state, mass = macro(both, left, right, fluid_rows, heat, nz)
         halos = (yhalo, xbefore, xafter)

time: 94.1 us -> 88 us (0.935)
  local copies, waits for them, and re-layouts: 7.75 us -> 0.01 us
  waiting for transfers between devices: 21.1 us -> 26.5 us
  starting transfers between devices: 40.9 us -> 39.3 us
  Pallas kernels: 21.8 us -> 20.3 us
    ppermute x18, waiting for transfers between devices: 9.19 us -> 12.8 us  [ring(): lax.ppermute(value, axis, [(i, (i + step) % count) for i in range(count)])]
    unnamed x16 -> x4, local copies, waits for them, and re-layouts: 3.26 us -> 0.01 us
    reshape x2 -> x0, local copies, waits for them, and re-layouts: 2.85 us -> none  [the longest x1 1.43 us: on_device(): heat = wall_temp.reshape(nx, width)]
    ppermute x12, waiting for transfers between devices: 11.9 us -> 13.7 us  [plane_pair(): return lax.ppermute(value, ('ty', 'vel'), pairs)]
    broadcast_in_dim x2 -> x0, local copies, waits for them, and re-layouts: 1.64 us -> none  [the longest x1 0.95 us: on_device(): fluid_cells = jnp.broadcast_to(fluid[..., None], (nx, ny, nz, LANES))]
    ppermute x12, starting transfers between devices: 12.1 us -> 10.6 us  [plane_pair(): return lax.ppermute(value, ('ty', 'vel'), pairs)]
    pallas_call x1 -> x2, Pallas kernels: 3.9 us -> 4.81 us  [the longest x1 3.72 us: prepare(): pl.pallas_call(functools.partial(prepare_kernel, total=total), in_specs=[...]
  transfers between devices with their start and end apart: 30 -> 30, of which waited for: 11 -> 16; matrix products, arithmetic and copies ran while one was open for 5% -> 0% of each run, Pallas kernels for 11% -> 11%
where the time goes in v3:
time: 88 us; the launch traced here: 87.7 us
  starting transfers between devices  39.3 us (45%)
  waiting for transfers between devices  26.5 us (30%)
  Pallas kernels  20.3 us (23%)
  between operations  1.56 us (2%)
    ppermute x18, starting transfers between devices, ring(): lax.ppermute(value, axis, [(i, (i + step) % count) for i in range(count)])  28.7 us
    ppermute x12, waiting for transfers between devices, plane_pair(): return lax.ppermute(value, ('ty', 'vel'), pairs)  13.7 us
    ppermute x18, waiting for transfers between devices, ring(): lax.ppermute(value, axis, [(i, (i + step) % count) for i in range(count)])  12.8 us
    ppermute x12, starting transfers between devices, plane_pair(): return lax.ppermute(value, ('ty', 'vel'), pairs)  10.6 us
    pallas_call x3, Pallas kernels, update(): pl.pallas_call(functools.partial(update_kernel, last=last, cells=cells),...  6.97 us
    pallas_call x3, Pallas kernels, macro(): pl.pallas_call(functools.partial(macro_kernel, nz=nz), out_shape=[jax.Sha...  4.46 us
    pallas_call x3, Pallas kernels, stream(): pl.pallas_call(stream_kernel, out_shape=jax.ShapeDtypeStruct(h.shape, f32...  4.01 us
    pallas_call x1, Pallas kernels, prepare(): pl.pallas_call(functools.partial(prepare_kernel, total=total), in_specs=[...  3.72 us
  transfers between devices with their start and end apart: 30, of which 16 were waited for; matrix products, arithmetic and copies ran while one was open for 0% of the time, Pallas kernels for 11%

profile of v3, /device:TPU:0, one launch (start us, length us, event | category | flops | bytes accessed | tf_op | source)
XLA Modules:
  0.0 87.7 jit_solution(3474965478685509574)
XLA Ops:
  1.3 3.7 %prepare.1 = (f32[8,8,16,768]{3,2,1,0:T(8,128)S(1)}, f32[112,128]{1,0:T(8,128)S(1)}, bf16[32,768]{1,0:T(8,128)(2,1)S(1)}, bf16[144,768]{1,0:T(8,128)(2,1)S(1)}, ...) custom-call(f32[3,768]{1,0:T(4,128)} %vel_far.1, ...), custom_call_target="tpu_custom_call" | custom-call | tf_op jit(solution)/shard_map/prepare/pallas_call | solution.py:130
  5.0 3.1 %collective-permute-start.6 = (f32[8,16,768]{2,1,0:T(8,128)S(1)}, f32[8,16,768]{2,1,0:T(8,128)S(1)}, u32[]{:S(2)}, u32[]{:S(2)}) collective-permute-start(f32[8,16,768]{2,1,0:T(8,128)S(1)} %get-tuple-element.50), channel_id=1, source_target_pairs={{0,4},{4,0},{1,5},{5,1},{2,6},{6,2},{3,7},{7,3},{8,12},{12,8},{9,1... | collective-permute-start | bytes 1179656 | tf_op jit(solution)/shard_map/ppermute | solution.py:454
  8.1 0.0 collective-permute-start
  8.1 1.2 %collective-permute-done = f32[112,128]{1,0:T(8,128)S(1)} collective-permute-done((f32[112,128]{1,0:T(8,128)S(1)}, f32[112,128]{1,0:T(8,128)S(1)}, u32[]{:S(2)}, u32[]{:S(2)}) %collective-permute-start) | collective-permute-done | bytes 57376 | tf_op jit(solution)/shard_map/ppermute | solution.py:471
  9.3 1.5 %collective-permute-start.3 = (f32[112,128]{1,0:T(8,128)S(1)}, f32[112,128]{1,0:T(8,128)S(1)}, u32[]{:S(2)}, u32[]{:S(2)}) collective-permute-start(f32[112,128]{1,0:T(8,128)S(1)} %add.9.mom), channel_id=1, source_target_pairs={{0,6},{1,7},{2,4},{3,5},{4,2},{5,3},{6,0},{7,1},{8,14},{9,15},{10,... | collective-permute-start | bytes 172040 | tf_op jit(solution)/shard_map/ppermute | solution.py:471
  10.8 1.6 %collective-permute-start.7 = (f32[8,16,384]{2,1,0:T(8,128)S(1)}, f32[8,16,384]{2,1,0:T(8,128)S(1)}, u32[]{:S(2)}, u32[]{:S(2)}) collective-permute-start(f32[8,16,384]{2,1,0:T(8,128)S(1)} %get-tuple-element.51), channel_id=1, source_target_pairs={{0,8},{8,16},{16,24},{24,0},{1,9},{9,17},{17,25},{25,1},{2,10},{10... | collective-permute-start | bytes 589832 | tf_op jit(solution)/shard_map/ppermute | solution.py:454
  12.4 2.2 %collective-permute-start.8 = (f32[8,16,384]{2,1,0:T(8,128)S(1)}, f32[8,16,384]{2,1,0:T(8,128)S(1)}, u32[]{:S(2)}, u32[]{:S(2)}) collective-permute-start(f32[8,16,384]{2,1,0:T(8,128)S(1)} %get-tuple-element.52), channel_id=1, source_target_pairs={{0,24},{8,0},{16,8},{24,16},{1,25},{9,1},{17,9},{25,17},{2,26},{10... | collective-permute-start | bytes 589832 | tf_op jit(solution)/shard_map/ppermute | solution.py:454
  14.7 1.5 %collective-permute-start.2 = (f32[112,128]{1,0:T(8,128)S(1)}, f32[112,128]{1,0:T(8,128)S(1)}, u32[]{:S(2)}, u32[]{:S(2)}) collective-permute-start(f32[112,128]{1,0:T(8,128)S(1)} %add.9.mom), channel_id=1, source_target_pairs={{0,4},{1,5},{2,6},{3,7},{4,0},{5,1},{6,2},{7,3},{8,12},{9,13},{10,... | collective-permute-start | bytes 172040 | tf_op jit(solution)/shard_map/ppermute | solution.py:471
  16.2 0.5 collective-permute-start.1
  16.7 2.9 %collective-permute-done.2.beside = f32[112,128]{1,0:T(8,128)S(1)} collective-permute-done((f32[112,128]{1,0:T(8,128)S(1)}, f32[112,128]{1,0:T(8,128)S(1)}, u32[]{:S(2)}, u32[]{:S(2)}) %collective-permute-start.2) | collective-permute-done | bytes 57376 | tf_op jit(solution)/shard_map/ppermute | solution.py:471
  19.7 0.7 collective-permute-done.1.across
  20.4 3.2 %collective-permute-start.5 = (f32[224,128]{1,0:T(8,128)S(1)}, f32[224,128]{1,0:T(8,128)S(1)}, u32[]{:S(2)}, u32[]{:S(2)}) collective-permute-start(f32[224,128]{1,0:T(8,128)S(1)} %get-tuple-element.44.mid), channel_id=1, source_target_pairs={{0,24},{8,0},{16,8},{24,16},{1,25},{9,1},{17,9},{25,17},{2,26},{10... | collective-permute-start | bytes 344072 | tf_op jit(solution)/shard_map/ppermute | solution.py:454
  23.6 2.8 %collective-permute-done.5.right = f32[224,128]{1,0:T(8,128)S(1)} collective-permute-done((f32[224,128]{1,0:T(8,128)S(1)}, f32[224,128]{1,0:T(8,128)S(1)}, u32[]{:S(2)}, u32[]{:S(2)}) %collective-permute-start.5) | collective-permute-done | bytes 114720 | tf_op jit(solution)/shard_map/ppermute | solution.py:454
  26.4 1.1 %collective-permute-start.9 = (f32[8,128]{1,0:T(8,128)S(1)}, f32[8,128]{1,0:T(8,128)S(1)}, u32[]{:S(2)}, u32[]{:S(2)}) collective-permute-start(f32[8,128]{1,0:T(8,128)S(1)} %get-tuple-element.54), channel_id=1, source_target_pairs={{0,16},{8,24},{16,0},{24,8},{1,17},{9,25},{17,1},{25,9},{2,18},{10... | collective-permute-start | bytes 12296 | tf_op jit(solution)/shard_map/ppermute | solution.py:454
  27.5 1.1 %walls.1 = (f32[8,128]{1,0:T(8,128)S(1)}, f32[8,128]{1,0:T(8,128)S(1)}, f32[8,8,16,128]{3,2,1,0:T(8,128)S(1)}) custom-call(s32[8,8,16]{2,1,0:T(8,128)S(1)} %copy-done, f32[8,8,16]{2,1,0:T(8,128)S(1)} %copy-done.1), custom_call_target="tpu_custom_call" | custom-call | tf_op jit(solution)/shard_map/walls/pallas_call | solution.py:173
  28.6 1.3 %stream.3.g = f32[8,8,16,768]{3,2,1,0:T(8,128)S(1)} custom-call(f32[8,8,16,768]{3,2,1,0:T(8,128)S(1)} %get-tuple-element.40.h, f32[8,768]{1,0:T(8,128)S(1)} %get-tuple-element.41.coef, f32[8,8,16,128]{3,2,1,0:T(8,128)S(1)} %get-tuple-element.42.fluid), custom_call_target="tpu_custom_call" | custom-call | tf_op jit(solution)/shard_map/stream/pallas_call | solution.py:225
  29.9 0.3 collective-permute-done.4.left
  30.2 1.7 %macro.3 = (f32[384,128]{1,0:T(8,128)S(1)}, f32[5,8,128]{2,1,0:T(8,128)}, f32[8,128]{1,0:T(8,128)S(1)}) custom-call(f32[224,128]{1,0:T(8,128)S(1)} %get-tuple-element.44.mid, f32[224,128]{1,0:T(8,128)S(1)} %collective-permute-done.4.left, f32[224,128]{1,0:T(8,128)S(1)} %collective-permute-done.5.right, f32[8,128]{1,0:T(8,128)S(1)} %get-tuple-element.45.fluid, ...), custom_call_target="tpu_custom_call" | custom-call | tf_op jit(solution)/shard_map/macro/pallas_call | solution.py:349
  31.9 0.0 collective-permute-done.9.far
  31.9 0.0 collective-permute-done.6.yhalo
  31.9 1.9 %update.3 = (f32[8,8,16,768]{3,2,1,0:T(8,128)S(1)}, f32[112,128]{1,0:T(8,128)S(1)}, f32[8,16,768]{2,1,0:T(8,128)S(1)}, f32[8,16,384]{2,1,0:T(8,128)S(1)}, f32[8,16,384]{2,1,0:T(8,128)S(1)}) custom-call(f32[8,128]{1,0:T(8,128)S(1)} %get-tuple-element.39.target, f32[8,8,16,768]{3,2,1,0:T(8,128)S(1)} %stream.3.g, f32[384,128]{1,0:T(8,128)S(1)} %get-tuple-element.47.mix, ...), custom_call_target="tpu_custom_call" | custom-call | tf_op jit(solution)/shard_map/update/pallas_call | solution.py:441
  33.8 1.5 %collective-permute-start.16 = (f32[8,16,768]{2,1,0:T(8,128)S(1)}, f32[8,16,768]{2,1,0:T(8,128)S(1)}, u32[]{:S(2)}, u32[]{:S(2)}) collective-permute-start(f32[8,16,768]{2,1,0:T(8,128)S(1)} %get-tuple-element.59), channel_id=1, source_target_pairs={{0,4},{4,0},{1,5},{5,1},{2,6},{6,2},{3,7},{7,3},{8,12},{12,8},{9,1... | collective-permute-start | bytes 1179656 | tf_op jit(solution)/shard_map/ppermute | solution.py:454
  35.4 0.0 collective-permute-start.10
  35.4 1.2 %collective-permute-done.10 = f32[112,128]{1,0:T(8,128)S(1)} collective-permute-done((f32[112,128]{1,0:T(8,128)S(1)}, f32[112,128]{1,0:T(8,128)S(1)}, u32[]{:S(2)}, u32[]{:S(2)}) %collective-permute-start.10) | collective-permute-done | bytes 57376 | tf_op jit(solution)/shard_map/ppermute | solution.py:471
  36.6 1.5 %collective-permute-start.13 = (f32[112,128]{1,0:T(8,128)S(1)}, f32[112,128]{1,0:T(8,128)S(1)}, u32[]{:S(2)}, u32[]{:S(2)}) collective-permute-start(f32[112,128]{1,0:T(8,128)S(1)} %add.10.mom), channel_id=1, source_target_pairs={{0,6},{1,7},{2,4},{3,5},{4,2},{5,3},{6,0},{7,1},{8,14},{9,15},{10,... | collective-permute-start | bytes 172040 | tf_op jit(solution)/shard_map/ppermute | solution.py:471
  38.1 3.5 %collective-permute-start.17 = (f32[8,16,384]{2,1,0:T(8,128)S(1)}, f32[8,16,384]{2,1,0:T(8,128)S(1)}, u32[]{:S(2)}, u32[]{:S(2)}) collective-permute-start(f32[8,16,384]{2,1,0:T(8,128)S(1)} %get-tuple-element.60), channel_id=1, source_target_pairs={{0,8},{8,16},{16,24},{24,0},{1,9},{9,17},{17,25},{25,1},{2,10},{10... | collective-permute-start | bytes 589832 | tf_op jit(solution)/shard_map/ppermute | solution.py:454
  41.6 0.3 collective-permute-start.18
  41.9 1.5 %collective-permute-start.12 = (f32[112,128]{1,0:T(8,128)S(1)}, f32[112,128]{1,0:T(8,128)S(1)}, u32[]{:S(2)}, u32[]{:S(2)}) collective-permute-start(f32[112,128]{1,0:T(8,128)S(1)} %add.10.mom), channel_id=1, source_target_pairs={{0,4},{1,5},{2,6},{3,7},{4,0},{5,1},{6,2},{7,3},{8,12},{9,13},{10,... | collective-permute-start | bytes 172040 | tf_op jit(solution)/shard_map/ppermute | solution.py:471
  43.5 0.0 collective-permute-done.13.corner
  43.5 0.5 collective-permute-start.11
  44.0 2.1 %collective-permute-done.12.beside = f32[112,128]{1,0:T(8,128)S(1)} collective-permute-done((f32[112,128]{1,0:T(8,128)S(1)}, f32[112,128]{1,0:T(8,128)S(1)}, u32[]{:S(2)}, u32[]{:S(2)}) %collective-permute-start.12) | collective-permute-done | bytes 57376 | tf_op jit(solution)/shard_map/ppermute | solution.py:471
  46.1 1.5 %collective-permute-done.11.across = f32[112,128]{1,0:T(8,128)S(1)} collective-permute-done((f32[112,128]{1,0:T(8,128)S(1)}, f32[112,128]{1,0:T(8,128)S(1)}, u32[]{:S(2)}, u32[]{:S(2)}) %collective-permute-start.11) | collective-permute-done | bytes 57376 | tf_op jit(solution)/shard_map/ppermute | solution.py:471
  47.7 1.6 %collective-permute-start.15 = (f32[224,128]{1,0:T(8,128)S(1)}, f32[224,128]{1,0:T(8,128)S(1)}, u32[]{:S(2)}, u32[]{:S(2)}) collective-permute-start(f32[224,128]{1,0:T(8,128)S(1)} %get-tuple-element.57.mid), channel_id=1, source_target_pairs={{0,24},{8,0},{16,8},{24,16},{1,25},{9,1},{17,9},{25,17},{2,26},{10... | collective-permute-start | bytes 344072 | tf_op jit(solution)/shard_map/ppermute | solution.py:454
  49.3 0.4 collective-permute-start.14
  49.7 4.6 %collective-permute-done.15.right = f32[224,128]{1,0:T(8,128)S(1)} collective-permute-done((f32[224,128]{1,0:T(8,128)S(1)}, f32[224,128]{1,0:T(8,128)S(1)}, u32[]{:S(2)}, u32[]{:S(2)}) %collective-permute-start.15) | collective-permute-done | bytes 114720 | tf_op jit(solution)/shard_map/ppermute | solution.py:454
  54.4 0.6 collective-permute-start.19
  55.0 1.3 %stream.4.g = f32[8,8,16,768]{3,2,1,0:T(8,128)S(1)} custom-call(f32[8,8,16,768]{3,2,1,0:T(8,128)S(1)} %get-tuple-element.55.h, f32[8,768]{1,0:T(8,128)S(1)} %get-tuple-element.41.coef, f32[8,8,16,128]{3,2,1,0:T(8,128)S(1)} %get-tuple-element.42.fluid), custom_call_target="tpu_custom_call" | custom-call | tf_op jit(solution)/shard_map/stream/pallas_call | solution.py:225
  56.3 0.0 collective-permute-done.14.left
  56.3 1.7 %macro.4 = (f32[384,128]{1,0:T(8,128)S(1)}, f32[5,8,128]{2,1,0:T(8,128)}, f32[8,128]{1,0:T(8,128)S(1)}) custom-call(f32[224,128]{1,0:T(8,128)S(1)} %get-tuple-element.57.mid, f32[224,128]{1,0:T(8,128)S(1)} %collective-permute-done.14.left, f32[224,128]{1,0:T(8,128)S(1)} %collective-permute-done.15.right, f32[8,128]{1,0:T(8,128)S(1)} %get-tuple-element.45.fluid, ...), custom_call_target="tpu_custom_call" | custom-call | tf_op jit(solution)/shard_map/macro/pallas_call | solution.py:349
  58.0 0.9 collective-permute-done.19.far
  58.9 0.0 collective-permute-done.17.xbefore
  58.9 0.0 collective-permute-done.18.xafter
  58.9 0.0 collective-permute-done.16.yhalo
  58.9 1.9 %update.4 = (f32[8,8,16,768]{3,2,1,0:T(8,128)S(1)}, f32[112,128]{1,0:T(8,128)S(1)}, f32[8,16,768]{2,1,0:T(8,128)S(1)}, f32[8,16,384]{2,1,0:T(8,128)S(1)}, f32[8,16,384]{2,1,0:T(8,128)S(1)}) custom-call(f32[8,128]{1,0:T(8,128)S(1)} %get-tuple-element.39.target, f32[8,8,16,768]{3,2,1,0:T(8,128)S(1)} %stream.4.g, f32[384,128]{1,0:T(8,128)S(1)} %get-tuple-element.58.mix, ...), custom_call_target="tpu_custom_call" | custom-call | tf_op jit(solution)/shard_map/update/pallas_call | solution.py:441
  60.8 1.5 %collective-permute-start.26 = (f32[8,16,768]{2,1,0:T(8,128)S(1)}, f32[8,16,768]{2,1,0:T(8,128)S(1)}, u32[]{:S(2)}, u32[]{:S(2)}) collective-permute-start(f32[8,16,768]{2,1,0:T(8,128)S(1)} %get-tuple-element.68), channel_id=1, source_target_pairs={{0,4},{4,0},{1,5},{5,1},{2,6},{6,2},{3,7},{7,3},{8,12},{12,8},{9,1... | collective-permute-start | bytes 1179656 | tf_op jit(solution)/shard_map/ppermute | solution.py:454
  62.3 1.2 %collective-permute-done.20 = f32[112,128]{1,0:T(8,128)S(1)} collective-permute-done((f32[112,128]{1,0:T(8,128)S(1)}, f32[112,128]{1,0:T(8,128)S(1)}, u32[]{:S(2)}, u32[]{:S(2)}) %collective-permute-start.20) | collective-permute-done | bytes 57376 | tf_op jit(solution)/shard_map/ppermute | solution.py:471
  63.6 0.3 collective-permute-start.23
  63.9 3.0 %collective-permute-start.27 = (f32[8,16,384]{2,1,0:T(8,128)S(1)}, f32[8,16,384]{2,1,0:T(8,128)S(1)}, u32[]{:S(2)}, u32[]{:S(2)}) collective-permute-start(f32[8,16,384]{2,1,0:T(8,128)S(1)} %get-tuple-element.69), channel_id=1, source_target_pairs={{0,8},{8,16},{16,24},{24,0},{1,9},{9,17},{17,25},{25,1},{2,10},{10... | collective-permute-start | bytes 589832 | tf_op jit(solution)/shard_map/ppermute | solution.py:454
  66.9 0.9 %collective-permute-start.28 = (f32[8,16,384]{2,1,0:T(8,128)S(1)}, f32[8,16,384]{2,1,0:T(8,128)S(1)}, u32[]{:S(2)}, u32[]{:S(2)}) collective-permute-start(f32[8,16,384]{2,1,0:T(8,128)S(1)} %get-tuple-element.70), channel_id=1, source_target_pairs={{0,24},{8,0},{16,8},{24,16},{1,25},{9,1},{17,9},{25,17},{2,26},{10... | collective-permute-start | bytes 589832 | tf_op jit(solution)/shard_map/ppermute | solution.py:454
  67.8 1.7 %collective-permute-start.22 = (f32[112,128]{1,0:T(8,128)S(1)}, f32[112,128]{1,0:T(8,128)S(1)}, u32[]{:S(2)}, u32[]{:S(2)}) collective-permute-start(f32[112,128]{1,0:T(8,128)S(1)} %add.11.mom), channel_id=1, source_target_pairs={{0,4},{1,5},{2,6},{3,7},{4,0},{5,1},{6,2},{7,3},{8,12},{9,13},{10,... | collective-permute-start | bytes 172040 | tf_op jit(solution)/shard_map/ppermute | solution.py:471
  69.5 0.0 collective-permute-done.23.corner
  69.5 1.5 %collective-permute-start.21 = (f32[112,128]{1,0:T(8,128)S(1)}, f32[112,128]{1,0:T(8,128)S(1)}, u32[]{:S(2)}, u32[]{:S(2)}) collective-permute-start(f32[112,128]{1,0:T(8,128)S(1)} %add.11.mom), channel_id=1, source_target_pairs={{0,2},{1,3},{2,0},{3,1},{4,6},{5,7},{6,4},{7,5},{8,10},{9,11},{10,... | collective-permute-start | bytes 172040 | tf_op jit(solution)/shard_map/ppermute | solution.py:471
  71.0 1.9 %collective-permute-done.22.beside = f32[112,128]{1,0:T(8,128)S(1)} collective-permute-done((f32[112,128]{1,0:T(8,128)S(1)}, f32[112,128]{1,0:T(8,128)S(1)}, u32[]{:S(2)}, u32[]{:S(2)}) %collective-permute-start.22) | collective-permute-done | bytes 57376 | tf_op jit(solution)/shard_map/ppermute | solution.py:471
  72.8 0.8 collective-permute-done.21.across
  73.7 2.8 %collective-permute-start.25 = (f32[224,128]{1,0:T(8,128)S(1)}, f32[224,128]{1,0:T(8,128)S(1)}, u32[]{:S(2)}, u32[]{:S(2)}) collective-permute-start(f32[224,128]{1,0:T(8,128)S(1)} %get-tuple-element.66.mid), channel_id=1, source_target_pairs={{0,24},{8,0},{16,8},{24,16},{1,25},{9,1},{17,9},{25,17},{2,26},{10... | collective-permute-start | bytes 344072 | tf_op jit(solution)/shard_map/ppermute | solution.py:454
  76.5 0.0 collective-permute-start.24
  76.5 3.4 %collective-permute-done.25.right = f32[224,128]{1,0:T(8,128)S(1)} collective-permute-done((f32[224,128]{1,0:T(8,128)S(1)}, f32[224,128]{1,0:T(8,128)S(1)}, u32[]{:S(2)}, u32[]{:S(2)}) %collective-permute-start.25) | collective-permute-done | bytes 114720 | tf_op jit(solution)/shard_map/ppermute | solution.py:454
  80.0 1.3 %collective-permute-start.29 = (f32[8,128]{1,0:T(8,128)S(1)}, f32[8,128]{1,0:T(8,128)S(1)}, u32[]{:S(2)}, u32[]{:S(2)}) collective-permute-start(f32[8,128]{1,0:T(8,128)S(1)} %get-tuple-element.72), channel_id=1, source_target_pairs={{0,16},{8,24},{16,0},{24,8},{1,17},{9,25},{17,1},{25,9},{2,18},{10... | collective-permute-start | bytes 12296 | tf_op jit(solution)/shard_map/ppermute | solution.py:454
  81.2 1.3 %stream.5.g = f32[8,8,16,768]{3,2,1,0:T(8,128)S(1)} custom-call(f32[8,8,16,768]{3,2,1,0:T(8,128)S(1)} %get-tuple-element.64.h, f32[8,768]{1,0:T(8,128)S(1)} %get-tuple-element.41.coef, f32[8,8,16,128]{3,2,1,0:T(8,128)S(1)} %get-tuple-element.42.fluid), custom_call_target="tpu_custom_call" | custom-call | tf_op jit(solution)/shard_map/stream/pallas_call | solution.py:225
  82.5 0.6 collective-permute-done.24.left
  83.1 1.1 %macro.5 = (f32[384,128]{1,0:T(8,128)S(1)}, f32[5,8,128]{2,1,0:T(8,128)S(1)}, f32[8,128]{1,0:T(8,128)S(1)}) custom-call(f32[224,128]{1,0:T(8,128)S(1)} %get-tuple-element.66.mid, f32[224,128]{1,0:T(8,128)S(1)} %collective-permute-done.24.left, f32[224,128]{1,0:T(8,128)S(1)} %collective-permute-done.25.right, f32[8,128]{1,0:T(8,128)S(1)} %get-tuple-element.45.fluid, ...), custom_call_target="tpu_custom_call" | custom-call | tf_op jit(solution)/shard_map/macro/pallas_call | solution.py:349
  84.3 0.2 collective-permute-done.29.far
  84.5 0.0 collective-permute-done.27.xbefore
  84.5 3.1 %update.5 = (f32[8,8,16,768]{3,2,1,0:T(8,128)}, f32[320,16]{1,0:T(8,128)}) custom-call(f32[8,128]{1,0:T(8,128)S(1)} %get-tuple-element.39.target, f32[8,8,16,768]{3,2,1,0:T(8,128)S(1)} %stream.5.g, f32[384,128]{1,0:T(8,128)S(1)} %get-tuple-element.67.mix, bf16[144,768]{1,0:T(8,128)(2,1)S(1)} %get-tuple-element.48.wmat, ...), custom_call_target="tpu_custom_call" | custom-call | tf_op jit(solution)/shard_map/update/pallas_call | solution.py:441
  (17 shorter events, 0.1 us)
Async XLA Ops:
  0.6 26.8 %copy-start.1 = (f32[8,8,16]{2,1,0:T(8,128)S(1)}, f32[8,8,16]{2,1,0:T(8,128)}, u32[]{:S(2)}) copy-start(f32[8,8,16]{2,1,0:T(8,128)} %wall_temp.1) | copy-start | bytes 12292
  0.6 26.8 %copy-start = (s32[8,8,16]{2,1,0:T(8,128)S(1)}, s32[8,8,16]{2,1,0:T(8,128)}, u32[]{:S(2)}) copy-start(s32[8,8,16]{2,1,0:T(8,128)} %wall.1) | copy-start | bytes 12292
  5.0 26.8 %collective-permute-start.6 = (f32[8,16,768]{2,1,0:T(8,128)S(1)}, f32[8,16,768]{2,1,0:T(8,128)S(1)}, u32[]{:S(2)}, u32[]{:S(2)}) collective-permute-start(f32[8,16,768]{2,1,0:T(8,128)S(1)} %get-tuple-element.50), channel_id=1, source_target_pairs={{0,4},{4,0},{1,5},{5,1},{2,6},{6,2},{3,7},{7,3},{8,12},{12,8},{9,1... | collective-permute-start | bytes 1179656 | tf_op jit(solution)/shard_map/ppermute | solution.py:454
  8.1 1.2 %collective-permute-start = (f32[112,128]{1,0:T(8,128)S(1)}, f32[112,128]{1,0:T(8,128)S(1)}, u32[]{:S(2)}, u32[]{:S(2)}) collective-permute-start(f32[112,128]{1,0:T(8,128)S(1)} %get-tuple-element.43), channel_id=1, source_target_pairs={{0,1},{1,0},{2,3},{3,2},{4,5},{5,4},{6,7},{7,6},{8,9},{9,8},{10,11... | collective-permute-start | bytes 172040 | tf_op jit(solution)/shard_map/ppermute | solution.py:471
  9.3 6.8 %collective-permute-start.3 = (f32[112,128]{1,0:T(8,128)S(1)}, f32[112,128]{1,0:T(8,128)S(1)}, u32[]{:S(2)}, u32[]{:S(2)}) collective-permute-start(f32[112,128]{1,0:T(8,128)S(1)} %add.9.mom), channel_id=1, source_target_pairs={{0,6},{1,7},{2,4},{3,5},{4,2},{5,3},{6,0},{7,1},{8,14},{9,15},{10,... | collective-permute-start | bytes 172040 | tf_op jit(solution)/shard_map/ppermute | solution.py:471
  10.8 21.0 %collective-permute-start.7 = (f32[8,16,384]{2,1,0:T(8,128)S(1)}, f32[8,16,384]{2,1,0:T(8,128)S(1)}, u32[]{:S(2)}, u32[]{:S(2)}) collective-permute-start(f32[8,16,384]{2,1,0:T(8,128)S(1)} %get-tuple-element.51), channel_id=1, source_target_pairs={{0,8},{8,16},{16,24},{24,0},{1,9},{9,17},{17,25},{25,1},{2,10},{10... | collective-permute-start | bytes 589832 | tf_op jit(solution)/shard_map/ppermute | solution.py:454
  12.4 19.4 %collective-permute-start.8 = (f32[8,16,384]{2,1,0:T(8,128)S(1)}, f32[8,16,384]{2,1,0:T(8,128)S(1)}, u32[]{:S(2)}, u32[]{:S(2)}) collective-permute-start(f32[8,16,384]{2,1,0:T(8,128)S(1)} %get-tuple-element.52), channel_id=1, source_target_pairs={{0,24},{8,0},{16,8},{24,16},{1,25},{9,1},{17,9},{25,17},{2,26},{10... | collective-permute-start | bytes 589832 | tf_op jit(solution)/shard_map/ppermute | solution.py:454
  14.7 5.0 %collective-permute-start.2 = (f32[112,128]{1,0:T(8,128)S(1)}, f32[112,128]{1,0:T(8,128)S(1)}, u32[]{:S(2)}, u32[]{:S(2)}) collective-permute-start(f32[112,128]{1,0:T(8,128)S(1)} %add.9.mom), channel_id=1, source_target_pairs={{0,4},{1,5},{2,6},{3,7},{4,0},{5,1},{6,2},{7,3},{8,12},{9,13},{10,... | collective-permute-start | bytes 172040 | tf_op jit(solution)/shard_map/ppermute | solution.py:471
  16.2 4.2 %collective-permute-start.1 = (f32[112,128]{1,0:T(8,128)S(1)}, f32[112,128]{1,0:T(8,128)S(1)}, u32[]{:S(2)}, u32[]{:S(2)}) collective-permute-start(f32[112,128]{1,0:T(8,128)S(1)} %add.9.mom), channel_id=1, source_target_pairs={{0,2},{1,3},{2,0},{3,1},{4,6},{5,7},{6,4},{7,5},{8,10},{9,11},{10,... | collective-permute-start | bytes 172040 | tf_op jit(solution)/shard_map/ppermute | solution.py:471
  20.4 6.0 %collective-permute-start.5 = (f32[224,128]{1,0:T(8,128)S(1)}, f32[224,128]{1,0:T(8,128)S(1)}, u32[]{:S(2)}, u32[]{:S(2)}) collective-permute-start(f32[224,128]{1,0:T(8,128)S(1)} %get-tuple-element.44.mid), channel_id=1, source_target_pairs={{0,24},{8,0},{16,8},{24,16},{1,25},{9,1},{17,9},{25,17},{2,26},{10... | collective-permute-start | bytes 344072 | tf_op jit(solution)/shard_map/ppermute | solution.py:454
  23.6 6.6 %collective-permute-start.4 = (f32[224,128]{1,0:T(8,128)S(1)}, f32[224,128]{1,0:T(8,128)S(1)}, u32[]{:S(2)}, u32[]{:S(2)}) collective-permute-start(f32[224,128]{1,0:T(8,128)S(1)} %get-tuple-element.44.mid), channel_id=1, source_target_pairs={{0,8},{8,16},{16,24},{24,0},{1,9},{9,17},{17,25},{25,1},{2,10},{10... | collective-permute-start | bytes 344072 | tf_op jit(solution)/shard_map/ppermute | solution.py:454
  26.4 5.5 %collective-permute-start.9 = (f32[8,128]{1,0:T(8,128)S(1)}, f32[8,128]{1,0:T(8,128)S(1)}, u32[]{:S(2)}, u32[]{:S(2)}) collective-permute-start(f32[8,128]{1,0:T(8,128)S(1)} %get-tuple-element.54), channel_id=1, source_target_pairs={{0,16},{8,24},{16,0},{24,8},{1,17},{9,25},{17,1},{25,9},{2,18},{10... | collective-permute-start | bytes 12296 | tf_op jit(solution)/shard_map/ppermute | solution.py:454
  33.8 25.1 %collective-permute-start.16 = (f32[8,16,768]{2,1,0:T(8,128)S(1)}, f32[8,16,768]{2,1,0:T(8,128)S(1)}, u32[]{:S(2)}, u32[]{:S(2)}) collective-permute-start(f32[8,16,768]{2,1,0:T(8,128)S(1)} %get-tuple-element.59), channel_id=1, source_target_pairs={{0,4},{4,0},{1,5},{5,1},{2,6},{6,2},{3,7},{7,3},{8,12},{12,8},{9,1... | collective-permute-start | bytes 1179656 | tf_op jit(solution)/shard_map/ppermute | solution.py:454
  35.4 1.2 %collective-permute-start.10 = (f32[112,128]{1,0:T(8,128)S(1)}, f32[112,128]{1,0:T(8,128)S(1)}, u32[]{:S(2)}, u32[]{:S(2)}) collective-permute-start(f32[112,128]{1,0:T(8,128)S(1)} %get-tuple-element.56), channel_id=1, source_target_pairs={{0,1},{1,0},{2,3},{3,2},{4,5},{5,4},{6,7},{7,6},{8,9},{9,8},{10,11... | collective-permute-start | bytes 172040 | tf_op jit(solution)/shard_map/ppermute | solution.py:471
  36.6 6.8 %collective-permute-start.13 = (f32[112,128]{1,0:T(8,128)S(1)}, f32[112,128]{1,0:T(8,128)S(1)}, u32[]{:S(2)}, u32[]{:S(2)}) collective-permute-start(f32[112,128]{1,0:T(8,128)S(1)} %add.10.mom), channel_id=1, source_target_pairs={{0,6},{1,7},{2,4},{3,5},{4,2},{5,3},{6,0},{7,1},{8,14},{9,15},{10,... | collective-permute-start | bytes 172040 | tf_op jit(solution)/shard_map/ppermute | solution.py:471
  38.1 20.8 %collective-permute-start.17 = (f32[8,16,384]{2,1,0:T(8,128)S(1)}, f32[8,16,384]{2,1,0:T(8,128)S(1)}, u32[]{:S(2)}, u32[]{:S(2)}) collective-permute-start(f32[8,16,384]{2,1,0:T(8,128)S(1)} %get-tuple-element.60), channel_id=1, source_target_pairs={{0,8},{8,16},{16,24},{24,0},{1,9},{9,17},{17,25},{25,1},{2,10},{10... | collective-permute-start | bytes 589832 | tf_op jit(solution)/shard_map/ppermute | solution.py:454
  41.6 17.3 %collective-permute-start.18 = (f32[8,16,384]{2,1,0:T(8,128)S(1)}, f32[8,16,384]{2,1,0:T(8,128)S(1)}, u32[]{:S(2)}, u32[]{:S(2)}) collective-permute-start(f32[8,16,384]{2,1,0:T(8,128)S(1)} %get-tuple-element.61), channel_id=1, source_target_pairs={{0,24},{8,0},{16,8},{24,16},{1,25},{9,1},{17,9},{25,17},{2,26},{10... | collective-permute-start | bytes 589832 | tf_op jit(solution)/shard_map/ppermute | solution.py:454
  41.9 4.2 %collective-permute-start.12 = (f32[112,128]{1,0:T(8,128)S(1)}, f32[112,128]{1,0:T(8,128)S(1)}, u32[]{:S(2)}, u32[]{:S(2)}) collective-permute-start(f32[112,128]{1,0:T(8,128)S(1)} %add.10.mom), channel_id=1, source_target_pairs={{0,4},{1,5},{2,6},{3,7},{4,0},{5,1},{6,2},{7,3},{8,12},{9,13},{10,... | collective-permute-start | bytes 172040 | tf_op jit(solution)/shard_map/ppermute | solution.py:471
  43.5 4.2 %collective-permute-start.11 = (f32[112,128]{1,0:T(8,128)S(1)}, f32[112,128]{1,0:T(8,128)S(1)}, u32[]{:S(2)}, u32[]{:S(2)}) collective-permute-start(f32[112,128]{1,0:T(8,128)S(1)} %add.10.mom), channel_id=1, source_target_pairs={{0,2},{1,3},{2,0},{3,1},{4,6},{5,7},{6,4},{7,5},{8,10},{9,11},{10,... | collective-permute-start | bytes 172040 | tf_op jit(solution)/shard_map/ppermute | solution.py:471
  47.7 6.7 %collective-permute-start.15 = (f32[224,128]{1,0:T(8,128)S(1)}, f32[224,128]{1,0:T(8,128)S(1)}, u32[]{:S(2)}, u32[]{:S(2)}) collective-permute-start(f32[224,128]{1,0:T(8,128)S(1)} %get-tuple-element.57.mid), channel_id=1, source_target_pairs={{0,24},{8,0},{16,8},{24,16},{1,25},{9,1},{17,9},{25,17},{2,26},{10... | collective-permute-start | bytes 344072 | tf_op jit(solution)/shard_map/ppermute | solution.py:454
  49.3 7.0 %collective-permute-start.14 = (f32[224,128]{1,0:T(8,128)S(1)}, f32[224,128]{1,0:T(8,128)S(1)}, u32[]{:S(2)}, u32[]{:S(2)}) collective-permute-start(f32[224,128]{1,0:T(8,128)S(1)} %get-tuple-element.57.mid), channel_id=1, source_target_pairs={{0,8},{8,16},{16,24},{24,0},{1,9},{9,17},{17,25},{25,1},{2,10},{10... | collective-permute-start | bytes 344072 | tf_op jit(solution)/shard_map/ppermute | solution.py:454
  54.4 4.5 %collective-permute-start.19 = (f32[8,128]{1,0:T(8,128)S(1)}, f32[8,128]{1,0:T(8,128)S(1)}, u32[]{:S(2)}, u32[]{:S(2)}) collective-permute-start(f32[8,128]{1,0:T(8,128)S(1)} %get-tuple-element.63), channel_id=1, source_target_pairs={{0,16},{8,24},{16,0},{24,8},{1,17},{9,25},{17,1},{25,9},{2,18},{10... | collective-permute-start | bytes 12296 | tf_op jit(solution)/shard_map/ppermute | solution.py:454
  60.8 23.7 %collective-permute-start.26 = (f32[8,16,768]{2,1,0:T(8,128)S(1)}, f32[8,16,768]{2,1,0:T(8,128)S(1)}, u32[]{:S(2)}, u32[]{:S(2)}) collective-permute-start(f32[8,16,768]{2,1,0:T(8,128)S(1)} %get-tuple-element.68), channel_id=1, source_target_pairs={{0,4},{4,0},{1,5},{5,1},{2,6},{6,2},{3,7},{7,3},{8,12},{12,8},{9,1... | collective-permute-start | bytes 1179656 | tf_op jit(solution)/shard_map/ppermute | solution.py:454
  62.3 1.2 %collective-permute-start.20 = (f32[112,128]{1,0:T(8,128)S(1)}, f32[112,128]{1,0:T(8,128)S(1)}, u32[]{:S(2)}, u32[]{:S(2)}) collective-permute-start(f32[112,128]{1,0:T(8,128)S(1)} %get-tuple-element.65), channel_id=1, source_target_pairs={{0,1},{1,0},{2,3},{3,2},{4,5},{5,4},{6,7},{7,6},{8,9},{9,8},{10,11... | collective-permute-start | bytes 172040 | tf_op jit(solution)/shard_map/ppermute | solution.py:471
  63.6 5.9 %collective-permute-start.23 = (f32[112,128]{1,0:T(8,128)S(1)}, f32[112,128]{1,0:T(8,128)S(1)}, u32[]{:S(2)}, u32[]{:S(2)}) collective-permute-start(f32[112,128]{1,0:T(8,128)S(1)} %add.11.mom), channel_id=1, source_target_pairs={{0,6},{1,7},{2,4},{3,5},{4,2},{5,3},{6,0},{7,1},{8,14},{9,15},{10,... | collective-permute-start | bytes 172040 | tf_op jit(solution)/shard_map/ppermute | solution.py:471
  63.9 20.6 %collective-permute-start.27 = (f32[8,16,384]{2,1,0:T(8,128)S(1)}, f32[8,16,384]{2,1,0:T(8,128)S(1)}, u32[]{:S(2)}, u32[]{:S(2)}) collective-permute-start(f32[8,16,384]{2,1,0:T(8,128)S(1)} %get-tuple-element.69), channel_id=1, source_target_pairs={{0,8},{8,16},{16,24},{24,0},{1,9},{9,17},{17,25},{25,1},{2,10},{10... | collective-permute-start | bytes 589832 | tf_op jit(solution)/shard_map/ppermute | solution.py:454
  66.9 17.6 %collective-permute-start.28 = (f32[8,16,384]{2,1,0:T(8,128)S(1)}, f32[8,16,384]{2,1,0:T(8,128)S(1)}, u32[]{:S(2)}, u32[]{:S(2)}) collective-permute-start(f32[8,16,384]{2,1,0:T(8,128)S(1)} %get-tuple-element.70), channel_id=1, source_target_pairs={{0,24},{8,0},{16,8},{24,16},{1,25},{9,1},{17,9},{25,17},{2,26},{10... | collective-permute-start | bytes 589832 | tf_op jit(solution)/shard_map/ppermute | solution.py:454
  67.8 5.0 %collective-permute-start.22 = (f32[112,128]{1,0:T(8,128)S(1)}, f32[112,128]{1,0:T(8,128)S(1)}, u32[]{:S(2)}, u32[]{:S(2)}) collective-permute-start(f32[112,128]{1,0:T(8,128)S(1)} %add.11.mom), channel_id=1, source_target_pairs={{0,4},{1,5},{2,6},{3,7},{4,0},{5,1},{6,2},{7,3},{8,12},{9,13},{10,... | collective-permute-start | bytes 172040 | tf_op jit(solution)/shard_map/ppermute | solution.py:471
  69.5 4.2 %collective-permute-start.21 = (f32[112,128]{1,0:T(8,128)S(1)}, f32[112,128]{1,0:T(8,128)S(1)}, u32[]{:S(2)}, u32[]{:S(2)}) collective-permute-start(f32[112,128]{1,0:T(8,128)S(1)} %add.11.mom), channel_id=1, source_target_pairs={{0,2},{1,3},{2,0},{3,1},{4,6},{5,7},{6,4},{7,5},{8,10},{9,11},{10,... | collective-permute-start | bytes 172040 | tf_op jit(solution)/shard_map/ppermute | solution.py:471
  73.7 6.3 %collective-permute-start.25 = (f32[224,128]{1,0:T(8,128)S(1)}, f32[224,128]{1,0:T(8,128)S(1)}, u32[]{:S(2)}, u32[]{:S(2)}) collective-permute-start(f32[224,128]{1,0:T(8,128)S(1)} %get-tuple-element.66.mid), channel_id=1, source_target_pairs={{0,24},{8,0},{16,8},{24,16},{1,25},{9,1},{17,9},{25,17},{2,26},{10... | collective-permute-start | bytes 344072 | tf_op jit(solution)/shard_map/ppermute | solution.py:454
  76.5 6.6 %collective-permute-start.24 = (f32[224,128]{1,0:T(8,128)S(1)}, f32[224,128]{1,0:T(8,128)S(1)}, u32[]{:S(2)}, u32[]{:S(2)}) collective-permute-start(f32[224,128]{1,0:T(8,128)S(1)} %get-tuple-element.66.mid), channel_id=1, source_target_pairs={{0,8},{8,16},{16,24},{24,0},{1,9},{9,17},{17,25},{25,1},{2,10},{10... | collective-permute-start | bytes 344072 | tf_op jit(solution)/shard_map/ppermute | solution.py:454
  80.0 4.5 %collective-permute-start.29 = (f32[8,128]{1,0:T(8,128)S(1)}, f32[8,128]{1,0:T(8,128)S(1)}, u32[]{:S(2)}, u32[]{:S(2)}) collective-permute-start(f32[8,128]{1,0:T(8,128)S(1)} %get-tuple-element.72), channel_id=1, source_target_pairs={{0,16},{8,24},{16,0},{24,8},{1,17},{9,25},{17,1},{25,9},{2,18},{10... | collective-permute-start | bytes 12296 | tf_op jit(solution)/shard_map/ppermute | solution.py:454

commit v4 on v3

--- a/solution.py
+++ b/solution.py
@@ -10,6 +10,7 @@
 
 ITERS = 3
 MACRO_STEPS = 4
+REACH = MACRO_STEPS + 1
 
 STEP_TIME = 0.1
 COLLISION = 1.0
@@ -230,14 +231,21 @@
     )(h, coef, fluid)
 
 
-def join_kernel(mom, across, beside, corner, both, mass):
+def join_kernel(mom, across, beside, corner, both, mass, ahead, behind):
     rows = mom.shape[0]
     nx = mass.shape[0]
     own = mom[...] + across[...]
     side = beside[...] + corner[...]
     both[0:rows, :] = own
     both[rows:, :] = side
-    mass[...] = own[0:nx] + side[0:nx]
+    sums = own[0:nx] + side[0:nx]
+    mass[...] = sums
+    comps = 2 * MOMENTS
+    for r in range(REACH):
+        ahead[r * comps : (r + 1) * comps, :] = both[pl.ds(nx - REACH + r, comps, stride=nx), :]
+        behind[r * comps : (r + 1) * comps, :] = both[pl.ds(r, comps, stride=nx), :]
+    ahead[REACH * comps :, :] = sums
+    behind[REACH * comps :, :] = sums
 
 
 def join(mom, across, beside, corner, nx):
@@ -247,6 +255,8 @@
         out_shape=[
             jax.ShapeDtypeStruct((2 * rows, width), f32),
             jax.ShapeDtypeStruct((nx, width), f32),
+            jax.ShapeDtypeStruct((2 * MOMENTS * REACH + nx, width), f32),
+            jax.ShapeDtypeStruct((2 * MOMENTS * REACH + nx, width), f32),
         ],
         name="join",
         compiler_params=pltpu.CompilerParams(vmem_limit_bytes=4 << 20),
@@ -255,12 +265,13 @@
 
 def macro_kernel(mid, left, right, fluid, heat, mix, state_out, mass_out, *, nz):
     nx, width = fluid.shape
+    blank = jnp.zeros((nx - REACH, width), f32)
 
     def field(k):
         halves = []
-        for start in (k * nx, (MOMENTS + k) * nx):
-            part = slice(start, start + nx)
-            halves.append(jnp.concatenate([left[part], mid[part], right[part]], axis=0))
+        for c in (k, MOMENTS + k):
+            near = pl.ds(c, REACH, stride=2 * MOMENTS)
+            halves.append(jnp.concatenate([blank, left[near, :], mid[c * nx : (c + 1) * nx], right[near, :], blank], axis=0))
         return jnp.concatenate(halves, axis=1)
 
     rows, lanes = 3 * nx, 2 * width
@@ -316,10 +327,8 @@
         rates.append(-(2.0 / 3.0) * div + 2.0 / 3.0 * CONDUCTION * laplace(state[4], near[4]) + sources[3])
         state = [s + MACRO_TIME * r for s, r in zip(state, rates)]
 
-    mass = None
-    for part in (mid, left, right):
-        for start in (0, MOMENTS * nx):
-            mass = part[start : start + nx] if mass is None else mass + part[start : start + nx]
+    edge = 2 * MOMENTS * REACH
+    mass = mid[0:nx] + mid[MOMENTS * nx : (MOMENTS + 1) * nx] + left[edge:] + right[edge:]
     mass_out[...] = mass
     is_fluid = fluid[...]
 
@@ -371,11 +380,6 @@
     offset = target[0:1, 0:1] - total / cells
     is_offset = lax.broadcasted_iota(jnp.int32, (KROWS, ny * nz), 0) == 40
     scale = jnp.where(is_offset, jnp.broadcast_to(offset, (KROWS, ny * nz)), 1.0)
-    if last:
-        for k in range(5):
-            value = state[k] + jnp.broadcast_to(offset, (nx, ny * nz)) if k == 0 else state[k]
-            for y in range(ny):
-                fields[pl.ds(k * nx * ny + y, nx, stride=ny), :] = value[:, y * nz : (y + 1) * nz]
     along_x, along_y = coef[1:2, :], coef[2:3, :]
     upward = coef[4:5, :] > 0.0
     first_y = jnp.where(upward, along_y, 0.0)
@@ -417,6 +421,10 @@
                 xdown[...] = h[x, :, :, half:]
     if last:
         copies[nx - 1].start()
+        for k in range(5):
+            value = state[k] + jnp.broadcast_to(offset, (nx, ny * nz)) if k == 0 else state[k]
+            for y in range(ny):
+                fields[pl.ds(k * nx * ny + y, nx, stride=ny), :] = value[:, y * nz : (y + 1) * nz]
         for copy in copies:
             copy.wait()
 
@@ -485,9 +493,9 @@
         yhalo = ring(ysend, "ty", 1)
         xbefore = ring(xup, "tx", 1)
         xafter = ring(xdown, "tx", -1)
-        both, sums = join(mom, across, beside, corner, nx)
-        left = ring(both, "tx", 1)
-        right = ring(both, "tx", -1)
+        both, sums, ahead, behind = join(mom, across, beside, corner, nx)
+        left = ring(ahead, "tx", 1)
+        right = ring(behind, "tx", -1)
         far = None
         for d in range(2, n_tx - 1):
             part = ring(sums, "tx", d)

time: 88 us -> 90 us (1.023)
  starting transfers between devices: 39.3 us -> 41.8 us
    ppermute x12, starting transfers between devices: 10.6 us -> 13.2 us  [plane_pair(): return lax.ppermute(value, ('ty', 'vel'), pairs)]
    ppermute x18, waiting for transfers between devices: 12.8 us -> 11.1 us  [ring(): lax.ppermute(value, axis, [(i, (i + step) % count) for i in range(count)])]
    ppermute x12, waiting for transfers between devices: 13.7 us -> 14.8 us  [plane_pair(): return lax.ppermute(value, ('ty', 'vel'), pairs)]
  transfers between devices with their start and end apart: 30 -> 30, of which waited for: 16 -> 13; matrix products, arithmetic and copies ran while one was open for 0% -> 0% of each run, Pallas kernels for 11% -> 11%
where the time goes in v4:
time: 90 us; the launch traced here: 89.7 us
  starting transfers between devices  41.8 us (46%)
  waiting for transfers between devices  26 us (29%)
  Pallas kernels  20.3 us (23%)
  between operations  1.59 us (2%)
    ppermute x18, starting transfers between devices, ring(): lax.ppermute(value, axis, [(i, (i + step) % count) for i in range(count)])  28.6 us
    ppermute x12, waiting for transfers between devices, plane_pair(): return lax.ppermute(value, ('ty', 'vel'), pairs)  14.8 us
    ppermute x12, starting transfers between devices, plane_pair(): return lax.ppermute(value, ('ty', 'vel'), pairs)  13.2 us
    ppermute x18, waiting for transfers between devices, ring(): lax.ppermute(value, axis, [(i, (i + step) % count) for i in range(count)])  11.1 us
    pallas_call x3, Pallas kernels, update(): pl.pallas_call(functools.partial(update_kernel, last=last, cells=cells),...  6.96 us
    pallas_call x3, Pallas kernels, macro(): pl.pallas_call(functools.partial(macro_kernel, nz=nz), out_shape=[jax.Sha...  4.41 us
    pallas_call x3, Pallas kernels, stream(): pl.pallas_call(stream_kernel, out_shape=jax.ShapeDtypeStruct(h.shape, f32...  4.01 us
    pallas_call x1, Pallas kernels, prepare(): pl.pallas_call(functools.partial(prepare_kernel, total=total), in_specs=[...  3.72 us
  transfers between devices with their start and end apart: 30, of which 13 were waited for; matrix products, arithmetic and copies ran while one was open for 0% of the time, Pallas kernels for 11%

profile of v4, /device:TPU:0, one launch (start us, length us, event | category | flops | bytes accessed | tf_op | source)
XLA Modules:
  0.0 89.7 jit_solution(17362152646351448269)
XLA Ops:
  1.3 3.7 %prepare.1 = (f32[8,8,16,768]{3,2,1,0:T(8,128)S(1)}, f32[112,128]{1,0:T(8,128)S(1)}, bf16[32,768]{1,0:T(8,128)(2,1)S(1)}, bf16[144,768]{1,0:T(8,128)(2,1)S(1)}, ...) custom-call(f32[3,768]{1,0:T(4,128)} %vel_far.1, ...), custom_call_target="tpu_custom_call" | custom-call | tf_op jit(solution)/shard_map/prepare/pallas_call | solution.py:131
  5.0 3.1 %collective-permute-start.6 = (f32[8,16,768]{2,1,0:T(8,128)S(1)}, f32[8,16,768]{2,1,0:T(8,128)S(1)}, u32[]{:S(2)}, u32[]{:S(2)}) collective-permute-start(f32[8,16,768]{2,1,0:T(8,128)S(1)} %get-tuple-element.58), channel_id=1, source_target_pairs={{0,4},{4,0},{1,5},{5,1},{2,6},{6,2},{3,7},{7,3},{8,12},{12,8},{9,1... | collective-permute-start | bytes 1179656 | tf_op jit(solution)/shard_map/ppermute | solution.py:462
  8.1 0.0 collective-permute-start
  8.1 1.6 %collective-permute-start.7 = (f32[8,16,384]{2,1,0:T(8,128)S(1)}, f32[8,16,384]{2,1,0:T(8,128)S(1)}, u32[]{:S(2)}, u32[]{:S(2)}) collective-permute-start(f32[8,16,384]{2,1,0:T(8,128)S(1)} %get-tuple-element.59), channel_id=1, source_target_pairs={{0,8},{8,16},{16,24},{24,0},{1,9},{9,17},{17,25},{25,1},{2,10},{10... | collective-permute-start | bytes 589832 | tf_op jit(solution)/shard_map/ppermute | solution.py:462
  9.7 2.2 %collective-permute-start.8 = (f32[8,16,384]{2,1,0:T(8,128)S(1)}, f32[8,16,384]{2,1,0:T(8,128)S(1)}, u32[]{:S(2)}, u32[]{:S(2)}) collective-permute-start(f32[8,16,384]{2,1,0:T(8,128)S(1)} %get-tuple-element.60), channel_id=1, source_target_pairs={{0,24},{8,0},{16,8},{24,16},{1,25},{9,1},{17,9},{25,17},{2,26},{10... | collective-permute-start | bytes 589832 | tf_op jit(solution)/shard_map/ppermute | solution.py:462
  11.9 0.0 collective-permute-done
  11.9 1.5 %collective-permute-start.3 = (f32[112,128]{1,0:T(8,128)S(1)}, f32[112,128]{1,0:T(8,128)S(1)}, u32[]{:S(2)}, u32[]{:S(2)}) collective-permute-start(f32[112,128]{1,0:T(8,128)S(1)} %add.9.mom), channel_id=1, source_target_pairs={{0,6},{1,7},{2,4},{3,5},{4,2},{5,3},{6,0},{7,1},{8,14},{9,15},{10,... | collective-permute-start | bytes 172040 | tf_op jit(solution)/shard_map/ppermute | solution.py:479
  13.4 1.5 %collective-permute-start.2 = (f32[112,128]{1,0:T(8,128)S(1)}, f32[112,128]{1,0:T(8,128)S(1)}, u32[]{:S(2)}, u32[]{:S(2)}) collective-permute-start(f32[112,128]{1,0:T(8,128)S(1)} %add.9.mom), channel_id=1, source_target_pairs={{0,4},{1,5},{2,6},{3,7},{4,0},{5,1},{6,2},{7,3},{8,12},{9,13},{10,... | collective-permute-start | bytes 172040 | tf_op jit(solution)/shard_map/ppermute | solution.py:479
  15.0 2.1 %collective-permute-done.3.corner = f32[112,128]{1,0:T(8,128)S(1)} collective-permute-done((f32[112,128]{1,0:T(8,128)S(1)}, f32[112,128]{1,0:T(8,128)S(1)}, u32[]{:S(2)}, u32[]{:S(2)}) %collective-permute-start.3) | collective-permute-done | bytes 57376 | tf_op jit(solution)/shard_map/ppermute | solution.py:479
  17.1 1.5 %collective-permute-start.1 = (f32[112,128]{1,0:T(8,128)S(1)}, f32[112,128]{1,0:T(8,128)S(1)}, u32[]{:S(2)}, u32[]{:S(2)}) collective-permute-start(f32[112,128]{1,0:T(8,128)S(1)} %add.9.mom), channel_id=1, source_target_pairs={{0,2},{1,3},{2,0},{3,1},{4,6},{5,7},{6,4},{7,5},{8,10},{9,11},{10,... | collective-permute-start | bytes 172040 | tf_op jit(solution)/shard_map/ppermute | solution.py:479
  18.6 1.1 %collective-permute-done.2.beside = f32[112,128]{1,0:T(8,128)S(1)} collective-permute-done((f32[112,128]{1,0:T(8,128)S(1)}, f32[112,128]{1,0:T(8,128)S(1)}, u32[]{:S(2)}, u32[]{:S(2)}) %collective-permute-start.2) | collective-permute-done | bytes 57376 | tf_op jit(solution)/shard_map/ppermute | solution.py:479
  19.7 1.6 %collective-permute-done.1.across = f32[112,128]{1,0:T(8,128)S(1)} collective-permute-done((f32[112,128]{1,0:T(8,128)S(1)}, f32[112,128]{1,0:T(8,128)S(1)}, u32[]{:S(2)}, u32[]{:S(2)}) %collective-permute-start.1) | collective-permute-done | bytes 57376 | tf_op jit(solution)/shard_map/ppermute | solution.py:479
  21.3 0.3 collective-permute-start.4
  21.6 3.6 %collective-permute-start.5 = (f32[148,128]{1,0:T(8,128)S(1)}, f32[148,128]{1,0:T(8,128)S(1)}, u32[]{:S(2)}, u32[]{:S(2)}) collective-permute-start(f32[148,128]{1,0:T(8,128)S(1)} %get-tuple-element.52), channel_id=1, source_target_pairs={{0,24},{8,0},{16,8},{24,16},{1,25},{9,1},{17,9},{25,17},{2,26},{10... | collective-permute-start | bytes 227336 | tf_op jit(solution)/shard_map/ppermute | solution.py:462
  25.2 2.5 %collective-permute-done.4.left = f32[148,128]{1,0:T(8,128)S(1)} collective-permute-done((f32[148,128]{1,0:T(8,128)S(1)}, f32[148,128]{1,0:T(8,128)S(1)}, u32[]{:S(2)}, u32[]{:S(2)}) %collective-permute-start.4) | collective-permute-done | bytes 75808 | tf_op jit(solution)/shard_map/ppermute | solution.py:462
  27.7 0.1 collective-permute-start.9
  27.8 1.1 %walls.1 = (f32[8,128]{1,0:T(8,128)S(1)}, f32[8,128]{1,0:T(8,128)S(1)}, f32[8,8,16,128]{3,2,1,0:T(8,128)S(1)}) custom-call(s32[8,8,16]{2,1,0:T(8,128)S(1)} %copy-done, f32[8,8,16]{2,1,0:T(8,128)S(1)} %copy-done.1), custom_call_target="tpu_custom_call" | custom-call | tf_op jit(solution)/shard_map/walls/pallas_call | solution.py:174
  28.9 1.3 %stream.3.g = f32[8,8,16,768]{3,2,1,0:T(8,128)S(1)} custom-call(f32[8,8,16,768]{3,2,1,0:T(8,128)S(1)} %get-tuple-element.46.h, f32[8,768]{1,0:T(8,128)S(1)} %get-tuple-element.47.coef, f32[8,8,16,128]{3,2,1,0:T(8,128)S(1)} %get-tuple-element.48.fluid), custom_call_target="tpu_custom_call" | custom-call | tf_op jit(solution)/shard_map/stream/pallas_call | solution.py:226
  30.3 0.0 collective-permute-done.5.right
  30.3 1.6 %macro.3 = (f32[384,128]{1,0:T(8,128)S(1)}, f32[5,8,128]{2,1,0:T(8,128)}, f32[8,128]{1,0:T(8,128)S(1)}) custom-call(f32[224,128]{1,0:T(8,128)S(1)} %get-tuple-element.50.mid, f32[148,128]{1,0:T(8,128)S(1)} %collective-permute-done.4.left, f32[148,128]{1,0:T(8,128)S(1)} %collective-permute-done.5.right, f32[8,128]{1,0:T(8,128)S(1)} %get-tuple-element.53.fluid, ...), custom_call_target="tpu_custom_call" | custom-call | tf_op jit(solution)/shard_map/macro/pallas_call | solution.py:358
  31.9 0.3 collective-permute-done.9.far
  32.2 0.0 collective-permute-done.7.xbefore
  32.2 0.0 collective-permute-done.8.xafter
  32.2 0.0 collective-permute-done.6.yhalo
  32.2 1.9 %update.3 = (f32[8,8,16,768]{3,2,1,0:T(8,128)S(1)}, f32[112,128]{1,0:T(8,128)S(1)}, f32[8,16,768]{2,1,0:T(8,128)S(1)}, f32[8,16,384]{2,1,0:T(8,128)S(1)}, f32[8,16,384]{2,1,0:T(8,128)S(1)}) custom-call(f32[8,128]{1,0:T(8,128)S(1)} %get-tuple-element.45.target, f32[8,8,16,768]{3,2,1,0:T(8,128)S(1)} %stream.3.g, f32[384,128]{1,0:T(8,128)S(1)} %get-tuple-element.55.mix, ...), custom_call_target="tpu_custom_call" | custom-call | tf_op jit(solution)/shard_map/update/pallas_call | solution.py:449
  34.1 1.2 %collective-permute-start.16 = (f32[8,16,768]{2,1,0:T(8,128)S(1)}, f32[8,16,768]{2,1,0:T(8,128)S(1)}, u32[]{:S(2)}, u32[]{:S(2)}) collective-permute-start(f32[8,16,768]{2,1,0:T(8,128)S(1)} %get-tuple-element.69), channel_id=1, source_target_pairs={{0,4},{4,0},{1,5},{5,1},{2,6},{6,2},{3,7},{7,3},{8,12},{12,8},{9,1... | collective-permute-start | bytes 1179656 | tf_op jit(solution)/shard_map/ppermute | solution.py:462
  35.4 0.0 collective-permute-start.10
  35.4 1.5 %collective-permute-start.17 = (f32[8,16,384]{2,1,0:T(8,128)S(1)}, f32[8,16,384]{2,1,0:T(8,128)S(1)}, u32[]{:S(2)}, u32[]{:S(2)}) collective-permute-start(f32[8,16,384]{2,1,0:T(8,128)S(1)} %get-tuple-element.70), channel_id=1, source_target_pairs={{0,8},{8,16},{16,24},{24,0},{1,9},{9,17},{17,25},{25,1},{2,10},{10... | collective-permute-start | bytes 589832 | tf_op jit(solution)/shard_map/ppermute | solution.py:462
  36.9 2.3 %collective-permute-start.18 = (f32[8,16,384]{2,1,0:T(8,128)S(1)}, f32[8,16,384]{2,1,0:T(8,128)S(1)}, u32[]{:S(2)}, u32[]{:S(2)}) collective-permute-start(f32[8,16,384]{2,1,0:T(8,128)S(1)} %get-tuple-element.71), channel_id=1, source_target_pairs={{0,24},{8,0},{16,8},{24,16},{1,25},{9,1},{17,9},{25,17},{2,26},{10... | collective-permute-start | bytes 589832 | tf_op jit(solution)/shard_map/ppermute | solution.py:462
  39.2 0.0 collective-permute-done.10
  39.2 1.8 %collective-permute-start.13 = (f32[112,128]{1,0:T(8,128)S(1)}, f32[112,128]{1,0:T(8,128)S(1)}, u32[]{:S(2)}, u32[]{:S(2)}) collective-permute-start(f32[112,128]{1,0:T(8,128)S(1)} %add.10.mom), channel_id=1, source_target_pairs={{0,6},{1,7},{2,4},{3,5},{4,2},{5,3},{6,0},{7,1},{8,14},{9,15},{10,... | collective-permute-start | bytes 172040 | tf_op jit(solution)/shard_map/ppermute | solution.py:479
  41.0 1.2 %collective-permute-start.12 = (f32[112,128]{1,0:T(8,128)S(1)}, f32[112,128]{1,0:T(8,128)S(1)}, u32[]{:S(2)}, u32[]{:S(2)}) collective-permute-start(f32[112,128]{1,0:T(8,128)S(1)} %add.10.mom), channel_id=1, source_target_pairs={{0,4},{1,5},{2,6},{3,7},{4,0},{5,1},{6,2},{7,3},{8,12},{9,13},{10,... | collective-permute-start | bytes 172040 | tf_op jit(solution)/shard_map/ppermute | solution.py:479
  42.3 2.1 %collective-permute-done.13.corner = f32[112,128]{1,0:T(8,128)S(1)} collective-permute-done((f32[112,128]{1,0:T(8,128)S(1)}, f32[112,128]{1,0:T(8,128)S(1)}, u32[]{:S(2)}, u32[]{:S(2)}) %collective-permute-start.13) | collective-permute-done | bytes 57376 | tf_op jit(solution)/shard_map/ppermute | solution.py:479
  44.4 1.5 %collective-permute-start.11 = (f32[112,128]{1,0:T(8,128)S(1)}, f32[112,128]{1,0:T(8,128)S(1)}, u32[]{:S(2)}, u32[]{:S(2)}) collective-permute-start(f32[112,128]{1,0:T(8,128)S(1)} %add.10.mom), channel_id=1, source_target_pairs={{0,2},{1,3},{2,0},{3,1},{4,6},{5,7},{6,4},{7,5},{8,10},{9,11},{10,... | collective-permute-start | bytes 172040 | tf_op jit(solution)/shard_map/ppermute | solution.py:479
  45.9 0.0 collective-permute-done.12.beside
  45.9 2.7 %collective-permute-done.11.across = f32[112,128]{1,0:T(8,128)S(1)} collective-permute-done((f32[112,128]{1,0:T(8,128)S(1)}, f32[112,128]{1,0:T(8,128)S(1)}, u32[]{:S(2)}, u32[]{:S(2)}) %collective-permute-start.11) | collective-permute-done | bytes 57376 | tf_op jit(solution)/shard_map/ppermute | solution.py:479
  48.6 0.1 collective-permute-start.14
  48.7 3.8 %collective-permute-start.15 = (f32[148,128]{1,0:T(8,128)S(1)}, f32[148,128]{1,0:T(8,128)S(1)}, u32[]{:S(2)}, u32[]{:S(2)}) collective-permute-start(f32[148,128]{1,0:T(8,128)S(1)} %get-tuple-element.67), channel_id=1, source_target_pairs={{0,24},{8,0},{16,8},{24,16},{1,25},{9,1},{17,9},{25,17},{2,26},{10... | collective-permute-start | bytes 227336 | tf_op jit(solution)/shard_map/ppermute | solution.py:462
  52.5 2.4 %collective-permute-done.14.left = f32[148,128]{1,0:T(8,128)S(1)} collective-permute-done((f32[148,128]{1,0:T(8,128)S(1)}, f32[148,128]{1,0:T(8,128)S(1)}, u32[]{:S(2)}, u32[]{:S(2)}) %collective-permute-start.14) | collective-permute-done | bytes 75808 | tf_op jit(solution)/shard_map/ppermute | solution.py:462
  54.9 0.0 collective-permute-start.19
  54.9 1.3 %stream.4.g = f32[8,8,16,768]{3,2,1,0:T(8,128)S(1)} custom-call(f32[8,8,16,768]{3,2,1,0:T(8,128)S(1)} %get-tuple-element.63.h, f32[8,768]{1,0:T(8,128)S(1)} %get-tuple-element.47.coef, f32[8,8,16,128]{3,2,1,0:T(8,128)S(1)} %get-tuple-element.48.fluid), custom_call_target="tpu_custom_call" | custom-call | tf_op jit(solution)/shard_map/stream/pallas_call | solution.py:226
  56.2 0.0 collective-permute-done.15.right
  56.2 1.6 %macro.4 = (f32[384,128]{1,0:T(8,128)S(1)}, f32[5,8,128]{2,1,0:T(8,128)}, f32[8,128]{1,0:T(8,128)S(1)}) custom-call(f32[224,128]{1,0:T(8,128)S(1)} %get-tuple-element.65.mid, f32[148,128]{1,0:T(8,128)S(1)} %collective-permute-done.14.left, f32[148,128]{1,0:T(8,128)S(1)} %collective-permute-done.15.right, f32[8,128]{1,0:T(8,128)S(1)} %get-tuple-element.53.fluid, ...), custom_call_target="tpu_custom_call" | custom-call | tf_op jit(solution)/shard_map/macro/pallas_call | solution.py:358
  57.9 1.5 %collective-permute-done.19.far = f32[8,128]{1,0:T(8,128)S(1)} collective-permute-done((f32[8,128]{1,0:T(8,128)S(1)}, f32[8,128]{1,0:T(8,128)S(1)}, u32[]{:S(2)}, u32[]{:S(2)}) %collective-permute-start.19) | collective-permute-done | bytes 4128 | tf_op jit(solution)/shard_map/ppermute | solution.py:462
  59.4 0.0 collective-permute-done.16.yhalo
  59.4 1.9 %update.4 = (f32[8,8,16,768]{3,2,1,0:T(8,128)S(1)}, f32[112,128]{1,0:T(8,128)S(1)}, f32[8,16,768]{2,1,0:T(8,128)S(1)}, f32[8,16,384]{2,1,0:T(8,128)S(1)}, f32[8,16,384]{2,1,0:T(8,128)S(1)}) custom-call(f32[8,128]{1,0:T(8,128)S(1)} %get-tuple-element.45.target, f32[8,8,16,768]{3,2,1,0:T(8,128)S(1)} %stream.4.g, f32[384,128]{1,0:T(8,128)S(1)} %get-tuple-element.68.mix, ...), custom_call_target="tpu_custom_call" | custom-call | tf_op jit(solution)/shard_map/update/pallas_call | solution.py:449
  61.3 0.9 %collective-permute-start.26 = (f32[8,16,768]{2,1,0:T(8,128)S(1)}, f32[8,16,768]{2,1,0:T(8,128)S(1)}, u32[]{:S(2)}, u32[]{:S(2)}) collective-permute-start(f32[8,16,768]{2,1,0:T(8,128)S(1)} %get-tuple-element.80), channel_id=1, source_target_pairs={{0,4},{4,0},{1,5},{5,1},{2,6},{6,2},{3,7},{7,3},{8,12},{12,8},{9,1... | collective-permute-start | bytes 1179656 | tf_op jit(solution)/shard_map/ppermute | solution.py:462
  62.2 3.8 %collective-permute-start.28 = (f32[8,16,384]{2,1,0:T(8,128)S(1)}, f32[8,16,384]{2,1,0:T(8,128)S(1)}, u32[]{:S(2)}, u32[]{:S(2)}) collective-permute-start(f32[8,16,384]{2,1,0:T(8,128)S(1)} %get-tuple-element.82), channel_id=1, source_target_pairs={{0,24},{8,0},{16,8},{24,16},{1,25},{9,1},{17,9},{25,17},{2,26},{10... | collective-permute-start | bytes 589832 | tf_op jit(solution)/shard_map/ppermute | solution.py:462
  66.1 2.1 %collective-permute-start.23 = (f32[112,128]{1,0:T(8,128)S(1)}, f32[112,128]{1,0:T(8,128)S(1)}, u32[]{:S(2)}, u32[]{:S(2)}) collective-permute-start(f32[112,128]{1,0:T(8,128)S(1)} %add.11.mom), channel_id=1, source_target_pairs={{0,6},{1,7},{2,4},{3,5},{4,2},{5,3},{6,0},{7,1},{8,14},{9,15},{10,... | collective-permute-start | bytes 172040 | tf_op jit(solution)/shard_map/ppermute | solution.py:479
  68.2 0.8 collective-permute-start.22
  69.0 2.3 %collective-permute-done.23.corner = f32[112,128]{1,0:T(8,128)S(1)} collective-permute-done((f32[112,128]{1,0:T(8,128)S(1)}, f32[112,128]{1,0:T(8,128)S(1)}, u32[]{:S(2)}, u32[]{:S(2)}) %collective-permute-start.23) | collective-permute-done | bytes 57376 | tf_op jit(solution)/shard_map/ppermute | solution.py:479
  71.3 1.3 %collective-permute-start.21 = (f32[112,128]{1,0:T(8,128)S(1)}, f32[112,128]{1,0:T(8,128)S(1)}, u32[]{:S(2)}, u32[]{:S(2)}) collective-permute-start(f32[112,128]{1,0:T(8,128)S(1)} %add.11.mom), channel_id=1, source_target_pairs={{0,2},{1,3},{2,0},{3,1},{4,6},{5,7},{6,4},{7,5},{8,10},{9,11},{10,... | collective-permute-start | bytes 172040 | tf_op jit(solution)/shard_map/ppermute | solution.py:479
  72.6 2.9 %collective-permute-done.21.across = f32[112,128]{1,0:T(8,128)S(1)} collective-permute-done((f32[112,128]{1,0:T(8,128)S(1)}, f32[112,128]{1,0:T(8,128)S(1)}, u32[]{:S(2)}, u32[]{:S(2)}) %collective-permute-start.21) | collective-permute-done | bytes 57376 | tf_op jit(solution)/shard_map/ppermute | solution.py:479
  75.5 0.2 collective-permute-start.24
  75.8 3.8 %collective-permute-start.25 = (f32[148,128]{1,0:T(8,128)S(1)}, f32[148,128]{1,0:T(8,128)S(1)}, u32[]{:S(2)}, u32[]{:S(2)}) collective-permute-start(f32[148,128]{1,0:T(8,128)S(1)} %get-tuple-element.78), channel_id=1, source_target_pairs={{0,24},{8,0},{16,8},{24,16},{1,25},{9,1},{17,9},{25,17},{2,26},{10... | collective-permute-start | bytes 227336 | tf_op jit(solution)/shard_map/ppermute | solution.py:462
  79.6 2.4 %collective-permute-done.24.left = f32[148,128]{1,0:T(8,128)S(1)} collective-permute-done((f32[148,128]{1,0:T(8,128)S(1)}, f32[148,128]{1,0:T(8,128)S(1)}, u32[]{:S(2)}, u32[]{:S(2)}) %collective-permute-start.24) | collective-permute-done | bytes 75808 | tf_op jit(solution)/shard_map/ppermute | solution.py:462
  82.0 0.0 collective-permute-start.29
  82.0 1.3 %stream.5.g = f32[8,8,16,768]{3,2,1,0:T(8,128)S(1)} custom-call(f32[8,8,16,768]{3,2,1,0:T(8,128)S(1)} %get-tuple-element.74.h, f32[8,768]{1,0:T(8,128)S(1)} %get-tuple-element.47.coef, f32[8,8,16,128]{3,2,1,0:T(8,128)S(1)} %get-tuple-element.48.fluid), custom_call_target="tpu_custom_call" | custom-call | tf_op jit(solution)/shard_map/stream/pallas_call | solution.py:226
  83.3 1.1 %macro.5 = (f32[384,128]{1,0:T(8,128)S(1)}, f32[5,8,128]{2,1,0:T(8,128)S(1)}, f32[8,128]{1,0:T(8,128)S(1)}) custom-call(f32[224,128]{1,0:T(8,128)S(1)} %get-tuple-element.76.mid, f32[148,128]{1,0:T(8,128)S(1)} %collective-permute-done.24.left, f32[148,128]{1,0:T(8,128)S(1)} %collective-permute-done.25.right, f32[8,128]{1,0:T(8,128)S(1)} %get-tuple-element.53.fluid, ...), custom_call_target="tpu_custom_call" | custom-call | tf_op jit(solution)/shard_map/macro/pallas_call | solution.py:358
  84.4 2.0 %collective-permute-done.29.far = f32[8,128]{1,0:T(8,128)S(1)} collective-permute-done((f32[8,128]{1,0:T(8,128)S(1)}, f32[8,128]{1,0:T(8,128)S(1)}, u32[]{:S(2)}, u32[]{:S(2)}) %collective-permute-start.29) | collective-permute-done | bytes 4128 | tf_op jit(solution)/shard_map/ppermute | solution.py:462
  86.5 0.0 collective-permute-done.27.xbefore
  86.5 0.0 collective-permute-done.28.xafter
  86.5 0.0 collective-permute-done.26.yhalo
  86.5 3.1 %update.5 = (f32[8,8,16,768]{3,2,1,0:T(8,128)}, f32[320,16]{1,0:T(8,128)}) custom-call(f32[8,128]{1,0:T(8,128)S(1)} %get-tuple-element.45.target, f32[8,8,16,768]{3,2,1,0:T(8,128)S(1)} %stream.5.g, f32[384,128]{1,0:T(8,128)S(1)} %get-tuple-element.79.mix, bf16[144,768]{1,0:T(8,128)(2,1)S(1)} %get-tuple-element.56.wmat, ...), custom_call_target="tpu_custom_call" | custom-call | tf_op jit(solution)/shard_map/update/pallas_call | solution.py:449
  (17 shorter events, 0.2 us)
Async XLA Ops:
  0.6 27.2 %copy-start.1 = (f32[8,8,16]{2,1,0:T(8,128)S(1)}, f32[8,8,16]{2,1,0:T(8,128)}, u32[]{:S(2)}) copy-start(f32[8,8,16]{2,1,0:T(8,128)} %wall_temp.1) | copy-start | bytes 12292
  0.6 27.2 %copy-start = (s32[8,8,16]{2,1,0:T(8,128)S(1)}, s32[8,8,16]{2,1,0:T(8,128)}, u32[]{:S(2)}) copy-start(s32[8,8,16]{2,1,0:T(8,128)} %wall.1) | copy-start | bytes 12292
  5.0 27.2 %collective-permute-start.6 = (f32[8,16,768]{2,1,0:T(8,128)S(1)}, f32[8,16,768]{2,1,0:T(8,128)S(1)}, u32[]{:S(2)}, u32[]{:S(2)}) collective-permute-start(f32[8,16,768]{2,1,0:T(8,128)S(1)} %get-tuple-element.58), channel_id=1, source_target_pairs={{0,4},{4,0},{1,5},{5,1},{2,6},{6,2},{3,7},{7,3},{8,12},{12,8},{9,1... | collective-permute-start | bytes 1179656 | tf_op jit(solution)/shard_map/ppermute | solution.py:462
  8.1 3.8 %collective-permute-start = (f32[112,128]{1,0:T(8,128)S(1)}, f32[112,128]{1,0:T(8,128)S(1)}, u32[]{:S(2)}, u32[]{:S(2)}) collective-permute-start(f32[112,128]{1,0:T(8,128)S(1)} %get-tuple-element.49), channel_id=1, source_target_pairs={{0,1},{1,0},{2,3},{3,2},{4,5},{5,4},{6,7},{7,6},{8,9},{9,8},{10,11... | collective-permute-start | bytes 172040 | tf_op jit(solution)/shard_map/ppermute | solution.py:479
  8.1 24.1 %collective-permute-start.7 = (f32[8,16,384]{2,1,0:T(8,128)S(1)}, f32[8,16,384]{2,1,0:T(8,128)S(1)}, u32[]{:S(2)}, u32[]{:S(2)}) collective-permute-start(f32[8,16,384]{2,1,0:T(8,128)S(1)} %get-tuple-element.59), channel_id=1, source_target_pairs={{0,8},{8,16},{16,24},{24,0},{1,9},{9,17},{17,25},{25,1},{2,10},{10... | collective-permute-start | bytes 589832 | tf_op jit(solution)/shard_map/ppermute | solution.py:462
  9.7 22.5 %collective-permute-start.8 = (f32[8,16,384]{2,1,0:T(8,128)S(1)}, f32[8,16,384]{2,1,0:T(8,128)S(1)}, u32[]{:S(2)}, u32[]{:S(2)}) collective-permute-start(f32[8,16,384]{2,1,0:T(8,128)S(1)} %get-tuple-element.60), channel_id=1, source_target_pairs={{0,24},{8,0},{16,8},{24,16},{1,25},{9,1},{17,9},{25,17},{2,26},{10... | collective-permute-start | bytes 589832 | tf_op jit(solution)/shard_map/ppermute | solution.py:462
  11.9 5.1 %collective-permute-start.3 = (f32[112,128]{1,0:T(8,128)S(1)}, f32[112,128]{1,0:T(8,128)S(1)}, u32[]{:S(2)}, u32[]{:S(2)}) collective-permute-start(f32[112,128]{1,0:T(8,128)S(1)} %add.9.mom), channel_id=1, source_target_pairs={{0,6},{1,7},{2,4},{3,5},{4,2},{5,3},{6,0},{7,1},{8,14},{9,15},{10,... | collective-permute-start | bytes 172040 | tf_op jit(solution)/shard_map/ppermute | solution.py:479
  13.4 6.2 %collective-permute-start.2 = (f32[112,128]{1,0:T(8,128)S(1)}, f32[112,128]{1,0:T(8,128)S(1)}, u32[]{:S(2)}, u32[]{:S(2)}) collective-permute-start(f32[112,128]{1,0:T(8,128)S(1)} %add.9.mom), channel_id=1, source_target_pairs={{0,4},{1,5},{2,6},{3,7},{4,0},{5,1},{6,2},{7,3},{8,12},{9,13},{10,... | collective-permute-start | bytes 172040 | tf_op jit(solution)/shard_map/ppermute | solution.py:479
  17.1 4.2 %collective-permute-start.1 = (f32[112,128]{1,0:T(8,128)S(1)}, f32[112,128]{1,0:T(8,128)S(1)}, u32[]{:S(2)}, u32[]{:S(2)}) collective-permute-start(f32[112,128]{1,0:T(8,128)S(1)} %add.9.mom), channel_id=1, source_target_pairs={{0,2},{1,3},{2,0},{3,1},{4,6},{5,7},{6,4},{7,5},{8,10},{9,11},{10,... | collective-permute-start | bytes 172040 | tf_op jit(solution)/shard_map/ppermute | solution.py:479
  21.3 6.4 %collective-permute-start.4 = (f32[148,128]{1,0:T(8,128)S(1)}, f32[148,128]{1,0:T(8,128)S(1)}, u32[]{:S(2)}, u32[]{:S(2)}) collective-permute-start(f32[148,128]{1,0:T(8,128)S(1)} %get-tuple-element.51), channel_id=1, source_target_pairs={{0,8},{8,16},{16,24},{24,0},{1,9},{9,17},{17,25},{25,1},{2,10},{10... | collective-permute-start | bytes 227336 | tf_op jit(solution)/shard_map/ppermute | solution.py:462
  21.6 8.7 %collective-permute-start.5 = (f32[148,128]{1,0:T(8,128)S(1)}, f32[148,128]{1,0:T(8,128)S(1)}, u32[]{:S(2)}, u32[]{:S(2)}) collective-permute-start(f32[148,128]{1,0:T(8,128)S(1)} %get-tuple-element.52), channel_id=1, source_target_pairs={{0,24},{8,0},{16,8},{24,16},{1,25},{9,1},{17,9},{25,17},{2,26},{10... | collective-permute-start | bytes 227336 | tf_op jit(solution)/shard_map/ppermute | solution.py:462
  27.7 4.5 %collective-permute-start.9 = (f32[8,128]{1,0:T(8,128)S(1)}, f32[8,128]{1,0:T(8,128)S(1)}, u32[]{:S(2)}, u32[]{:S(2)}) collective-permute-start(f32[8,128]{1,0:T(8,128)S(1)} %get-tuple-element.62), channel_id=1, source_target_pairs={{0,16},{8,24},{16,0},{24,8},{1,17},{9,25},{17,1},{25,9},{2,18},{10... | collective-permute-start | bytes 12296 | tf_op jit(solution)/shard_map/ppermute | solution.py:462
  34.1 25.2 %collective-permute-start.16 = (f32[8,16,768]{2,1,0:T(8,128)S(1)}, f32[8,16,768]{2,1,0:T(8,128)S(1)}, u32[]{:S(2)}, u32[]{:S(2)}) collective-permute-start(f32[8,16,768]{2,1,0:T(8,128)S(1)} %get-tuple-element.69), channel_id=1, source_target_pairs={{0,4},{4,0},{1,5},{5,1},{2,6},{6,2},{3,7},{7,3},{8,12},{12,8},{9,1... | collective-permute-start | bytes 1179656 | tf_op jit(solution)/shard_map/ppermute | solution.py:462
  35.4 3.8 %collective-permute-start.10 = (f32[112,128]{1,0:T(8,128)S(1)}, f32[112,128]{1,0:T(8,128)S(1)}, u32[]{:S(2)}, u32[]{:S(2)}) collective-permute-start(f32[112,128]{1,0:T(8,128)S(1)} %get-tuple-element.64), channel_id=1, source_target_pairs={{0,1},{1,0},{2,3},{3,2},{4,5},{5,4},{6,7},{7,6},{8,9},{9,8},{10,11... | collective-permute-start | bytes 172040 | tf_op jit(solution)/shard_map/ppermute | solution.py:479
  35.4 24.0 %collective-permute-start.17 = (f32[8,16,384]{2,1,0:T(8,128)S(1)}, f32[8,16,384]{2,1,0:T(8,128)S(1)}, u32[]{:S(2)}, u32[]{:S(2)}) collective-permute-start(f32[8,16,384]{2,1,0:T(8,128)S(1)} %get-tuple-element.70), channel_id=1, source_target_pairs={{0,8},{8,16},{16,24},{24,0},{1,9},{9,17},{17,25},{25,1},{2,10},{10... | collective-permute-start | bytes 589832 | tf_op jit(solution)/shard_map/ppermute | solution.py:462
  36.9 22.4 %collective-permute-start.18 = (f32[8,16,384]{2,1,0:T(8,128)S(1)}, f32[8,16,384]{2,1,0:T(8,128)S(1)}, u32[]{:S(2)}, u32[]{:S(2)}) collective-permute-start(f32[8,16,384]{2,1,0:T(8,128)S(1)} %get-tuple-element.71), channel_id=1, source_target_pairs={{0,24},{8,0},{16,8},{24,16},{1,25},{9,1},{17,9},{25,17},{2,26},{10... | collective-permute-start | bytes 589832 | tf_op jit(solution)/shard_map/ppermute | solution.py:462
  39.2 5.1 %collective-permute-start.13 = (f32[112,128]{1,0:T(8,128)S(1)}, f32[112,128]{1,0:T(8,128)S(1)}, u32[]{:S(2)}, u32[]{:S(2)}) collective-permute-start(f32[112,128]{1,0:T(8,128)S(1)} %add.10.mom), channel_id=1, source_target_pairs={{0,6},{1,7},{2,4},{3,5},{4,2},{5,3},{6,0},{7,1},{8,14},{9,15},{10,... | collective-permute-start | bytes 172040 | tf_op jit(solution)/shard_map/ppermute | solution.py:479
  41.0 4.8 %collective-permute-start.12 = (f32[112,128]{1,0:T(8,128)S(1)}, f32[112,128]{1,0:T(8,128)S(1)}, u32[]{:S(2)}, u32[]{:S(2)}) collective-permute-start(f32[112,128]{1,0:T(8,128)S(1)} %add.10.mom), channel_id=1, source_target_pairs={{0,4},{1,5},{2,6},{3,7},{4,0},{5,1},{6,2},{7,3},{8,12},{9,13},{10,... | collective-permute-start | bytes 172040 | tf_op jit(solution)/shard_map/ppermute | solution.py:479
  44.4 4.2 %collective-permute-start.11 = (f32[112,128]{1,0:T(8,128)S(1)}, f32[112,128]{1,0:T(8,128)S(1)}, u32[]{:S(2)}, u32[]{:S(2)}) collective-permute-start(f32[112,128]{1,0:T(8,128)S(1)} %add.10.mom), channel_id=1, source_target_pairs={{0,2},{1,3},{2,0},{3,1},{4,6},{5,7},{6,4},{7,5},{8,10},{9,11},{10,... | collective-permute-start | bytes 172040 | tf_op jit(solution)/shard_map/ppermute | solution.py:479
  48.6 6.2 %collective-permute-start.14 = (f32[148,128]{1,0:T(8,128)S(1)}, f32[148,128]{1,0:T(8,128)S(1)}, u32[]{:S(2)}, u32[]{:S(2)}) collective-permute-start(f32[148,128]{1,0:T(8,128)S(1)} %get-tuple-element.66), channel_id=1, source_target_pairs={{0,8},{8,16},{16,24},{24,0},{1,9},{9,17},{17,25},{25,1},{2,10},{10... | collective-permute-start | bytes 227336 | tf_op jit(solution)/shard_map/ppermute | solution.py:462
  48.7 7.5 %collective-permute-start.15 = (f32[148,128]{1,0:T(8,128)S(1)}, f32[148,128]{1,0:T(8,128)S(1)}, u32[]{:S(2)}, u32[]{:S(2)}) collective-permute-start(f32[148,128]{1,0:T(8,128)S(1)} %get-tuple-element.67), channel_id=1, source_target_pairs={{0,24},{8,0},{16,8},{24,16},{1,25},{9,1},{17,9},{25,17},{2,26},{10... | collective-permute-start | bytes 227336 | tf_op jit(solution)/shard_map/ppermute | solution.py:462
  54.9 4.5 %collective-permute-start.19 = (f32[8,128]{1,0:T(8,128)S(1)}, f32[8,128]{1,0:T(8,128)S(1)}, u32[]{:S(2)}, u32[]{:S(2)}) collective-permute-start(f32[8,128]{1,0:T(8,128)S(1)} %get-tuple-element.73), channel_id=1, source_target_pairs={{0,16},{8,24},{16,0},{24,8},{1,17},{9,25},{17,1},{25,9},{2,18},{10... | collective-permute-start | bytes 12296 | tf_op jit(solution)/shard_map/ppermute | solution.py:462
  61.3 25.2 %collective-permute-start.26 = (f32[8,16,768]{2,1,0:T(8,128)S(1)}, f32[8,16,768]{2,1,0:T(8,128)S(1)}, u32[]{:S(2)}, u32[]{:S(2)}) collective-permute-start(f32[8,16,768]{2,1,0:T(8,128)S(1)} %get-tuple-element.80), channel_id=1, source_target_pairs={{0,4},{4,0},{1,5},{5,1},{2,6},{6,2},{3,7},{7,3},{8,12},{12,8},{9,1... | collective-permute-start | bytes 1179656 | tf_op jit(solution)/shard_map/ppermute | solution.py:462
  62.2 3.8 %collective-permute-start.20 = (f32[112,128]{1,0:T(8,128)S(1)}, f32[112,128]{1,0:T(8,128)S(1)}, u32[]{:S(2)}, u32[]{:S(2)}) collective-permute-start(f32[112,128]{1,0:T(8,128)S(1)} %get-tuple-element.75), channel_id=1, source_target_pairs={{0,1},{1,0},{2,3},{3,2},{4,5},{5,4},{6,7},{7,6},{8,9},{9,8},{10,11... | collective-permute-start | bytes 172040 | tf_op jit(solution)/shard_map/ppermute | solution.py:479
  62.2 24.2 %collective-permute-start.27 = (f32[8,16,384]{2,1,0:T(8,128)S(1)}, f32[8,16,384]{2,1,0:T(8,128)S(1)}, u32[]{:S(2)}, u32[]{:S(2)}) collective-permute-start(f32[8,16,384]{2,1,0:T(8,128)S(1)} %get-tuple-element.81), channel_id=1, source_target_pairs={{0,8},{8,16},{16,24},{24,0},{1,9},{9,17},{17,25},{25,1},{2,10},{10... | collective-permute-start | bytes 589832 | tf_op jit(solution)/shard_map/ppermute | solution.py:462
  62.2 24.2 %collective-permute-start.28 = (f32[8,16,384]{2,1,0:T(8,128)S(1)}, f32[8,16,384]{2,1,0:T(8,128)S(1)}, u32[]{:S(2)}, u32[]{:S(2)}) collective-permute-start(f32[8,16,384]{2,1,0:T(8,128)S(1)} %get-tuple-element.82), channel_id=1, source_target_pairs={{0,24},{8,0},{16,8},{24,16},{1,25},{9,1},{17,9},{25,17},{2,26},{10... | collective-permute-start | bytes 589832 | tf_op jit(solution)/shard_map/ppermute | solution.py:462
  66.1 5.2 %collective-permute-start.23 = (f32[112,128]{1,0:T(8,128)S(1)}, f32[112,128]{1,0:T(8,128)S(1)}, u32[]{:S(2)}, u32[]{:S(2)}) collective-permute-start(f32[112,128]{1,0:T(8,128)S(1)} %add.11.mom), channel_id=1, source_target_pairs={{0,6},{1,7},{2,4},{3,5},{4,2},{5,3},{6,0},{7,1},{8,14},{9,15},{10,... | collective-permute-start | bytes 172040 | tf_op jit(solution)/shard_map/ppermute | solution.py:479
  68.2 4.4 %collective-permute-start.22 = (f32[112,128]{1,0:T(8,128)S(1)}, f32[112,128]{1,0:T(8,128)S(1)}, u32[]{:S(2)}, u32[]{:S(2)}) collective-permute-start(f32[112,128]{1,0:T(8,128)S(1)} %add.11.mom), channel_id=1, source_target_pairs={{0,4},{1,5},{2,6},{3,7},{4,0},{5,1},{6,2},{7,3},{8,12},{9,13},{10,... | collective-permute-start | bytes 172040 | tf_op jit(solution)/shard_map/ppermute | solution.py:479
  71.3 4.2 %collective-permute-start.21 = (f32[112,128]{1,0:T(8,128)S(1)}, f32[112,128]{1,0:T(8,128)S(1)}, u32[]{:S(2)}, u32[]{:S(2)}) collective-permute-start(f32[112,128]{1,0:T(8,128)S(1)} %add.11.mom), channel_id=1, source_target_pairs={{0,2},{1,3},{2,0},{3,1},{4,6},{5,7},{6,4},{7,5},{8,10},{9,11},{10,... | collective-permute-start | bytes 172040 | tf_op jit(solution)/shard_map/ppermute | solution.py:479
  75.5 6.4 %collective-permute-start.24 = (f32[148,128]{1,0:T(8,128)S(1)}, f32[148,128]{1,0:T(8,128)S(1)}, u32[]{:S(2)}, u32[]{:S(2)}) collective-permute-start(f32[148,128]{1,0:T(8,128)S(1)} %get-tuple-element.77), channel_id=1, source_target_pairs={{0,8},{8,16},{16,24},{24,0},{1,9},{9,17},{17,25},{25,1},{2,10},{10... | collective-permute-start | bytes 227336 | tf_op jit(solution)/shard_map/ppermute | solution.py:462
  75.8 7.5 %collective-permute-start.25 = (f32[148,128]{1,0:T(8,128)S(1)}, f32[148,128]{1,0:T(8,128)S(1)}, u32[]{:S(2)}, u32[]{:S(2)}) collective-permute-start(f32[148,128]{1,0:T(8,128)S(1)} %get-tuple-element.78), channel_id=1, source_target_pairs={{0,24},{8,0},{16,8},{24,16},{1,25},{9,1},{17,9},{25,17},{2,26},{10... | collective-permute-start | bytes 227336 | tf_op jit(solution)/shard_map/ppermute | solution.py:462
  82.0 4.5 %collective-permute-start.29 = (f32[8,128]{1,0:T(8,128)S(1)}, f32[8,128]{1,0:T(8,128)S(1)}, u32[]{:S(2)}, u32[]{:S(2)}) collective-permute-start(f32[8,128]{1,0:T(8,128)S(1)} %get-tuple-element.84), channel_id=1, source_target_pairs={{0,16},{8,24},{16,0},{24,8},{1,17},{9,25},{17,1},{25,9},{2,18},{10... | collective-permute-start | bytes 12296 | tf_op jit(solution)/shard_map/ppermute | solution.py:462

commit v5 on v4

--- a/solution.py
+++ b/solution.py
@@ -114,8 +114,10 @@
     wmat[KROWS : 2 * KROWS, :] = high
     wmat[2 * KROWS : 3 * KROWS, :] = low
 
-    for x in order:
-        copies[x].wait()
+    for i, x in enumerate(order):
+        if i % 4 == 0:
+            for other in order[i : i + 4]:
+                copies[other].wait()
         plane = h[x].reshape(ny * nz, nv)
         out = local_moments(proj[...], plane)
         mom[pl.ds(x, MOMENTS, stride=planes), :] = out[:MOMENTS]
@@ -263,7 +265,7 @@
     )(mom, across, beside, corner)
 
 
-def macro_kernel(mid, left, right, fluid, heat, mix, state_out, mass_out, *, nz):
+def macro_kernel(mid, left, right, fluid, heat, mix, mass_out, *state_out, nz):
     nx, width = fluid.shape
     blank = jnp.zeros((nx - REACH, width), f32)
 
@@ -349,19 +351,20 @@
     emit(41, heat[...] * (1.0 - is_fluid))
     for k in range(42, KROWS):
         emit(k, jnp.zeros((nx, width), f32))
-    for k in range(5):
-        state_out[k] = centre(state[k])
-
-
-def macro(mid, left, right, fluid, heat, nz):
+    for out in state_out:
+        for k in range(5):
+            out[k] = centre(state[k])
+
+
+def macro(mid, left, right, fluid, heat, nz, last):
     nx, width = fluid.shape
     return pl.pallas_call(
         functools.partial(macro_kernel, nz=nz),
         out_shape=[
             jax.ShapeDtypeStruct((KROWS * nx, width), f32),
-            jax.ShapeDtypeStruct((5, nx, width), f32),
             jax.ShapeDtypeStruct((nx, width), f32),
-        ],
+        ]
+        + [jax.ShapeDtypeStruct((5, nx, width), f32)] * last,
         name="macro",
         compiler_params=pltpu.CompilerParams(vmem_limit_bytes=8 << 20),
     )(mid, left, right, fluid, heat)
@@ -371,7 +374,7 @@
     nx, ny, nz, nv = g.shape
     half = nv // 2
     if last:
-        state, result, fields, h, sent = refs
+        state, result, fields_far, h, fields, sent = refs
         copies = [pltpu.make_async_copy(h.at[x], result.at[x], sent.at[x]) for x in range(nx)]
     else:
         h, mom, ysend, xup, xdown = refs
@@ -380,6 +383,12 @@
     offset = target[0:1, 0:1] - total / cells
     is_offset = lax.broadcasted_iota(jnp.int32, (KROWS, ny * nz), 0) == 40
     scale = jnp.where(is_offset, jnp.broadcast_to(offset, (KROWS, ny * nz)), 1.0)
+    if last:
+        fields_copy = pltpu.make_async_copy(fields, fields_far, sent.at[nx])
+        for k in range(5):
+            value = state[k] + jnp.broadcast_to(offset, (nx, ny * nz)) if k == 0 else state[k]
+            for y in range(ny):
+                fields[pl.ds(k * nx * ny + y, nx, stride=ny), :] = value[:, y * nz : (y + 1) * nz]
     along_x, along_y = coef[1:2, :], coef[2:3, :]
     upward = coef[4:5, :] > 0.0
     first_y = jnp.where(upward, along_y, 0.0)
@@ -409,8 +418,11 @@
         plane = jnp.concatenate(pieces, axis=0)
         h[x] = plane.reshape(ny, nz, nv)
         if last:
-            if x:
-                copies[x - 1].start()
+            if x % 2 == 1:
+                if x < 2:
+                    fields_copy.start()
+                for other in range(x + 1 - 2, x + 1):
+                    copies[other].start()
         else:
             out = local_moments(proj[...], plane)
             mom[pl.ds(x, MOMENTS, stride=nx), :] = out[:MOMENTS]
@@ -420,18 +432,15 @@
             if x == 0:
                 xdown[...] = h[x, :, :, half:]
     if last:
-        copies[nx - 1].start()
-        for k in range(5):
-            value = state[k] + jnp.broadcast_to(offset, (nx, ny * nz)) if k == 0 else state[k]
-            for y in range(ny):
-                fields[pl.ds(k * nx * ny + y, nx, stride=ny), :] = value[:, y * nz : (y + 1) * nz]
-        for copy in copies:
+        for other in range(nx - nx % 2, nx):
+            copies[other].start()
+        for copy in [fields_copy, *copies]:
             copy.wait()
 
 
 def update(target, g, mix, wmat, proj, coef, fluid, halos, mass, far, state, cells):
     nx, ny, nz, nv = g.shape
-    last = state is not None
+    last = bool(state)
     shapes = [jax.ShapeDtypeStruct(g.shape, f32)]
     if last:
         shapes.append(jax.ShapeDtypeStruct((5 * nx * ny, nz), f32))
@@ -444,14 +453,20 @@
         ]
     operands = [target, g, mix, wmat, proj, coef, fluid, *halos, mass, far]
     if last:
-        operands.append(state)
+        operands += state
     vmem = pl.BlockSpec(memory_space=pltpu.VMEM)
     return pl.pallas_call(
         functools.partial(update_kernel, last=last, cells=cells),
         in_specs=[vmem] * len(operands),
         out_shape=shapes,
-        out_specs=[pl.BlockSpec(memory_space=pltpu.HBM), vmem] if last else [vmem] * len(shapes),
-        scratch_shapes=[pltpu.VMEM(g.shape, f32), pltpu.SemaphoreType.DMA((nx,))] if last else [],
+        out_specs=[pl.BlockSpec(memory_space=pltpu.HBM)] * 2 if last else [vmem] * len(shapes),
+        scratch_shapes=[
+            pltpu.VMEM(g.shape, f32),
+            pltpu.VMEM((5 * nx * ny, nz), f32),
+            pltpu.SemaphoreType.DMA((nx + 1,)),
+        ]
+        if last
+        else [],
         name="update",
         compiler_params=pltpu.CompilerParams(vmem_limit_bytes=14 << 20),
     )(*operands)
@@ -505,9 +520,9 @@
         if iteration == 0:
             fluid_rows, heat, fluid_cells = walls(wall, wall_temp)
         g = stream(h, coef, fluid_cells)
-        mix, state, mass = macro(both, left, right, fluid_rows, heat, nz)
+        mix, mass, *state = macro(both, left, right, fluid_rows, heat, nz, last)
         halos = (yhalo, xbefore, xafter)
-        outs = update(target, g, mix, wmat, proj, coef, fluid_cells, halos, mass, far, state if last else None, cells)
+        outs = update(target, g, mix, wmat, proj, coef, fluid_cells, halos, mass, far, state, cells)
         h = outs[0]
         if not last:
             mom, ysend, xup, xdown = outs[1:]

time: 90 us -> 88.5 us (0.983)
  Pallas kernels: 20.3 us -> 18.2 us
    pallas_call x1, Pallas kernels: 3.72 us -> 2.63 us  [prepare(): pl.pallas_call(functools.partial(prepare_kernel, total=total), in_specs=[...]
    pallas_call x3, Pallas kernels: 4.41 us -> 3.38 us  [macro(): pl.pallas_call(functools.partial(macro_kernel, nz=nz), out_shape=[jax.Sha...]
    ppermute x18, waiting for transfers between devices: 11.1 us -> 12.1 us  [ring(): lax.ppermute(value, axis, [(i, (i + step) % count) for i in range(count)])]
  transfers between devices with their start and end apart: 30 -> 30, of which waited for: 13 -> 13; matrix products, arithmetic and copies ran while one was open for 0% -> 0% of each run, Pallas kernels for 11% -> 10%
where the time goes in v5:
time: 88.5 us; the launch traced here: 88.3 us
  starting transfers between devices  41.7 us (47%)
  waiting for transfers between devices  26.7 us (30%)
  Pallas kernels  18.2 us (21%)
  between operations  1.6 us (2%)
    ppermute x18, starting transfers between devices, ring(): lax.ppermute(value, axis, [(i, (i + step) % count) for i in range(count)])  28.3 us
    ppermute x12, waiting for transfers between devices, plane_pair(): return lax.ppermute(value, ('ty', 'vel'), pairs)  14.6 us
    ppermute x12, starting transfers between devices, plane_pair(): return lax.ppermute(value, ('ty', 'vel'), pairs)  13.5 us
    ppermute x18, waiting for transfers between devices, ring(): lax.ppermute(value, axis, [(i, (i + step) % count) for i in range(count)])  12.1 us
    pallas_call x3, Pallas kernels, update(): pl.pallas_call(functools.partial(update_kernel, last=last, cells=cells),...  6.99 us
    pallas_call x3, Pallas kernels, stream(): pl.pallas_call(stream_kernel, out_shape=jax.ShapeDtypeStruct(h.shape, f32...  4.01 us
    pallas_call x3, Pallas kernels, macro(): pl.pallas_call(functools.partial(macro_kernel, nz=nz), out_shape=[jax.Sha...  3.38 us
    pallas_call x1, Pallas kernels, prepare(): pl.pallas_call(functools.partial(prepare_kernel, total=total), in_specs=[...  2.63 us
  transfers between devices with their start and end apart: 30, of which 13 were waited for; matrix products, arithmetic and copies ran while one was open for 0% of the time, Pallas kernels for 10%

profile of v5, /device:TPU:0, one launch (start us, length us, event | category | flops | bytes accessed | tf_op | source)
XLA Modules:
  0.0 88.3 jit_solution(9671525795196194932)
XLA Ops:
  1.3 2.6 %prepare.1 = (f32[8,8,16,768]{3,2,1,0:T(8,128)S(1)}, f32[112,128]{1,0:T(8,128)S(1)}, bf16[32,768]{1,0:T(8,128)(2,1)S(1)}, bf16[144,768]{1,0:T(8,128)(2,1)S(1)}, ...) custom-call(f32[3,768]{1,0:T(4,128)} %vel_far.1, ...), custom_call_target="tpu_custom_call" | custom-call | tf_op jit(solution)/shard_map/prepare/pallas_call | solution.py:133
  3.9 3.1 %collective-permute-start.6 = (f32[8,16,768]{2,1,0:T(8,128)S(1)}, f32[8,16,768]{2,1,0:T(8,128)S(1)}, u32[]{:S(2)}, u32[]{:S(2)}) collective-permute-start(f32[8,16,768]{2,1,0:T(8,128)S(1)} %get-tuple-element.58), channel_id=1, source_target_pairs={{0,4},{4,0},{1,5},{5,1},{2,6},{6,2},{3,7},{7,3},{8,12},{12,8},{9,1... | collective-permute-start | bytes 1179656 | tf_op jit(solution)/shard_map/ppermute | solution.py:477
  7.0 0.0 collective-permute-start
  7.0 1.6 %collective-permute-start.7 = (f32[8,16,384]{2,1,0:T(8,128)S(1)}, f32[8,16,384]{2,1,0:T(8,128)S(1)}, u32[]{:S(2)}, u32[]{:S(2)}) collective-permute-start(f32[8,16,384]{2,1,0:T(8,128)S(1)} %get-tuple-element.59), channel_id=1, source_target_pairs={{0,8},{8,16},{16,24},{24,0},{1,9},{9,17},{17,25},{25,1},{2,10},{10... | collective-permute-start | bytes 589832 | tf_op jit(solution)/shard_map/ppermute | solution.py:477
  8.6 2.2 %collective-permute-start.8 = (f32[8,16,384]{2,1,0:T(8,128)S(1)}, f32[8,16,384]{2,1,0:T(8,128)S(1)}, u32[]{:S(2)}, u32[]{:S(2)}) collective-permute-start(f32[8,16,384]{2,1,0:T(8,128)S(1)} %get-tuple-element.60), channel_id=1, source_target_pairs={{0,24},{8,0},{16,8},{24,16},{1,25},{9,1},{17,9},{25,17},{2,26},{10... | collective-permute-start | bytes 589832 | tf_op jit(solution)/shard_map/ppermute | solution.py:477
  10.8 0.0 collective-permute-done
  10.8 1.5 %collective-permute-start.3 = (f32[112,128]{1,0:T(8,128)S(1)}, f32[112,128]{1,0:T(8,128)S(1)}, u32[]{:S(2)}, u32[]{:S(2)}) collective-permute-start(f32[112,128]{1,0:T(8,128)S(1)} %add.9.mom), channel_id=1, source_target_pairs={{0,6},{1,7},{2,4},{3,5},{4,2},{5,3},{6,0},{7,1},{8,14},{9,15},{10,... | collective-permute-start | bytes 172040 | tf_op jit(solution)/shard_map/ppermute | solution.py:494
  12.3 1.5 %collective-permute-start.2 = (f32[112,128]{1,0:T(8,128)S(1)}, f32[112,128]{1,0:T(8,128)S(1)}, u32[]{:S(2)}, u32[]{:S(2)}) collective-permute-start(f32[112,128]{1,0:T(8,128)S(1)} %add.9.mom), channel_id=1, source_target_pairs={{0,4},{1,5},{2,6},{3,7},{4,0},{5,1},{6,2},{7,3},{8,12},{9,13},{10,... | collective-permute-start | bytes 172040 | tf_op jit(solution)/shard_map/ppermute | solution.py:494
  13.9 2.1 %collective-permute-done.3.corner = f32[112,128]{1,0:T(8,128)S(1)} collective-permute-done((f32[112,128]{1,0:T(8,128)S(1)}, f32[112,128]{1,0:T(8,128)S(1)}, u32[]{:S(2)}, u32[]{:S(2)}) %collective-permute-start.3) | collective-permute-done | bytes 57376 | tf_op jit(solution)/shard_map/ppermute | solution.py:494
  16.0 1.5 %collective-permute-start.1 = (f32[112,128]{1,0:T(8,128)S(1)}, f32[112,128]{1,0:T(8,128)S(1)}, u32[]{:S(2)}, u32[]{:S(2)}) collective-permute-start(f32[112,128]{1,0:T(8,128)S(1)} %add.9.mom), channel_id=1, source_target_pairs={{0,2},{1,3},{2,0},{3,1},{4,6},{5,7},{6,4},{7,5},{8,10},{9,11},{10,... | collective-permute-start | bytes 172040 | tf_op jit(solution)/shard_map/ppermute | solution.py:494
  17.5 1.1 %collective-permute-done.2.beside = f32[112,128]{1,0:T(8,128)S(1)} collective-permute-done((f32[112,128]{1,0:T(8,128)S(1)}, f32[112,128]{1,0:T(8,128)S(1)}, u32[]{:S(2)}, u32[]{:S(2)}) %collective-permute-start.2) | collective-permute-done | bytes 57376 | tf_op jit(solution)/shard_map/ppermute | solution.py:494
  18.6 1.6 %collective-permute-done.1.across = f32[112,128]{1,0:T(8,128)S(1)} collective-permute-done((f32[112,128]{1,0:T(8,128)S(1)}, f32[112,128]{1,0:T(8,128)S(1)}, u32[]{:S(2)}, u32[]{:S(2)}) %collective-permute-start.1) | collective-permute-done | bytes 57376 | tf_op jit(solution)/shard_map/ppermute | solution.py:494
  20.2 0.3 collective-permute-start.4
  20.5 3.6 %collective-permute-start.5 = (f32[148,128]{1,0:T(8,128)S(1)}, f32[148,128]{1,0:T(8,128)S(1)}, u32[]{:S(2)}, u32[]{:S(2)}) collective-permute-start(f32[148,128]{1,0:T(8,128)S(1)} %get-tuple-element.52), channel_id=1, source_target_pairs={{0,24},{8,0},{16,8},{24,16},{1,25},{9,1},{17,9},{25,17},{2,26},{10... | collective-permute-start | bytes 227336 | tf_op jit(solution)/shard_map/ppermute | solution.py:477
  24.1 2.5 %collective-permute-done.4.left = f32[148,128]{1,0:T(8,128)S(1)} collective-permute-done((f32[148,128]{1,0:T(8,128)S(1)}, f32[148,128]{1,0:T(8,128)S(1)}, u32[]{:S(2)}, u32[]{:S(2)}) %collective-permute-start.4) | collective-permute-done | bytes 75808 | tf_op jit(solution)/shard_map/ppermute | solution.py:477
  26.6 0.1 collective-permute-start.9
  26.7 1.1 %walls.1 = (f32[8,128]{1,0:T(8,128)S(1)}, f32[8,128]{1,0:T(8,128)S(1)}, f32[8,8,16,128]{3,2,1,0:T(8,128)S(1)}) custom-call(s32[8,8,16]{2,1,0:T(8,128)S(1)} %copy-done, f32[8,8,16]{2,1,0:T(8,128)S(1)} %copy-done.1), custom_call_target="tpu_custom_call" | custom-call | tf_op jit(solution)/shard_map/walls/pallas_call | solution.py:176
  27.8 1.3 %stream.3.g = f32[8,8,16,768]{3,2,1,0:T(8,128)S(1)} custom-call(f32[8,8,16,768]{3,2,1,0:T(8,128)S(1)} %get-tuple-element.46.h, f32[8,768]{1,0:T(8,128)S(1)} %get-tuple-element.47.coef, f32[8,8,16,128]{3,2,1,0:T(8,128)S(1)} %get-tuple-element.48.fluid), custom_call_target="tpu_custom_call" | custom-call | tf_op jit(solution)/shard_map/stream/pallas_call | solution.py:228
  29.2 0.0 collective-permute-done.5.right
  29.2 1.1 %macro.3 = (f32[384,128]{1,0:T(8,128)S(1)}, f32[8,128]{1,0:T(8,128)S(1)}) custom-call(f32[224,128]{1,0:T(8,128)S(1)} %get-tuple-element.50.mid, f32[148,128]{1,0:T(8,128)S(1)} %collective-permute-done.4.left, f32[148,128]{1,0:T(8,128)S(1)} %collective-permute-done.5.right, f32[8,128]{1,0:T(8,128)S(1)} %get-tuple-element.53.fluid, ...), custom_call_target="tpu_custom_call" | custom-call | tf_op jit(solution)/shard_map/macro/pallas_call | solution.py:361
  30.3 0.8 collective-permute-done.9.far
  31.1 0.0 collective-permute-done.7.xbefore
  31.1 0.0 collective-permute-done.6.yhalo
  31.1 1.9 %update.3 = (f32[8,8,16,768]{3,2,1,0:T(8,128)S(1)}, f32[112,128]{1,0:T(8,128)S(1)}, f32[8,16,768]{2,1,0:T(8,128)S(1)}, f32[8,16,384]{2,1,0:T(8,128)S(1)}, f32[8,16,384]{2,1,0:T(8,128)S(1)}) custom-call(f32[8,128]{1,0:T(8,128)S(1)} %get-tuple-element.45.target, f32[8,8,16,768]{3,2,1,0:T(8,128)S(1)} %stream.3.g, f32[384,128]{1,0:T(8,128)S(1)} %get-tuple-element.55.mix, ...), custom_call_target="tpu_custom_call" | custom-call | tf_op jit(solution)/shard_map/update/pallas_call | solution.py:458
  33.1 0.8 collective-permute-start.16
  33.8 1.5 %collective-permute-start.17 = (f32[8,16,384]{2,1,0:T(8,128)S(1)}, f32[8,16,384]{2,1,0:T(8,128)S(1)}, u32[]{:S(2)}, u32[]{:S(2)}) collective-permute-start(f32[8,16,384]{2,1,0:T(8,128)S(1)} %get-tuple-element.70), channel_id=1, source_target_pairs={{0,8},{8,16},{16,24},{24,0},{1,9},{9,17},{17,25},{25,1},{2,10},{10... | collective-permute-start | bytes 589832 | tf_op jit(solution)/shard_map/ppermute | solution.py:477
  35.3 2.3 %collective-permute-start.18 = (f32[8,16,384]{2,1,0:T(8,128)S(1)}, f32[8,16,384]{2,1,0:T(8,128)S(1)}, u32[]{:S(2)}, u32[]{:S(2)}) collective-permute-start(f32[8,16,384]{2,1,0:T(8,128)S(1)} %get-tuple-element.71), channel_id=1, source_target_pairs={{0,24},{8,0},{16,8},{24,16},{1,25},{9,1},{17,9},{25,17},{2,26},{10... | collective-permute-start | bytes 589832 | tf_op jit(solution)/shard_map/ppermute | solution.py:477
  37.7 2.3 %collective-permute-start.13 = (f32[112,128]{1,0:T(8,128)S(1)}, f32[112,128]{1,0:T(8,128)S(1)}, u32[]{:S(2)}, u32[]{:S(2)}) collective-permute-start(f32[112,128]{1,0:T(8,128)S(1)} %add.10.mom), channel_id=1, source_target_pairs={{0,6},{1,7},{2,4},{3,5},{4,2},{5,3},{6,0},{7,1},{8,14},{9,15},{10,... | collective-permute-start | bytes 172040 | tf_op jit(solution)/shard_map/ppermute | solution.py:494
  39.9 0.7 collective-permute-start.12
  40.7 2.2 %collective-permute-done.13.corner = f32[112,128]{1,0:T(8,128)S(1)} collective-permute-done((f32[112,128]{1,0:T(8,128)S(1)}, f32[112,128]{1,0:T(8,128)S(1)}, u32[]{:S(2)}, u32[]{:S(2)}) %collective-permute-start.13) | collective-permute-done | bytes 57376 | tf_op jit(solution)/shard_map/ppermute | solution.py:494
  42.9 1.4 %collective-permute-start.11 = (f32[112,128]{1,0:T(8,128)S(1)}, f32[112,128]{1,0:T(8,128)S(1)}, u32[]{:S(2)}, u32[]{:S(2)}) collective-permute-start(f32[112,128]{1,0:T(8,128)S(1)} %add.10.mom), channel_id=1, source_target_pairs={{0,2},{1,3},{2,0},{3,1},{4,6},{5,7},{6,4},{7,5},{8,10},{9,11},{10,... | collective-permute-start | bytes 172040 | tf_op jit(solution)/shard_map/ppermute | solution.py:494
  44.3 0.0 collective-permute-done.12.beside
  44.3 2.7 %collective-permute-done.11.across = f32[112,128]{1,0:T(8,128)S(1)} collective-permute-done((f32[112,128]{1,0:T(8,128)S(1)}, f32[112,128]{1,0:T(8,128)S(1)}, u32[]{:S(2)}, u32[]{:S(2)}) %collective-permute-start.11) | collective-permute-done | bytes 57376 | tf_op jit(solution)/shard_map/ppermute | solution.py:494
  47.1 0.1 collective-permute-start.14
  47.2 3.8 %collective-permute-start.15 = (f32[148,128]{1,0:T(8,128)S(1)}, f32[148,128]{1,0:T(8,128)S(1)}, u32[]{:S(2)}, u32[]{:S(2)}) collective-permute-start(f32[148,128]{1,0:T(8,128)S(1)} %get-tuple-element.67), channel_id=1, source_target_pairs={{0,24},{8,0},{16,8},{24,16},{1,25},{9,1},{17,9},{25,17},{2,26},{10... | collective-permute-start | bytes 227336 | tf_op jit(solution)/shard_map/ppermute | solution.py:477
  51.0 2.4 %collective-permute-done.14.left = f32[148,128]{1,0:T(8,128)S(1)} collective-permute-done((f32[148,128]{1,0:T(8,128)S(1)}, f32[148,128]{1,0:T(8,128)S(1)}, u32[]{:S(2)}, u32[]{:S(2)}) %collective-permute-start.14) | collective-permute-done | bytes 75808 | tf_op jit(solution)/shard_map/ppermute | solution.py:477
  53.3 0.0 collective-permute-start.19
  53.3 1.3 %stream.4.g = f32[8,8,16,768]{3,2,1,0:T(8,128)S(1)} custom-call(f32[8,8,16,768]{3,2,1,0:T(8,128)S(1)} %get-tuple-element.63.h, f32[8,768]{1,0:T(8,128)S(1)} %get-tuple-element.47.coef, f32[8,8,16,128]{3,2,1,0:T(8,128)S(1)} %get-tuple-element.48.fluid), custom_call_target="tpu_custom_call" | custom-call | tf_op jit(solution)/shard_map/stream/pallas_call | solution.py:228
  54.7 1.1 %macro.4 = (f32[384,128]{1,0:T(8,128)S(1)}, f32[8,128]{1,0:T(8,128)S(1)}) custom-call(f32[224,128]{1,0:T(8,128)S(1)} %get-tuple-element.65.mid, f32[148,128]{1,0:T(8,128)S(1)} %collective-permute-done.14.left, f32[148,128]{1,0:T(8,128)S(1)} %collective-permute-done.15.right, f32[8,128]{1,0:T(8,128)S(1)} %get-tuple-element.53.fluid, ...), custom_call_target="tpu_custom_call" | custom-call | tf_op jit(solution)/shard_map/macro/pallas_call | solution.py:361
  55.8 2.0 %collective-permute-done.19.far = f32[8,128]{1,0:T(8,128)S(1)} collective-permute-done((f32[8,128]{1,0:T(8,128)S(1)}, f32[8,128]{1,0:T(8,128)S(1)}, u32[]{:S(2)}, u32[]{:S(2)}) %collective-permute-start.19) | collective-permute-done | bytes 4128 | tf_op jit(solution)/shard_map/ppermute | solution.py:477
  57.9 0.0 collective-permute-done.17.xbefore
  57.9 0.0 collective-permute-done.18.xafter
  57.9 0.0 collective-permute-done.16.yhalo
  57.9 1.9 %update.4 = (f32[8,8,16,768]{3,2,1,0:T(8,128)S(1)}, f32[112,128]{1,0:T(8,128)S(1)}, f32[8,16,768]{2,1,0:T(8,128)S(1)}, f32[8,16,384]{2,1,0:T(8,128)S(1)}, f32[8,16,384]{2,1,0:T(8,128)S(1)}) custom-call(f32[8,128]{1,0:T(8,128)S(1)} %get-tuple-element.45.target, f32[8,8,16,768]{3,2,1,0:T(8,128)S(1)} %stream.4.g, f32[384,128]{1,0:T(8,128)S(1)} %get-tuple-element.68.mix, ...), custom_call_target="tpu_custom_call" | custom-call | tf_op jit(solution)/shard_map/update/pallas_call | solution.py:458
  59.8 1.2 %collective-permute-start.26 = (f32[8,16,768]{2,1,0:T(8,128)S(1)}, f32[8,16,768]{2,1,0:T(8,128)S(1)}, u32[]{:S(2)}, u32[]{:S(2)}) collective-permute-start(f32[8,16,768]{2,1,0:T(8,128)S(1)} %get-tuple-element.80), channel_id=1, source_target_pairs={{0,4},{4,0},{1,5},{5,1},{2,6},{6,2},{3,7},{7,3},{8,12},{12,8},{9,1... | collective-permute-start | bytes 1179656 | tf_op jit(solution)/shard_map/ppermute | solution.py:477
  61.0 0.0 collective-permute-start.20
  61.0 0.0 collective-permute-start.27
  61.0 3.8 %collective-permute-start.28 = (f32[8,16,384]{2,1,0:T(8,128)S(1)}, f32[8,16,384]{2,1,0:T(8,128)S(1)}, u32[]{:S(2)}, u32[]{:S(2)}) collective-permute-start(f32[8,16,384]{2,1,0:T(8,128)S(1)} %get-tuple-element.82), channel_id=1, source_target_pairs={{0,24},{8,0},{16,8},{24,16},{1,25},{9,1},{17,9},{25,17},{2,26},{10... | collective-permute-start | bytes 589832 | tf_op jit(solution)/shard_map/ppermute | solution.py:477
  64.9 0.0 collective-permute-done.20
  64.9 1.7 %collective-permute-start.23 = (f32[112,128]{1,0:T(8,128)S(1)}, f32[112,128]{1,0:T(8,128)S(1)}, u32[]{:S(2)}, u32[]{:S(2)}) collective-permute-start(f32[112,128]{1,0:T(8,128)S(1)} %add.11.mom), channel_id=1, source_target_pairs={{0,6},{1,7},{2,4},{3,5},{4,2},{5,3},{6,0},{7,1},{8,14},{9,15},{10,... | collective-permute-start | bytes 172040 | tf_op jit(solution)/shard_map/ppermute | solution.py:494
  66.6 1.3 %collective-permute-start.22 = (f32[112,128]{1,0:T(8,128)S(1)}, f32[112,128]{1,0:T(8,128)S(1)}, u32[]{:S(2)}, u32[]{:S(2)}) collective-permute-start(f32[112,128]{1,0:T(8,128)S(1)} %add.11.mom), channel_id=1, source_target_pairs={{0,4},{1,5},{2,6},{3,7},{4,0},{5,1},{6,2},{7,3},{8,12},{9,13},{10,... | collective-permute-start | bytes 172040 | tf_op jit(solution)/shard_map/ppermute | solution.py:494
  67.9 2.1 %collective-permute-done.23.corner = f32[112,128]{1,0:T(8,128)S(1)} collective-permute-done((f32[112,128]{1,0:T(8,128)S(1)}, f32[112,128]{1,0:T(8,128)S(1)}, u32[]{:S(2)}, u32[]{:S(2)}) %collective-permute-start.23) | collective-permute-done | bytes 57376 | tf_op jit(solution)/shard_map/ppermute | solution.py:494
  70.0 1.5 %collective-permute-start.21 = (f32[112,128]{1,0:T(8,128)S(1)}, f32[112,128]{1,0:T(8,128)S(1)}, u32[]{:S(2)}, u32[]{:S(2)}) collective-permute-start(f32[112,128]{1,0:T(8,128)S(1)} %add.11.mom), channel_id=1, source_target_pairs={{0,2},{1,3},{2,0},{3,1},{4,6},{5,7},{6,4},{7,5},{8,10},{9,11},{10,... | collective-permute-start | bytes 172040 | tf_op jit(solution)/shard_map/ppermute | solution.py:494
  71.5 0.0 collective-permute-done.22.beside
  71.5 2.7 %collective-permute-done.21.across = f32[112,128]{1,0:T(8,128)S(1)} collective-permute-done((f32[112,128]{1,0:T(8,128)S(1)}, f32[112,128]{1,0:T(8,128)S(1)}, u32[]{:S(2)}, u32[]{:S(2)}) %collective-permute-start.21) | collective-permute-done | bytes 57376 | tf_op jit(solution)/shard_map/ppermute | solution.py:494
  74.2 0.1 collective-permute-start.24
  74.3 3.8 %collective-permute-start.25 = (f32[148,128]{1,0:T(8,128)S(1)}, f32[148,128]{1,0:T(8,128)S(1)}, u32[]{:S(2)}, u32[]{:S(2)}) collective-permute-start(f32[148,128]{1,0:T(8,128)S(1)} %get-tuple-element.78), channel_id=1, source_target_pairs={{0,24},{8,0},{16,8},{24,16},{1,25},{9,1},{17,9},{25,17},{2,26},{10... | collective-permute-start | bytes 227336 | tf_op jit(solution)/shard_map/ppermute | solution.py:477
  78.1 2.4 %collective-permute-done.24.left = f32[148,128]{1,0:T(8,128)S(1)} collective-permute-done((f32[148,128]{1,0:T(8,128)S(1)}, f32[148,128]{1,0:T(8,128)S(1)}, u32[]{:S(2)}, u32[]{:S(2)}) %collective-permute-start.24) | collective-permute-done | bytes 75808 | tf_op jit(solution)/shard_map/ppermute | solution.py:477
  80.5 1.3 %stream.5.g = f32[8,8,16,768]{3,2,1,0:T(8,128)S(1)} custom-call(f32[8,8,16,768]{3,2,1,0:T(8,128)S(1)} %get-tuple-element.74.h, f32[8,768]{1,0:T(8,128)S(1)} %get-tuple-element.47.coef, f32[8,8,16,128]{3,2,1,0:T(8,128)S(1)} %get-tuple-element.48.fluid), custom_call_target="tpu_custom_call" | custom-call | tf_op jit(solution)/shard_map/stream/pallas_call | solution.py:228
  81.8 0.0 collective-permute-done.25.right
  81.8 1.1 %macro.5 = (f32[384,128]{1,0:T(8,128)S(1)}, f32[8,128]{1,0:T(8,128)S(1)}, f32[5,8,128]{2,1,0:T(8,128)S(1)}) custom-call(f32[224,128]{1,0:T(8,128)S(1)} %get-tuple-element.76.mid, f32[148,128]{1,0:T(8,128)S(1)} %collective-permute-done.24.left, f32[148,128]{1,0:T(8,128)S(1)} %collective-permute-done.25.right, f32[8,128]{1,0:T(8,128)S(1)} %get-tuple-element.53.fluid, ...), custom_call_target="tpu_custom_call" | custom-call | tf_op jit(solution)/shard_map/macro/pallas_call | solution.py:361
  83.0 2.0 %collective-permute-done.29.far = f32[8,128]{1,0:T(8,128)S(1)} collective-permute-done((f32[8,128]{1,0:T(8,128)S(1)}, f32[8,128]{1,0:T(8,128)S(1)}, u32[]{:S(2)}, u32[]{:S(2)}) %collective-permute-start.29) | collective-permute-done | bytes 4128 | tf_op jit(solution)/shard_map/ppermute | solution.py:477
  85.0 0.0 collective-permute-done.26.yhalo
  85.0 3.1 %update.5 = (f32[8,8,16,768]{3,2,1,0:T(8,128)}, f32[320,16]{1,0:T(8,128)}) custom-call(f32[8,128]{1,0:T(8,128)S(1)} %get-tuple-element.45.target, f32[8,8,16,768]{3,2,1,0:T(8,128)S(1)} %stream.5.g, f32[384,128]{1,0:T(8,128)S(1)} %get-tuple-element.79.mix, bf16[144,768]{1,0:T(8,128)(2,1)S(1)} %get-tuple-element.56.wmat, ...), custom_call_target="tpu_custom_call" | custom-call | tf_op jit(solution)/shard_map/update/pallas_call | solution.py:458
  (17 shorter events, 0.2 us)
Async XLA Ops:
  0.6 26.1 %copy-start.1 = (f32[8,8,16]{2,1,0:T(8,128)S(1)}, f32[8,8,16]{2,1,0:T(8,128)}, u32[]{:S(2)}) copy-start(f32[8,8,16]{2,1,0:T(8,128)} %wall_temp.1) | copy-start | bytes 12292
  0.6 26.1 %copy-start = (s32[8,8,16]{2,1,0:T(8,128)S(1)}, s32[8,8,16]{2,1,0:T(8,128)}, u32[]{:S(2)}) copy-start(s32[8,8,16]{2,1,0:T(8,128)} %wall.1) | copy-start | bytes 12292
  3.9 27.2 %collective-permute-start.6 = (f32[8,16,768]{2,1,0:T(8,128)S(1)}, f32[8,16,768]{2,1,0:T(8,128)S(1)}, u32[]{:S(2)}, u32[]{:S(2)}) collective-permute-start(f32[8,16,768]{2,1,0:T(8,128)S(1)} %get-tuple-element.58), channel_id=1, source_target_pairs={{0,4},{4,0},{1,5},{5,1},{2,6},{6,2},{3,7},{7,3},{8,12},{12,8},{9,1... | collective-permute-start | bytes 1179656 | tf_op jit(solution)/shard_map/ppermute | solution.py:477
  7.0 3.8 %collective-permute-start = (f32[112,128]{1,0:T(8,128)S(1)}, f32[112,128]{1,0:T(8,128)S(1)}, u32[]{:S(2)}, u32[]{:S(2)}) collective-permute-start(f32[112,128]{1,0:T(8,128)S(1)} %get-tuple-element.49), channel_id=1, source_target_pairs={{0,1},{1,0},{2,3},{3,2},{4,5},{5,4},{6,7},{7,6},{8,9},{9,8},{10,11... | collective-permute-start | bytes 172040 | tf_op jit(solution)/shard_map/ppermute | solution.py:494
  7.0 24.1 %collective-permute-start.7 = (f32[8,16,384]{2,1,0:T(8,128)S(1)}, f32[8,16,384]{2,1,0:T(8,128)S(1)}, u32[]{:S(2)}, u32[]{:S(2)}) collective-permute-start(f32[8,16,384]{2,1,0:T(8,128)S(1)} %get-tuple-element.59), channel_id=1, source_target_pairs={{0,8},{8,16},{16,24},{24,0},{1,9},{9,17},{17,25},{25,1},{2,10},{10... | collective-permute-start | bytes 589832 | tf_op jit(solution)/shard_map/ppermute | solution.py:477
  8.6 22.5 %collective-permute-start.8 = (f32[8,16,384]{2,1,0:T(8,128)S(1)}, f32[8,16,384]{2,1,0:T(8,128)S(1)}, u32[]{:S(2)}, u32[]{:S(2)}) collective-permute-start(f32[8,16,384]{2,1,0:T(8,128)S(1)} %get-tuple-element.60), channel_id=1, source_target_pairs={{0,24},{8,0},{16,8},{24,16},{1,25},{9,1},{17,9},{25,17},{2,26},{10... | collective-permute-start | bytes 589832 | tf_op jit(solution)/shard_map/ppermute | solution.py:477
  10.8 5.1 %collective-permute-start.3 = (f32[112,128]{1,0:T(8,128)S(1)}, f32[112,128]{1,0:T(8,128)S(1)}, u32[]{:S(2)}, u32[]{:S(2)}) collective-permute-start(f32[112,128]{1,0:T(8,128)S(1)} %add.9.mom), channel_id=1, source_target_pairs={{0,6},{1,7},{2,4},{3,5},{4,2},{5,3},{6,0},{7,1},{8,14},{9,15},{10,... | collective-permute-start | bytes 172040 | tf_op jit(solution)/shard_map/ppermute | solution.py:494
  12.3 6.2 %collective-permute-start.2 = (f32[112,128]{1,0:T(8,128)S(1)}, f32[112,128]{1,0:T(8,128)S(1)}, u32[]{:S(2)}, u32[]{:S(2)}) collective-permute-start(f32[112,128]{1,0:T(8,128)S(1)} %add.9.mom), channel_id=1, source_target_pairs={{0,4},{1,5},{2,6},{3,7},{4,0},{5,1},{6,2},{7,3},{8,12},{9,13},{10,... | collective-permute-start | bytes 172040 | tf_op jit(solution)/shard_map/ppermute | solution.py:494
  16.0 4.2 %collective-permute-start.1 = (f32[112,128]{1,0:T(8,128)S(1)}, f32[112,128]{1,0:T(8,128)S(1)}, u32[]{:S(2)}, u32[]{:S(2)}) collective-permute-start(f32[112,128]{1,0:T(8,128)S(1)} %add.9.mom), channel_id=1, source_target_pairs={{0,2},{1,3},{2,0},{3,1},{4,6},{5,7},{6,4},{7,5},{8,10},{9,11},{10,... | collective-permute-start | bytes 172040 | tf_op jit(solution)/shard_map/ppermute | solution.py:494
  20.2 6.4 %collective-permute-start.4 = (f32[148,128]{1,0:T(8,128)S(1)}, f32[148,128]{1,0:T(8,128)S(1)}, u32[]{:S(2)}, u32[]{:S(2)}) collective-permute-start(f32[148,128]{1,0:T(8,128)S(1)} %get-tuple-element.51), channel_id=1, source_target_pairs={{0,8},{8,16},{16,24},{24,0},{1,9},{9,17},{17,25},{25,1},{2,10},{10... | collective-permute-start | bytes 227336 | tf_op jit(solution)/shard_map/ppermute | solution.py:477
  20.5 8.7 %collective-permute-start.5 = (f32[148,128]{1,0:T(8,128)S(1)}, f32[148,128]{1,0:T(8,128)S(1)}, u32[]{:S(2)}, u32[]{:S(2)}) collective-permute-start(f32[148,128]{1,0:T(8,128)S(1)} %get-tuple-element.52), channel_id=1, source_target_pairs={{0,24},{8,0},{16,8},{24,16},{1,25},{9,1},{17,9},{25,17},{2,26},{10... | collective-permute-start | bytes 227336 | tf_op jit(solution)/shard_map/ppermute | solution.py:477
  26.6 4.5 %collective-permute-start.9 = (f32[8,128]{1,0:T(8,128)S(1)}, f32[8,128]{1,0:T(8,128)S(1)}, u32[]{:S(2)}, u32[]{:S(2)}) collective-permute-start(f32[8,128]{1,0:T(8,128)S(1)} %get-tuple-element.62), channel_id=1, source_target_pairs={{0,16},{8,24},{16,0},{24,8},{1,17},{9,25},{17,1},{25,9},{2,18},{10... | collective-permute-start | bytes 12296 | tf_op jit(solution)/shard_map/ppermute | solution.py:477
  33.1 24.8 %collective-permute-start.16 = (f32[8,16,768]{2,1,0:T(8,128)S(1)}, f32[8,16,768]{2,1,0:T(8,128)S(1)}, u32[]{:S(2)}, u32[]{:S(2)}) collective-permute-start(f32[8,16,768]{2,1,0:T(8,128)S(1)} %get-tuple-element.69), channel_id=1, source_target_pairs={{0,4},{4,0},{1,5},{5,1},{2,6},{6,2},{3,7},{7,3},{8,12},{12,8},{9,1... | collective-permute-start | bytes 1179656 | tf_op jit(solution)/shard_map/ppermute | solution.py:477
  33.8 3.8 %collective-permute-start.10 = (f32[112,128]{1,0:T(8,128)S(1)}, f32[112,128]{1,0:T(8,128)S(1)}, u32[]{:S(2)}, u32[]{:S(2)}) collective-permute-start(f32[112,128]{1,0:T(8,128)S(1)} %get-tuple-element.64), channel_id=1, source_target_pairs={{0,1},{1,0},{2,3},{3,2},{4,5},{5,4},{6,7},{7,6},{8,9},{9,8},{10,11... | collective-permute-start | bytes 172040 | tf_op jit(solution)/shard_map/ppermute | solution.py:494
  33.8 24.0 %collective-permute-start.17 = (f32[8,16,384]{2,1,0:T(8,128)S(1)}, f32[8,16,384]{2,1,0:T(8,128)S(1)}, u32[]{:S(2)}, u32[]{:S(2)}) collective-permute-start(f32[8,16,384]{2,1,0:T(8,128)S(1)} %get-tuple-element.70), channel_id=1, source_target_pairs={{0,8},{8,16},{16,24},{24,0},{1,9},{9,17},{17,25},{25,1},{2,10},{10... | collective-permute-start | bytes 589832 | tf_op jit(solution)/shard_map/ppermute | solution.py:477
  35.3 22.5 %collective-permute-start.18 = (f32[8,16,384]{2,1,0:T(8,128)S(1)}, f32[8,16,384]{2,1,0:T(8,128)S(1)}, u32[]{:S(2)}, u32[]{:S(2)}) collective-permute-start(f32[8,16,384]{2,1,0:T(8,128)S(1)} %get-tuple-element.71), channel_id=1, source_target_pairs={{0,24},{8,0},{16,8},{24,16},{1,25},{9,1},{17,9},{25,17},{2,26},{10... | collective-permute-start | bytes 589832 | tf_op jit(solution)/shard_map/ppermute | solution.py:477
  37.7 5.2 %collective-permute-start.13 = (f32[112,128]{1,0:T(8,128)S(1)}, f32[112,128]{1,0:T(8,128)S(1)}, u32[]{:S(2)}, u32[]{:S(2)}) collective-permute-start(f32[112,128]{1,0:T(8,128)S(1)} %add.10.mom), channel_id=1, source_target_pairs={{0,6},{1,7},{2,4},{3,5},{4,2},{5,3},{6,0},{7,1},{8,14},{9,15},{10,... | collective-permute-start | bytes 172040 | tf_op jit(solution)/shard_map/ppermute | solution.py:494
  39.9 4.4 %collective-permute-start.12 = (f32[112,128]{1,0:T(8,128)S(1)}, f32[112,128]{1,0:T(8,128)S(1)}, u32[]{:S(2)}, u32[]{:S(2)}) collective-permute-start(f32[112,128]{1,0:T(8,128)S(1)} %add.10.mom), channel_id=1, source_target_pairs={{0,4},{1,5},{2,6},{3,7},{4,0},{5,1},{6,2},{7,3},{8,12},{9,13},{10,... | collective-permute-start | bytes 172040 | tf_op jit(solution)/shard_map/ppermute | solution.py:494
  42.9 4.2 %collective-permute-start.11 = (f32[112,128]{1,0:T(8,128)S(1)}, f32[112,128]{1,0:T(8,128)S(1)}, u32[]{:S(2)}, u32[]{:S(2)}) collective-permute-start(f32[112,128]{1,0:T(8,128)S(1)} %add.10.mom), channel_id=1, source_target_pairs={{0,2},{1,3},{2,0},{3,1},{4,6},{5,7},{6,4},{7,5},{8,10},{9,11},{10,... | collective-permute-start | bytes 172040 | tf_op jit(solution)/shard_map/ppermute | solution.py:494
  47.1 6.2 %collective-permute-start.14 = (f32[148,128]{1,0:T(8,128)S(1)}, f32[148,128]{1,0:T(8,128)S(1)}, u32[]{:S(2)}, u32[]{:S(2)}) collective-permute-start(f32[148,128]{1,0:T(8,128)S(1)} %get-tuple-element.66), channel_id=1, source_target_pairs={{0,8},{8,16},{16,24},{24,0},{1,9},{9,17},{17,25},{25,1},{2,10},{10... | collective-permute-start | bytes 227336 | tf_op jit(solution)/shard_map/ppermute | solution.py:477
  47.2 7.5 %collective-permute-start.15 = (f32[148,128]{1,0:T(8,128)S(1)}, f32[148,128]{1,0:T(8,128)S(1)}, u32[]{:S(2)}, u32[]{:S(2)}) collective-permute-start(f32[148,128]{1,0:T(8,128)S(1)} %get-tuple-element.67), channel_id=1, source_target_pairs={{0,24},{8,0},{16,8},{24,16},{1,25},{9,1},{17,9},{25,17},{2,26},{10... | collective-permute-start | bytes 227336 | tf_op jit(solution)/shard_map/ppermute | solution.py:477
  53.3 4.5 %collective-permute-start.19 = (f32[8,128]{1,0:T(8,128)S(1)}, f32[8,128]{1,0:T(8,128)S(1)}, u32[]{:S(2)}, u32[]{:S(2)}) collective-permute-start(f32[8,128]{1,0:T(8,128)S(1)} %get-tuple-element.73), channel_id=1, source_target_pairs={{0,16},{8,24},{16,0},{24,8},{1,17},{9,25},{17,1},{25,9},{2,18},{10... | collective-permute-start | bytes 12296 | tf_op jit(solution)/shard_map/ppermute | solution.py:477
  59.8 25.2 %collective-permute-start.26 = (f32[8,16,768]{2,1,0:T(8,128)S(1)}, f32[8,16,768]{2,1,0:T(8,128)S(1)}, u32[]{:S(2)}, u32[]{:S(2)}) collective-permute-start(f32[8,16,768]{2,1,0:T(8,128)S(1)} %get-tuple-element.80), channel_id=1, source_target_pairs={{0,4},{4,0},{1,5},{5,1},{2,6},{6,2},{3,7},{7,3},{8,12},{12,8},{9,1... | collective-permute-start | bytes 1179656 | tf_op jit(solution)/shard_map/ppermute | solution.py:477
  61.0 3.8 %collective-permute-start.20 = (f32[112,128]{1,0:T(8,128)S(1)}, f32[112,128]{1,0:T(8,128)S(1)}, u32[]{:S(2)}, u32[]{:S(2)}) collective-permute-start(f32[112,128]{1,0:T(8,128)S(1)} %get-tuple-element.75), channel_id=1, source_target_pairs={{0,1},{1,0},{2,3},{3,2},{4,5},{5,4},{6,7},{7,6},{8,9},{9,8},{10,11... | collective-permute-start | bytes 172040 | tf_op jit(solution)/shard_map/ppermute | solution.py:494
  61.0 24.0 %collective-permute-start.27 = (f32[8,16,384]{2,1,0:T(8,128)S(1)}, f32[8,16,384]{2,1,0:T(8,128)S(1)}, u32[]{:S(2)}, u32[]{:S(2)}) collective-permute-start(f32[8,16,384]{2,1,0:T(8,128)S(1)} %get-tuple-element.81), channel_id=1, source_target_pairs={{0,8},{8,16},{16,24},{24,0},{1,9},{9,17},{17,25},{25,1},{2,10},{10... | collective-permute-start | bytes 589832 | tf_op jit(solution)/shard_map/ppermute | solution.py:477
  61.0 24.0 %collective-permute-start.28 = (f32[8,16,384]{2,1,0:T(8,128)S(1)}, f32[8,16,384]{2,1,0:T(8,128)S(1)}, u32[]{:S(2)}, u32[]{:S(2)}) collective-permute-start(f32[8,16,384]{2,1,0:T(8,128)S(1)} %get-tuple-element.82), channel_id=1, source_target_pairs={{0,24},{8,0},{16,8},{24,16},{1,25},{9,1},{17,9},{25,17},{2,26},{10... | collective-permute-start | bytes 589832 | tf_op jit(solution)/shard_map/ppermute | solution.py:477
  64.9 5.1 %collective-permute-start.23 = (f32[112,128]{1,0:T(8,128)S(1)}, f32[112,128]{1,0:T(8,128)S(1)}, u32[]{:S(2)}, u32[]{:S(2)}) collective-permute-start(f32[112,128]{1,0:T(8,128)S(1)} %add.11.mom), channel_id=1, source_target_pairs={{0,6},{1,7},{2,4},{3,5},{4,2},{5,3},{6,0},{7,1},{8,14},{9,15},{10,... | collective-permute-start | bytes 172040 | tf_op jit(solution)/shard_map/ppermute | solution.py:494
  66.6 4.9 %collective-permute-start.22 = (f32[112,128]{1,0:T(8,128)S(1)}, f32[112,128]{1,0:T(8,128)S(1)}, u32[]{:S(2)}, u32[]{:S(2)}) collective-permute-start(f32[112,128]{1,0:T(8,128)S(1)} %add.11.mom), channel_id=1, source_target_pairs={{0,4},{1,5},{2,6},{3,7},{4,0},{5,1},{6,2},{7,3},{8,12},{9,13},{10,... | collective-permute-start | bytes 172040 | tf_op jit(solution)/shard_map/ppermute | solution.py:494
  70.0 4.2 %collective-permute-start.21 = (f32[112,128]{1,0:T(8,128)S(1)}, f32[112,128]{1,0:T(8,128)S(1)}, u32[]{:S(2)}, u32[]{:S(2)}) collective-permute-start(f32[112,128]{1,0:T(8,128)S(1)} %add.11.mom), channel_id=1, source_target_pairs={{0,2},{1,3},{2,0},{3,1},{4,6},{5,7},{6,4},{7,5},{8,10},{9,11},{10,... | collective-permute-start | bytes 172040 | tf_op jit(solution)/shard_map/ppermute | solution.py:494
  74.2 6.2 %collective-permute-start.24 = (f32[148,128]{1,0:T(8,128)S(1)}, f32[148,128]{1,0:T(8,128)S(1)}, u32[]{:S(2)}, u32[]{:S(2)}) collective-permute-start(f32[148,128]{1,0:T(8,128)S(1)} %get-tuple-element.77), channel_id=1, source_target_pairs={{0,8},{8,16},{16,24},{24,0},{1,9},{9,17},{17,25},{25,1},{2,10},{10... | collective-permute-start | bytes 227336 | tf_op jit(solution)/shard_map/ppermute | solution.py:477
  74.3 7.5 %collective-permute-start.25 = (f32[148,128]{1,0:T(8,128)S(1)}, f32[148,128]{1,0:T(8,128)S(1)}, u32[]{:S(2)}, u32[]{:S(2)}) collective-permute-start(f32[148,128]{1,0:T(8,128)S(1)} %get-tuple-element.78), channel_id=1, source_target_pairs={{0,24},{8,0},{16,8},{24,16},{1,25},{9,1},{17,9},{25,17},{2,26},{10... | collective-permute-start | bytes 227336 | tf_op jit(solution)/shard_map/ppermute | solution.py:477
  80.5 4.5 %collective-permute-start.29 = (f32[8,128]{1,0:T(8,128)S(1)}, f32[8,128]{1,0:T(8,128)S(1)}, u32[]{:S(2)}, u32[]{:S(2)}) collective-permute-start(f32[8,128]{1,0:T(8,128)S(1)} %get-tuple-element.84), channel_id=1, source_target_pairs={{0,16},{8,24},{16,0},{24,8},{1,17},{9,25},{17,1},{25,9},{2,18},{10... | collective-permute-start | bytes 12296 | tf_op jit(solution)/shard_map/ppermute | solution.py:477
